TPU v7x, 32 devices: a whole 2x2x4 slice. The times are simulated.
32 devices in a mesh: grp: 2 (over y), pts: 8 (over z, x), sen: 2 (over core).
Axes of the slice: x: 2, y: 2, z: 4, core: 2. Of those that a mesh axis runs over, the one named last changes fastest.
Arguments:
- probes: bfloat16 [16, 64, 420], P(None, ('grp', 'pts')), parts along dimension 1, may hold values from -6 to 6
- kernel: bfloat16 [2, 64, 128, 421], P(None, ('grp', 'pts'), 'sen'), parts along dimension 1, may hold values from -1 to 1
- noise_weight: float32 [256], P(('grp', 'sen')), parts along dimension 0, may hold values from 0.3 to 3
- prior_scale: float32 [32], P('pts'), may hold values from 0.3 to 3
- basis: bfloat16 [13440, 1024], P('pts', 'sen'), may hold values from -0.15625 to 0.15625
- deflation: float32 [1024], P('sen'), may hold values from 0.3 to 0.95
Outputs:
- deflated: float32 [16, 64, 420], P(None, ('grp', 'pts')), parts along dimension 1
There are 2 independent parts, one for each index of `grp`. A program takes and returns all parts, laid end to end along the dimension named above; an argument that names none is the same for every part. Nothing has to cross between parts.
All inputs are finite; a program needn't handle non-finite values.
Results may differ from a plain program's by a relative error of at most 0.015.
Values may be sent and summed in bfloat16 or wider, within the bound.
No kernel may reach another device: no remote copies, remote signals or barrier semaphores. Data moves between devices by JAX's collectives and lax.ppermute only.
A program may use at most 64 MiB of HBM per device.

v0:
```python
import math

import jax
import jax.numpy as jnp
from jax import lax
from jax.sharding import PartitionSpec as P


def tables(steps_count):
    bins_count = steps_count + 1
    turns = (
        jnp.arange(steps_count, dtype=jnp.int32)[:, None]
        * jnp.arange(bins_count, dtype=jnp.int32)[None, :]
        % (2 * steps_count)
    )
    angle = turns.astype(jnp.float32) * (math.pi / steps_count)
    cosine = jnp.cos(angle)
    sine = jnp.sin(angle)
    freq = jnp.arange(bins_count, dtype=jnp.int32)
    edge = (freq == 0) | (freq == steps_count)
    weights = jnp.where(edge, 1.0, 2.0).astype(jnp.float32) / (2.0 * steps_count)
    forward = jnp.concatenate([cosine, -sine], axis=1)
    inverse = jnp.concatenate([cosine * weights[None, :], -sine * weights[None, :]], axis=1)
    return (forward, inverse)


def widened(value):
    return lax.optimization_barrier(value).astype(jnp.float32)


def complex_data(spec_real, spec_imag, kern_real, kern_imag):
    data_real = jnp.einsum(
        "kpf,psf->ksf", spec_real, kern_real, preferred_element_type=jnp.float32
    ) - jnp.einsum("kpf,psf->ksf", spec_imag, kern_imag, preferred_element_type=jnp.float32)
    data_imag = jnp.einsum(
        "kpf,psf->ksf", spec_real, kern_imag, preferred_element_type=jnp.float32
    ) + jnp.einsum("kpf,psf->ksf", spec_imag, kern_real, preferred_element_type=jnp.float32)
    return (data_real, data_imag)


def complex_adjoint(weight_real, weight_imag, kern_real, kern_imag):
    adj_real = jnp.einsum(
        "ksf,psf->kpf", weight_real, kern_real, preferred_element_type=jnp.float32
    ) + jnp.einsum("ksf,psf->kpf", weight_imag, kern_imag, preferred_element_type=jnp.float32)
    adj_imag = jnp.einsum(
        "ksf,psf->kpf", weight_imag, kern_real, preferred_element_type=jnp.float32
    ) - jnp.einsum("ksf,psf->kpf", weight_real, kern_imag, preferred_element_type=jnp.float32)
    return (adj_real, adj_imag)


def local(probes, kernel, noise_weight, prior_scale, basis, deflation):
    highest = lax.Precision.HIGHEST
    probe_count, point_count, steps_count = probes.shape
    bins_count = steps_count + 1
    sensor_count = noise_weight.shape[0]
    forward, inverse = tables(steps_count)
    scaled = probes.astype(jnp.float32) * prior_scale[None, :, None]
    spectrum = jnp.dot(scaled, forward, precision=highest).astype(jnp.bfloat16)
    noise_rows = jnp.tile(noise_weight, probe_count)
    width = lax.axis_size("pts")
    block = (bins_count + width - 1) // width
    extra = block * width - bins_count
    kern_pad = jnp.pad(kernel, ((0, 0), (0, 0), (0, 0), (0, extra)))
    spec_pad = jnp.pad(
        spectrum.reshape(probe_count, point_count, 2, bins_count),
        ((0, 0), (0, 0), (0, 0), (0, extra)),
    )
    kern_bins, spec_bins = (
        lax.all_to_all(kern_pad, "pts", split_axis=3, concat_axis=1, tiled=True),
        lax.all_to_all(spec_pad, "pts", split_axis=3, concat_axis=1, tiled=True),
    )
    bin_kern_real = kern_bins[0]
    bin_kern_imag = kern_bins[1]
    data_real, data_imag = complex_data(
        spec_bins[:, :, 0], spec_bins[:, :, 1], bin_kern_real, bin_kern_imag
    )
    data_bins = jnp.stack([data_real, data_imag], axis=2).reshape(
        probe_count * sensor_count, 2, block
    )
    rows_time = lax.all_to_all(
        data_bins.astype(jnp.bfloat16), "pts", split_axis=0, concat_axis=2, tiled=True
    ).astype(data_bins.dtype)
    local_rows = rows_time.shape[0]
    begin = lax.axis_index("pts") * local_rows
    local_noise = lax.dynamic_slice_in_dim(noise_rows, begin, local_rows)
    data_rows = rows_time[:, :, :bins_count].reshape(local_rows, 2 * bins_count)
    observed = jnp.dot(data_rows, inverse.T, precision=highest)
    residual = (observed * local_noise[:, None]).astype(jnp.bfloat16)
    weighted_local = (
        jnp.dot(widened(residual), inverse, precision=highest)
        .astype(jnp.bfloat16)
        .reshape(local_rows, 2, bins_count)
    )
    weighted_pad = jnp.pad(weighted_local, ((0, 0), (0, 0), (0, extra)))
    weighted_bins = lax.all_to_all(weighted_pad, "pts", split_axis=2, concat_axis=0, tiled=True)
    weighted_bins = weighted_bins.reshape(probe_count, sensor_count, 2, block)
    adj_real, adj_imag = complex_adjoint(
        weighted_bins[:, :, 0], weighted_bins[:, :, 1], bin_kern_real, bin_kern_imag
    )
    adj_bins = jnp.stack([adj_real, adj_imag], axis=2)
    adj_points = lax.all_to_all(
        adj_bins.astype(jnp.bfloat16), "pts", split_axis=1, concat_axis=3, tiled=True
    ).astype(adj_bins.dtype)
    adjoint = adj_points[..., :bins_count].reshape(probe_count, point_count, 2 * bins_count)
    back = jnp.dot(adjoint, forward.T, precision=highest)
    back = lax.psum(back.astype(jnp.bfloat16), "sen").astype(jnp.float32)
    hessian = back * prior_scale[None, :, None]
    flat = hessian.reshape(probe_count, point_count * steps_count)
    flat_low = flat.astype(jnp.bfloat16)
    coeff = jnp.dot(flat_low, basis, preferred_element_type=jnp.float32)
    coeff = lax.psum(coeff, "pts")
    shrunk = (coeff * deflation[None, :]).astype(jnp.bfloat16)
    correction = lax.dot_general(
        shrunk, basis, (((1,), (1,)), ((), ())), preferred_element_type=jnp.float32
    )
    correction = lax.psum(correction.astype(jnp.bfloat16), "sen").astype(jnp.float32)
    return (flat - correction).reshape(probe_count, point_count, steps_count)


def solution(mesh):
    placed = (
        P(None, ("grp", "pts"), None),
        P(None, ("grp", "pts"), "sen", None),
        P(("grp", "sen")),
        P("pts"),
        P("pts", "sen"),
        P("sen"),
    )
    return jax.shard_map(
        local, mesh=mesh, in_specs=placed, out_specs=P(None, ("grp", "pts"), None), check_vma=False
    )
```

profile of v0, /device:TPU:0, one launch (start us, length us, event | category | flops | bytes accessed | tf_op | source)
XLA Modules:
  0.0 193.4 jit_solution(13421877079795178455)
XLA Ops:
  0.0 3.6 %sine_negate_fusion = (f32[420,421]{1,0:T(8,128)S(1)}, f32[420,421]{1,0:T(8,128)S(1)}) fusion(), kind=kLoop, calls=%fused_computation.24 | loop fusion | flops 1768200 | bytes 1414560 | tf_op jit(solution)/shard_map/neg | solution.py:22
  3.7 1.7 convolution_convert_fusion.2
  5.4 1.7 reshape.46
  7.1 3.5 %copy.86 = bf16[16,4,2,421]{0,2,1,3:T(2,128)(2,1)} copy(bf16[16,4,2,421]{3,2,0,1:T(2,128)(2,1)} %reshape.46) | data formatting | bytes 215552 | tf_op jit(solution)/shard_map/reshape | solution.py:65
  10.6 3.0 %pad_bitcast_fusion = bf16[424,4,2,16]{3,2,1,0:T(2,128)(2,1)} fusion(bf16[16,4,2,421]{0,2,1,3:T(2,128)(2,1)} %copy.86), kind=kLoop, calls=%fused_computation.64 | loop fusion | bytes 216320
  13.6 2.8 %reshape.56 = bf16[8,2,3392]{2,1,0:T(2,128)(2,1)} reshape(bf16[424,4,2,16]{3,2,1,0:T(2,128)(2,1)} %pad_bitcast_fusion) | data formatting | bytes 217088
  16.4 7.3 %all-to-all-start.1 = ((bf16[8,2,3392]{2,1,0:T(2,128)(2,1)}), bf16[8,2,3392]{2,1,0:T(2,128)(2,1)}, u32[]{:S(2)}, u32[]{:S(2)}) async-start(bf16[8,2,3392]{2,1,0:T(2,128)(2,1)} %reshape.56), calls=%async_computation.1 | async-start | bytes 221184 | tf_op jit(solution)/shard_map/all_to_all | solution.py:70
  23.7 1.4 copy.82
  25.1 1.6 pad_bitcast_fusion.1
  26.7 1.3 reshape.54
  28.0 2.9 %all-to-all-done.1 = bf16[8,2,3392]{2,1,0:T(2,128)(2,1)} async-done(((bf16[8,2,3392]{2,1,0:T(2,128)(2,1)}), bf16[8,2,3392]{2,1,0:T(2,128)(2,1)}, u32[]{:S(2)}, u32[]{:S(2)}) %all-to-all-start.1) | async-done | bytes 108576 | tf_op jit(solution)/shard_map/all_to_all | solution.py:70
  31.0 4.3 %all-to-all-start = ((bf16[8,2,13568]{2,1,0:T(2,128)(2,1)}), bf16[8,2,13568]{2,1,0:T(2,128)(2,1)}, u32[]{:S(2)}, u32[]{:S(2)}) async-start(bf16[8,2,13568]{2,1,0:T(2,128)(2,1)} %reshape.54), calls=%async_computation | async-start | bytes 868352 | tf_op jit(solution)/shard_map/all_to_all | solution.py:69
  35.5 1.5 reshape.57
  37.0 2.0 %copy.105 = bf16[16,4,2,8,53]{4,0,2,1,3:T(8,128)(2,1)} copy(bf16[16,4,2,8,53]{0,2,1,4,3:T(2,128)(2,1)S(1)} %bitcast.105) | data formatting | bytes 217088 | tf_op jit(solution)/shard_map/all_to_all | solution.py:70
  39.0 1.0 fusion.38
  40.0 1.0 copy.107
  40.9 1.0 copy.108
  41.9 4.7 %all-to-all-done = bf16[8,2,13568]{2,1,0:T(2,128)(2,1)} async-done(((bf16[8,2,13568]{2,1,0:T(2,128)(2,1)}), bf16[8,2,13568]{2,1,0:T(2,128)(2,1)}, u32[]{:S(2)}, u32[]{:S(2)}) %all-to-all-start) | async-done | bytes 434208 | tf_op jit(solution)/shard_map/all_to_all | solution.py:69
  46.6 2.4 %reshape.55 = bf16[424,2,4,64]{3,2,1,0:T(4,128)(2,1)S(1)} reshape(bf16[8,2,13568]{2,1,0:T(2,128)(2,1)} %all-to-all-done) | data formatting | bytes 868352
  49.0 1.9 copy.103
  50.9 2.3 %fusion.37 = (bf16[1,8,4,64,53]{4,1,3,2,0:T(8,128)(2,1)}, bf16[1,8,4,64,53]{4,1,3,2,0:T(8,128)(2,1)}) fusion(bf16[2,8,4,64,53]{4,1,3,2,0:T(8,128)(2,1)} %bitcast.104), kind=kLoop, calls=%fused_computation.62 | loop fusion | bytes 868352 | tf_op jit(solution)/shard_map/slice | solution.py:73
  53.1 2.0 %copy.84 = bf16[1,8,4,64,53]{3,2,1,4,0:T(4,128)(2,1)S(1)} copy(bf16[1,8,4,64,53]{4,1,3,2,0:T(8,128)(2,1)} %get-tuple-element.6) | data formatting | bytes 434176 | tf_op jit(solution)/shard_map/slice | solution.py:72
  55.1 2.0 %copy.90 = bf16[1,8,4,64,53]{3,2,1,4,0:T(4,128)(2,1)S(1)} copy(bf16[1,8,4,64,53]{4,1,3,2,0:T(8,128)(2,1)} %get-tuple-element.5) | data formatting | bytes 434176 | tf_op jit(solution)/shard_map/slice | solution.py:73
  57.1 1.2 fusion.19
  58.3 2.0 %fusion.21 = f32[53,64,16]{1,2,0:T(8,128)} fusion(bf16[32,64,53]{1,0,2:T(8,128)(2,1)S(1)} %bitcast.96, bf16[16,32,1,53]{1,0,3,2:T(8,128)(2,1)} %copy.107), kind=kOutput, calls=%fused_computation.40 | convolution fusion | flops 3473408 | bytes 488448 | tf_op jit(solution)/shard_map/kpf,psf->ksf/dot_general | solution.py:35
  60.3 1.0 fusion.5
  61.2 1.8 stack.21
  63.0 1.9 copy.92
  64.9 2.1 %fusion.4 = bf16[16,64,53]{1,0,2:T(8,128)(2,1)} fusion(f32[53,64,16]{1,2,0:T(8,128)} %fusion.21, bf16[32,64,53]{1,0,2:T(8,128)(2,1)S(1)} %bitcast.101, bf16[16,32,1,53]{1,0,3,2:T(8,128)(2,1)} %copy.108), kind=kOutput, calls=%fused_computation.13 | convolution fusion | flops 3581952 | bytes 596992 | tf_op jit(solution)/shard_map/kpf,psf->ksf/dot_general | solution.py:37
  67.0 1.8 stack.22
  68.8 1.9 copy.93
  70.7 3.4 %pad_maximum_fusion.3 = bf16[1024,2,53]{2,1,0:T(2,128)(2,1)} fusion(bf16[1024,1,53]{2,1,0:T(2,128)(2,1)} %copy.93, bf16[1024,1,53]{2,1,0:T(2,128)(2,1)} %copy.92), kind=kLoop, calls=%fused_computation.30 | loop fusion | flops 434176 | bytes 434176 | tf_op jit(solution)/shard_map/stack | solution.py:77
  74.1 2.6 %reshape.58 = bf16[8,2,6784]{2,1,0:T(2,128)(2,1)} reshape(bf16[1024,2,53]{2,1,0:T(2,128)(2,1)} %pad_maximum_fusion.3) | data formatting | bytes 434176
  76.7 4.3 %all-to-all-start.2 = ((bf16[8,2,6784]{2,1,0:T(2,128)(2,1)}), bf16[8,2,6784]{2,1,0:T(2,128)(2,1)}, u32[]{:S(2)}, u32[]{:S(2)}) async-start(bf16[8,2,6784]{2,1,0:T(2,128)(2,1)} %reshape.58), calls=%async_computation.2 | async-start | bytes 434176 | tf_op jit(solution)/shard_map/all_to_all | solution.py:80
  81.0 4.6 %broadcast_multiply_fusion.1 = (f32[420,421]{1,0:T(8,128)}, f32[420,421]{1,0:T(8,128)}) fusion(f32[421]{0:T(512)S(1)} %select_multiply_fusion), kind=kLoop, calls=%fused_computation.33 | loop fusion | flops 2121840 | bytes 1416244 | tf_op jit(solution)/shard_map/mul | solution.py:23
  85.6 3.1 %all-to-all-done.2 = bf16[8,2,6784]{2,1,0:T(2,128)(2,1)} async-done(((bf16[8,2,6784]{2,1,0:T(2,128)(2,1)}), bf16[8,2,6784]{2,1,0:T(2,128)(2,1)}, u32[]{:S(2)}, u32[]{:S(2)}) %all-to-all-start.2) | async-done | bytes 217120 | tf_op jit(solution)/shard_map/all_to_all | solution.py:80
  88.7 3.2 %reshape.59 = bf16[1024,2,53]{2,1,0:T(2,128)(2,1)} reshape(bf16[8,2,6784]{2,1,0:T(2,128)(2,1)} %all-to-all-done.2) | data formatting | bytes 434176
  91.9 2.1 %copy.106 = bf16[8,128,2,53]{1,0,3,2:T(8,128)(2,1)} copy(bf16[8,128,2,53]{3,2,1,0:T(2,128)(2,1)} %bitcast.107) | data formatting | bytes 434176 | tf_op jit(solution)/shard_map/all_to_all | solution.py:80
  94.0 1.1 copy.95
  95.3 0.7 copy.96
  96.0 1.7 reshape.47
  97.6 2.6 %fusion.8 = bf16[128,420]{0,1:T(8,128)(2,1)S(1)} fusion(bf16[128,842]{0,1:T(8,128)(2,1)} %reshape.47, f32[420,421]{1,0:T(8,128)} %get-tuple-element.10, f32[420,421]{1,0:T(8,128)} %get-tuple-element.9, f32[128]{0:T(128)S(1)} %dynamic_slice.3), kind=kOutput, calls=%fused_computation.19 | convolution fusion | flops 543652224 | bytes 1738144 | tf_op jit(solution)/shard_map/dot_general | solution.py:87
  100.2 2.5 %convolution_convert_fusion.1 = bf16[128,842]{0,1:T(8,128)(2,1)} fusion(bf16[128,420]{0,1:T(8,128)(2,1)S(1)} %fusion.8, f32[420,421]{1,0:T(8,128)S(1)} %copy-done.4, f32[420,421]{1,0:T(8,128)S(1)} %copy-done.3), kind=kOutput, calls=%fused_computation.8 | convolution fusion | flops 543652480 | bytes 1737632 | tf_op jit(solution)/shard_map/dot_general | solution.py:90
  102.8 1.7 reshape.48
  104.5 1.1 copy.109
  105.7 10.7 %all_to_all.84 = bf16[128,2,424]{0,1,2:T(2,128)(2,1)S(1)} all-to-all(bf16[128,2,424]{0,1,2:T(2,128)(2,1)S(1)} %pad.14.clone), channel_id=1, replica_groups=mesh['grp'=2,'pts'=8,'sen'=2] {'pts'}, dimensions={2} | all-to-all | bytes 434176 | tf_op jit(solution)/shard_map/all_to_all | solution.py:95
  116.4 0.7 copy.98
  117.1 1.9 reshape.49
  119.0 1.3 fusion.23
  120.4 1.3 fusion.24
  122.4 0.9 pad_maximum_fusion.4
  123.3 2.4 %copy.99 = bf16[16,32,2,53]{3,0,2,1:T(8,128)(2,1)} copy(bf16[16,32,2,53]{1,0,3,2:T(8,128)(2,1)} %pad_maximum_fusion.4) | data formatting | bytes 217088 | tf_op jit(solution)/shard_map/stack | solution.py:100
  125.7 2.0 %reshape.60 = bf16[8,2,3392]{2,1,0:T(2,128)(2,1)} reshape(bf16[32,2,16,53]{3,2,1,0:T(8,128)(2,1)} %bitcast.109) | data formatting | bytes 217088
  127.8 11.2 %all_to_all.85 = bf16[8,2,3392]{2,1,0:T(2,128)(2,1)} all-to-all(bf16[8,2,3392]{2,1,0:T(2,128)(2,1)} %reshape.60), channel_id=1, replica_groups=mesh['grp'=2,'pts'=8,'sen'=2] {'pts'}, dimensions={0} | all-to-all | bytes 217088 | tf_op jit(solution)/shard_map/all_to_all | solution.py:101
  138.9 2.4 %reshape.61 = bf16[32,2,16,53]{3,2,1,0:T(8,128)(2,1)} reshape(bf16[8,2,3392]{2,1,0:T(2,128)(2,1)} %all_to_all.85) | data formatting | bytes 217088
  141.3 1.8 copy.100
  143.2 1.9 all_to_all.78
  145.0 1.7 copy.101
  146.7 1.7 reshape.50
  148.4 1.9 fusion.10
  150.3 3.6 %psum.21 = bf16[16,4,420]{2,0,1:T(8,128)(2,1)S(1)} all-reduce(bf16[16,4,420]{2,0,1:T(8,128)(2,1)S(1)} %fusion.10), channel_id=1, replica_groups=mesh['grp'=2,'pts'=8,'sen'=2] {'sen'}, use_global_device_ids=true, to_apply=%region_0.1 | all-reduce | flops 26880 | bytes 107520 | tf_op jit(solution)/shard_map/psum | solution.py:106
  154.6 33.8 %psum.22 = f32[16,512]{1,0:T(8,128)S(1)} all-reduce(f32[16,512]{1,0:T(8,128)S(1)} %fusion.29), channel_id=1, replica_groups=mesh['grp'=2,'pts'=8,'sen'=2] {'pts'}, use_global_device_ids=true, to_apply=%region_1.2 | all-reduce | flops 8192 | bytes 65536 | tf_op jit(solution)/shard_map/psum | solution.py:111
  189.0 3.6 %psum.23 = bf16[16,1680]{1,0:T(8,128)(2,1)S(1)} all-reduce(bf16[16,1680]{1,0:T(8,128)(2,1)S(1)} %convolution_convert_fusion), channel_id=1, replica_groups=mesh['grp'=2,'pts'=8,'sen'=2] {'sen'}, use_global_device_ids=true, to_apply=%region_2.3 | all-reduce | flops 26880 | bytes 107520 | tf_op jit(solution)/shard_map/psum | solution.py:116
  192.6 0.8 reshape.52
  (38 shorter events, 2.4 us)
Async XLA Ops:
  0.0 154.3 %copy-start = (bf16[1680,512]{1,0:T(8,128)(2,1)S(1)}, bf16[1680,512]{1,0:T(8,128)(2,1)}, u32[]{:S(2)}) copy-start(bf16[1680,512]{1,0:T(8,128)(2,1)} %param.10) | copy-start | bytes 5160964
  0.0 3.6 %copy-start.8 = (bf16[16,4,420]{2,1,0:T(4,128)(2,1)S(1)}, bf16[16,4,420]{2,1,0:T(4,128)(2,1)}, u32[]{:S(2)}) copy-start(bf16[16,4,420]{2,1,0:T(4,128)(2,1)} %param.6) | copy-start | bytes 161284
  0.0 3.6 %copy-start.9 = (f32[4]{0:T(128)S(1)}, f32[4]{0:T(128)}, u32[]{:S(2)}) copy-start(f32[4]{0:T(128)} %param.9) | copy-start | bytes 52
  3.6 7.0 %copy-start.1 = (f32[420,421]{1,0:T(8,128)}, f32[420,421]{1,0:T(8,128)S(1)}, u32[]{:S(2)}) copy-start(f32[420,421]{1,0:T(8,128)S(1)} %get-tuple-element.12) | copy-start | bytes 2121844
  13.6 10.1 %copy-start.7 = (bf16[2,4,64,421]{3,2,1,0:T(8,128)(2,1)S(1)}, bf16[2,4,64,421]{3,2,1,0:T(8,128)(2,1)}, u32[]{:S(2)}) copy-start(bf16[2,4,64,421]{3,2,1,0:T(8,128)(2,1)} %param.7) | copy-start | bytes 1293316
  16.4 14.6 %all-to-all-start.1 = ((bf16[8,2,3392]{2,1,0:T(2,128)(2,1)}), bf16[8,2,3392]{2,1,0:T(2,128)(2,1)}, u32[]{:S(2)}, u32[]{:S(2)}) async-start(bf16[8,2,3392]{2,1,0:T(2,128)(2,1)} %reshape.56), calls=%async_computation.1 | async-start | bytes 221184 | tf_op jit(solution)/shard_map/all_to_all | solution.py:70
  26.7 8.6 %copy-start.11 = (f32[64]{0:T(128)S(1)}, f32[64]{0:T(128)}, u32[]{:S(2)}) copy-start(f32[64]{0:T(128)} %param.8) | copy-start | bytes 772
  31.0 15.6 %all-to-all-start = ((bf16[8,2,13568]{2,1,0:T(2,128)(2,1)}), bf16[8,2,13568]{2,1,0:T(2,128)(2,1)}, u32[]{:S(2)}, u32[]{:S(2)}) async-start(bf16[8,2,13568]{2,1,0:T(2,128)(2,1)} %reshape.54), calls=%async_computation | async-start | bytes 868352 | tf_op jit(solution)/shard_map/all_to_all | solution.py:69
  57.1 3.2 %copy-start.6 = (bf16[16,32,1,53]{1,0,3,2:T(8,128)(2,1)S(1)}, bf16[16,32,1,53]{1,0,3,2:T(8,128)(2,1)}, u32[]{:S(2)}) copy-start(bf16[16,32,1,53]{1,0,3,2:T(8,128)(2,1)} %copy.108) | copy-start | bytes 162820
  76.7 12.0 %all-to-all-start.2 = ((bf16[8,2,6784]{2,1,0:T(2,128)(2,1)}), bf16[8,2,6784]{2,1,0:T(2,128)(2,1)}, u32[]{:S(2)}, u32[]{:S(2)}) async-start(bf16[8,2,6784]{2,1,0:T(2,128)(2,1)} %reshape.58), calls=%async_computation.2 | async-start | bytes 434176 | tf_op jit(solution)/shard_map/all_to_all | solution.py:80
  97.6 2.6 %copy-start.3 = (f32[420,421]{1,0:T(8,128)S(1)}, f32[420,421]{1,0:T(8,128)}, u32[]{:S(2)}) copy-start(f32[420,421]{1,0:T(8,128)} %get-tuple-element.9) | copy-start | bytes 2121844
  97.6 2.6 %copy-start.4 = (f32[420,421]{1,0:T(8,128)S(1)}, f32[420,421]{1,0:T(8,128)}, u32[]{:S(2)}) copy-start(f32[420,421]{1,0:T(8,128)} %get-tuple-element.10) | copy-start | bytes 2121844
  119.0 2.7 %copy-start.5 = (bf16[16,64,2,53]{1,0,3,2:T(8,128)(2,1)S(1)}, bf16[16,64,2,53]{1,0,3,2:T(8,128)(2,1)}, u32[]{:S(2)}) copy-start(bf16[16,64,2,53]{1,0,3,2:T(8,128)(2,1)} %reshape.49) | copy-start | bytes 651268
  123.3 25.1 %copy-start.2 = (f32[420,421]{1,0:T(8,128)S(1)}, f32[420,421]{1,0:T(8,128)}, u32[]{:S(2)}) copy-start(f32[420,421]{1,0:T(8,128)} %copy-done.1) | copy-start | bytes 2121844
  150.3 38.1 %copy-start.10 = (f32[512]{0:T(512)S(1)}, f32[512]{0:T(512)}, u32[]{:S(2)}) copy-start(f32[512]{0:T(512)} %param.11) | copy-start | bytes 6148
where the time goes:
time: 195 us; the launch traced here: 193 us
  local copies, waits for them, and re-layouts  71.9 us (37%)
  blocking collectives  62.9 us (32%)
  matrix products  19.2 us (10%)
  starting transfers between devices  15.8 us (8%)
  other arithmetic  12.7 us (7%)
  waiting for transfers between devices  10.7 us (5%)
    psum x1, blocking collectives, local(): coeff = lax.psum(coeff, 'pts')  33.8 us
    unnamed x38, local copies, waits for them, and re-layouts  27.4 us
    all_to_all x1, blocking collectives, local(): lax.all_to_all(adj_bins.astype(jnp.bfloat16), 'pts', split_axis=1, concat...  11.2 us
    all_to_all x1, blocking collectives, local(): lax.all_to_all(weighted_pad, 'pts', split_axis=2, concat_axis=0, tiled=True)  10.7 us
    another operation x4, local copies, waits for them, and re-layouts, local(): jnp.stack([data_real, data_imag], axis=2)  7.36 us
    all_to_all x1, starting transfers between devices, local(): lax.all_to_all(spec_pad, 'pts', split_axis=3, concat_axis=1, tiled=True)  7.29 us
    reshape x2, local copies, waits for them, and re-layouts, local(): spectrum.reshape(probe_count, point_count, 2, bins_count)  5.18 us
    all_to_all x1, waiting for transfers between devices, local(): lax.all_to_all(kern_pad, 'pts', split_axis=3, concat_axis=1, tiled=True)  4.7 us
  transfers between devices with their start and end apart: 3, of which 3 were waited for; matrix products, arithmetic and copies ran while one was open for 8% of the time, Pallas kernels for 0%

commit v1 on v0

--- a/solution.py
+++ b/solution.py
@@ -1,9 +1,16 @@
+import functools
 import math
 
 import jax
 import jax.numpy as jnp
+import numpy as np
 from jax import lax
+from jax.experimental import pallas as pl
+from jax.experimental.pallas import tpu as pltpu
 from jax.sharding import PartitionSpec as P
+
+LANES = 128
+ROWS = 8
 
 
 def tables(steps_count):
@@ -117,6 +124,253 @@
     return (flat - correction).reshape(probe_count, point_count, steps_count)
 
 
+def round_up(value, step):
+    return (value + step - 1) // step * step
+
+
+def packed_tables(steps_count, wide):
+    bins_count = steps_count + 1
+    turns = np.arange(steps_count)[:, None] * np.arange(bins_count)[None, :] % (2 * steps_count)
+    angle = turns.astype(np.float64) * (math.pi / steps_count)
+    table = np.zeros((steps_count, 2 * wide), np.float32)
+    table[:, :bins_count] = np.cos(angle)
+    table[:, wide : wide + bins_count] = -np.sin(angle)
+    weights = np.zeros((1, wide), np.float32)
+    weights[0, :bins_count] = 2.0 / (2.0 * steps_count)
+    weights[0, 0] = weights[0, steps_count] = 1.0 / (2.0 * steps_count)
+    return jnp.asarray(table.astype(jnp.bfloat16)), jnp.asarray(weights)
+
+
+NT = (((1,), (1,)), ((), ()))
+
+
+def gathered_at(relative, width):
+    place = 0
+    step = width // 2
+    bit = 1
+    while step:
+        place += (relative // step) % 2 * bit
+        step //= 2
+        bit *= 2
+    return place
+
+
+def bins_kernel(
+    index_ref, b0, b1, b2, b3, own, other, noise, table, weights, out,
+    kern, wide_spec, data, wdata, adjoint,
+    *, width, points, sens, probes_half, wide,
+):
+    me = index_ref[0]
+    tiles = wide // LANES
+    block = points * probes_half
+    f32 = jnp.float32
+    table_v = table[...]
+    rows = 0
+    for ref in (b0, b1, b2, b3):
+        count = ref.shape[0] * block
+        got = jnp.dot(ref[...].reshape(count, ref.shape[2]), table_v, preferred_element_type=f32)
+        real = got[:, :wide]
+        imag = got[:, wide:]
+        wide_spec[0, rows : rows + count] = real + imag
+        wide_spec[1, rows : rows + count] = imag
+        wide_spec[2, rows : rows + count] = real
+        rows += count
+    for half, ref in ((0, own), (1, other)):
+        def widen(j, carry, half=half, ref=ref):
+            for p in range(points):
+                real = ref[j, 0, p].astype(f32)
+                imag = ref[j, 1, p].astype(f32)
+                lo = half * sens
+                kern[0, j * points + p, lo : lo + sens] = real
+                kern[1, j * points + p, lo : lo + sens] = real + imag
+                kern[2, j * points + p, lo : lo + sens] = real - imag
+            return carry
+        lax.fori_loop(0, width, widen, 0)
+    all_sens = 2 * sens
+    weight_rows = weights[...]
+    for s0 in range(0, all_sens, sens):
+        def tile_step(ft, carry, s0=s0):
+            lanes = pl.ds(pl.multiple_of(ft * LANES, LANES), LANES)
+
+            def source(j, acc):
+                acc = list(acc)
+                base = gathered_at(me ^ j, width) * block
+                for p in range(points):
+                    at = pl.ds(pl.multiple_of(base + p * probes_half, ROWS), probes_half)
+                    both = wide_spec[0, at, lanes]
+                    imag = wide_spec[1, at, lanes]
+                    real = wide_spec[2, at, lanes]
+                    for s in range(sens):
+                        row = pl.ds(s0 + s, 1)
+                        acc[3 * s] += kern[0, j * points + p, row, lanes] * both
+                        acc[3 * s + 1] += kern[1, j * points + p, row, lanes] * imag
+                        acc[3 * s + 2] += kern[2, j * points + p, row, lanes] * real
+                return tuple(acc)
+
+            zero = jnp.zeros((probes_half, LANES), f32)
+            acc = lax.fori_loop(0, width, source, (zero,) * (3 * sens))
+            factor = weights[:, lanes]
+            for s in range(sens):
+                at = slice((s0 + s) * probes_half, (s0 + s + 1) * probes_half)
+                data[at, lanes] = (acc[3 * s] - acc[3 * s + 1]) * factor
+                shifted = pl.ds(pl.multiple_of(wide + ft * LANES, LANES), LANES)
+                data[at, shifted] = (acc[3 * s] - acc[3 * s + 2]) * factor
+            return carry
+
+        lax.fori_loop(0, tiles, tile_step, 0)
+    observed = lax.dot_general(
+        data[...].astype(jnp.bfloat16), table_v, NT, preferred_element_type=f32
+    )
+    residual = (observed * noise[...]).astype(jnp.bfloat16)
+    weighted = jnp.dot(residual, table_v, preferred_element_type=f32)
+    real = weighted[:, :wide] * weight_rows
+    imag = weighted[:, wide:] * weight_rows
+    wdata[0] = real + imag
+    wdata[1] = imag
+    wdata[2] = real
+
+    def adjoint_tile(step, carry):
+        j = step // tiles
+        ft = step % tiles
+        lanes = pl.ds(pl.multiple_of(ft * LANES, LANES), LANES)
+        shifted = pl.ds(pl.multiple_of(wide + ft * LANES, LANES), LANES)
+        zero = jnp.zeros((probes_half, LANES), f32)
+        acc = [zero] * (3 * points)
+        for s in range(all_sens):
+            at = slice(s * probes_half, (s + 1) * probes_half)
+            both = wdata[0, at, lanes]
+            imag = wdata[1, at, lanes]
+            real = wdata[2, at, lanes]
+            for p in range(points):
+                row = slice(s, s + 1)
+                acc[3 * p] += kern[0, j * points + p, row, lanes] * both
+                acc[3 * p + 1] += kern[2, j * points + p, row, lanes] * imag
+                acc[3 * p + 2] += kern[1, j * points + p, row, lanes] * real
+        for p in range(points):
+            at = pl.ds(pl.multiple_of((j * points + p) * probes_half, ROWS), probes_half)
+            adjoint[at, lanes] = acc[3 * p] - acc[3 * p + 1]
+            adjoint[at, shifted] = acc[3 * p] - acc[3 * p + 2]
+        return carry
+
+    lax.fori_loop(0, width * tiles, adjoint_tile, 0)
+    back = lax.dot_general(
+        adjoint[...].astype(jnp.bfloat16), table_v, NT, preferred_element_type=f32
+    )
+    out[...] = back.astype(jnp.bfloat16).reshape(out.shape)
+
+
+def coeff_kernel(parts, prior, basis_own, basis_other, flat, coeff, *, points, steps, probes_half, rank):
+    f32 = jnp.float32
+    total = parts[0].astype(f32)
+    for j in range(1, parts.shape[0]):
+        total += parts[j].astype(f32)
+    total = total * prior[...]
+    for p in range(points):
+        flat[:, p * steps : (p + 1) * steps] = total[p * probes_half : (p + 1) * probes_half]
+    low = flat[...].astype(jnp.bfloat16)
+    own = jnp.dot(low, basis_own[...], preferred_element_type=f32).astype(jnp.bfloat16)
+    other = jnp.dot(low, basis_other[...], preferred_element_type=f32).astype(jnp.bfloat16)
+    for j in range(coeff.shape[0]):
+        coeff[j, :, :rank] = own
+        coeff[j, :, rank:] = other
+
+
+def deflate_kernel(parts, deflation, flat, basis_own, basis_other, out, *, points, steps, rank):
+    f32 = jnp.float32
+    total = parts[0].astype(f32)
+    for j in range(1, parts.shape[0]):
+        total += parts[j].astype(f32)
+    shrunk = (total * deflation[...]).astype(jnp.bfloat16)
+    correction = lax.dot_general(shrunk[:, :rank], basis_own[...], NT, preferred_element_type=f32)
+    correction += lax.dot_general(shrunk[:, rank:], basis_other[...], NT, preferred_element_type=f32)
+    result = flat[...] - correction
+    for p in range(points):
+        out[:, p, :] = result[:, p * steps : (p + 1) * steps]
+
+
+def whole_specs(count):
+    return [pl.BlockSpec(memory_space=pltpu.VMEM) for _ in range(count)]
+
+
+def local_split(probes, kernel, noise_weight, prior_scale, basis, deflation):
+    bf16 = jnp.bfloat16
+    f32 = jnp.float32
+    probe_count, points, steps = probes.shape
+    bins_count = steps + 1
+    width = lax.axis_size("pts")
+    sens = noise_weight.shape[0] // width
+    half = probe_count // 2
+    rank = basis.shape[1]
+    wide = round_up(bins_count, LANES)
+    me = lax.axis_index("pts")
+    core = lax.axis_index("sen")
+    swap = [(0, 1), (1, 0)]
+    table, weights = packed_tables(steps, wide)
+
+    send = kernel.reshape(2, points, width, sens, bins_count).transpose(2, 0, 1, 3, 4)
+    send = jnp.pad(send, ((0, 0),) * 4 + ((0, wide - bins_count),))
+    own = lax.all_to_all(send, "pts", split_axis=0, concat_axis=0, tiled=False)
+    other = lax.ppermute(own, "sen", swap)
+
+    mine = lax.dynamic_slice_in_dim(probes, core * half, half, axis=0)
+    scaled = (mine.astype(f32) * prior_scale[None, :, None]).astype(bf16)
+    b0 = scaled.transpose(1, 0, 2).reshape(1, points * half, steps)
+    blocks = [b0]
+    step = width // 2
+    while step:
+        sent = blocks[0] if len(blocks) == 1 else jnp.concatenate(blocks, axis=0)
+        blocks.append(lax.ppermute(sent, "pts", [(i, i ^ step) for i in range(width)]))
+        step //= 2
+    noise_other = lax.ppermute(noise_weight, "sen", swap)
+    noise = jnp.concatenate(
+        [lax.dynamic_slice_in_dim(v, me * sens, sens) for v in (noise_weight, noise_other)]
+    )
+    noise_rows = jnp.repeat(noise, half)[:, None]
+    basis_other = lax.ppermute(basis, "sen", swap)
+    deflation_both = jnp.concatenate([deflation, lax.ppermute(deflation, "sen", swap)])[None, :]
+    perm = jnp.full((1,), me, jnp.int32)
+    all_rows = width * points * half
+    back = pl.pallas_call(
+        functools.partial(
+            bins_kernel, width=width, points=points, sens=sens, probes_half=half, wide=wide
+        ),
+        out_shape=jax.ShapeDtypeStruct((width, points * half, steps), bf16),
+        in_specs=[pl.BlockSpec(memory_space=pltpu.SMEM)] + whole_specs(9),
+        out_specs=pl.BlockSpec(memory_space=pltpu.VMEM),
+        scratch_shapes=[
+            pltpu.VMEM((3, width * points, 2 * sens, wide), f32),
+            pltpu.VMEM((3, all_rows, wide), f32),
+            pltpu.VMEM((2 * sens * half, 2 * wide), f32),
+            pltpu.VMEM((3, 2 * sens * half, wide), f32),
+            pltpu.VMEM((all_rows, 2 * wide), f32),
+        ],
+        name="bins",
+    )(perm, *blocks, own, other, noise_rows, table, weights)
+    parts = lax.all_to_all(back, "pts", split_axis=0, concat_axis=0, tiled=False)
+    prior_rows = jnp.repeat(prior_scale, half)[:, None]
+    flat, coeff = pl.pallas_call(
+        functools.partial(
+            coeff_kernel, points=points, steps=steps, probes_half=half, rank=rank
+        ),
+        out_shape=(
+            jax.ShapeDtypeStruct((half, points * steps), f32),
+            jax.ShapeDtypeStruct((width, half, 2 * rank), bf16),
+        ),
+        in_specs=whole_specs(4),
+        out_specs=tuple(whole_specs(2)),
+        name="coeff",
+    )(parts, prior_rows, basis, basis_other)
+    coeff_parts = lax.all_to_all(coeff, "pts", split_axis=0, concat_axis=0, tiled=False)
+    result = pl.pallas_call(
+        functools.partial(deflate_kernel, points=points, steps=steps, rank=rank),
+        out_shape=jax.ShapeDtypeStruct((half, points, steps), f32),
+        in_specs=whole_specs(5),
+        out_specs=pl.BlockSpec(memory_space=pltpu.VMEM),
+        name="deflate",
+    )(coeff_parts, deflation_both, flat, basis, basis_other)
+    return lax.all_gather(result, "sen", axis=0, tiled=True)
+
+
 def solution(mesh):
     placed = (
         P(None, ("grp", "pts"), None),
@@ -126,6 +380,17 @@
         P("pts", "sen"),
         P("sen"),
     )
+
+    def body(*args):
+        width = mesh.shape["pts"]
+        probe_count = args[0].shape[0]
+        sensors = args[2].shape[0]
+        power = width & (width - 1) == 0
+        split = mesh.shape["sen"] == 2 and power and 1 < width <= 8
+        if split and sensors == width * ROWS and probe_count == 2 * ROWS:
+            return local_split(*args)
+        return local(*args)
+
     return jax.shard_map(
-        local, mesh=mesh, in_specs=placed, out_specs=P(None, ("grp", "pts"), None), check_vma=False
-    )
+        body, mesh=mesh, in_specs=placed, out_specs=P(None, ("grp", "pts"), None), check_vma=False
+    )

time: 195 us -> 84.8 us (0.43)
  local copies, waits for them, and re-layouts: 71.9 us -> 8.42 us
  blocking collectives: 62.9 us -> 2.1 us
  waiting for transfers between devices: 10.7 us -> 39 us
  matrix products: 19.2 us -> 0 us
  Pallas kernels: 0 us -> 17.6 us
  other arithmetic: 12.7 us -> 1.44 us
    psum x3 -> x0, blocking collectives: 41 us -> none  [the longest x1 33.8 us: local(): coeff = lax.psum(coeff, 'pts')]
    unnamed x38 -> x29, local copies, waits for them, and re-layouts: 27.4 us -> 3.88 us
    all_to_all x2 -> x0, blocking collectives: 21.9 us -> none  [the longest x1 11.2 us: local(): lax.all_to_all(adj_bins.astype(jnp.bfloat16), 'pts', split_axis=1, concat...]
    dot_general x14 -> x0, matrix products: 19.2 us -> none  [the longest x1 2.58 us: local(): observed = jnp.dot(data_rows, inverse.T, precision=highest)]
    pallas_call x0 -> x3, Pallas kernels: none -> 17.6 us  [the longest x1 10.4 us: local_split(): pl.pallas_call(functools.partial(bins_kernel, width=width, points=points,...]
    all_to_all x3, waiting for transfers between devices: 10.7 us -> 26.6 us  [the longest x1 14.4 us: local_split(): own = lax.all_to_all(send, 'pts', split_axis=0, concat_axis=0, tiled=False)]
    reshape x8 -> x0, local copies, waits for them, and re-layouts: 13.1 us -> none  [the longest x2 5.18 us: local(): spectrum.reshape(probe_count, point_count, 2, bins_count)]
    ppermute x0 -> x7, waiting for transfers between devices: none -> 12.5 us  [the longest x3 10.2 us: local_split(): lax.ppermute(sent, 'pts', [(i, i ^ step) for i in range(width)])]
  transfers between devices with their start and end apart: 3 -> 10, of which waited for: 3 -> 8; matrix products, arithmetic and copies ran while one was open for 8% -> 6% of each run, Pallas kernels for 0% -> 12%
where the time goes in v1:
time: 84.8 us; the launch traced here: 84.3 us
  waiting for transfers between devices  39 us (46%)
  Pallas kernels  17.6 us (21%)
  starting transfers between devices  15.6 us (18%)
  local copies, waits for them, and re-layouts  8.42 us (10%)
  blocking collectives  2.1 us (2%)
  other arithmetic  1.44 us (2%)
    all_to_all x1, waiting for transfers between devices, local_split(): own = lax.all_to_all(send, 'pts', split_axis=0, concat_axis=0, tiled=False)  14.4 us
    pallas_call x1, Pallas kernels, local_split(): pl.pallas_call(functools.partial(bins_kernel, width=width, points=points,...  10.4 us
    ppermute x3, waiting for transfers between devices, local_split(): lax.ppermute(sent, 'pts', [(i, i ^ step) for i in range(width)])  10.2 us
    all_to_all x1, starting transfers between devices, local_split(): own = lax.all_to_all(send, 'pts', split_axis=0, concat_axis=0, tiled=False)  7.28 us
    all_to_all x1, waiting for transfers between devices, local_split(): lax.all_to_all(back, 'pts', split_axis=0, concat_axis=0, tiled=False)  6.75 us
    all_to_all x1, waiting for transfers between devices, local_split(): lax.all_to_all(coeff, 'pts', split_axis=0, concat_axis=0, tiled=False)  5.44 us
    unnamed x29, local copies, waits for them, and re-layouts  3.88 us
    pallas_call x1, Pallas kernels, local_split(): pl.pallas_call(functools.partial(deflate_kernel, points=points, steps=ste...  3.76 us
  transfers between devices with their start and end apart: 10, of which 8 were waited for; matrix products, arithmetic and copies ran while one was open for 6% of the time, Pallas kernels for 12%

profile of v1, /device:TPU:0, one launch (start us, length us, event | category | flops | bytes accessed | tf_op | source)
XLA Modules:
  0.0 84.3 jit_solution(13928483746096796302)
XLA Ops:
  0.0 0.0 copy-start
  0.0 0.0 copy-start.1
  0.0 0.0 copy-start.11
  0.0 0.0 copy-start.10
  0.0 0.0 copy-start.13
  0.0 1.0 %copy-done = bf16[2,4,64,421]{3,2,1,0:T(8,128)(2,1)S(1)} copy-done((bf16[2,4,64,421]{3,2,1,0:T(8,128)(2,1)S(1)}, bf16[2,4,64,421]{3,2,1,0:T(8,128)(2,1)}, u32[]{:S(2)}) %copy-start) | copy-done | bytes 431128
  1.1 0.9 %pad.4 = bf16[8,2,4,8,512]{4,3,2,1,0:T(8,128)(2,1)} pad(bf16[8,2,4,8,421]{4,3,2,1,0:T(8,128)(2,1)S(1)} %copy_bitcast_fusion, bf16[]{:T(256)} %constant.20.clone.1), padding=0_0x0_0x0_0x0_0x0_91 | pad | bytes 955394 | tf_op jit(solution)/shard_map/jit(_pad)/pad | solution.py:311
  1.9 7.3 %all-to-all-start = ((bf16[8,2,4,8,512]{4,3,2,1,0:T(8,128)(2,1)}), bf16[8,2,4,8,512]{4,3,2,1,0:T(8,128)(2,1)S(1)}, u32[]{:S(2)}, u32[]{:S(2)}) async-start(bf16[8,2,4,8,512]{4,3,2,1,0:T(8,128)(2,1)} %pad.4), calls=%async_computation | async-start | bytes 1048576 | tf_op jit(solution)/shard_map/all_to_all | solution.py:312
  9.2 0.0 copy-done.1
  9.2 0.1 collective-permute-start.5
  9.3 14.4 %all-to-all-done.own = bf16[8,2,4,8,512]{4,3,2,1,0:T(8,128)(2,1)S(1)} async-done(((bf16[8,2,4,8,512]{4,3,2,1,0:T(8,128)(2,1)}), bf16[8,2,4,8,512]{4,3,2,1,0:T(8,128)(2,1)S(1)}, u32[]{:S(2)}, u32[]{:S(2)}) %all-to-all-start) | async-done | bytes 524320 | tf_op jit(solution)/shard_map/all_to_all | solution.py:312
  23.7 0.0 copy-start.2
  23.7 0.0 collective-permute-start.3
  23.7 0.0 copy-done.11
  23.7 0.0 copy-done.10
  23.7 0.1 fusion
  23.8 0.0 copy-start.4
  23.8 0.2 collective-permute-start
  24.1 5.2 %collective-permute-done.b1 = bf16[1,32,420]{2,1,0:T(8,128)(2,1)S(1)} collective-permute-done((bf16[1,32,420]{2,1,0:T(8,128)(2,1)S(1)}, bf16[1,32,420]{2,1,0:T(8,128)(2,1)S(1)}, u32[]{:S(2)}, u32[]{:S(2)}) %collective-permute-start) | collective-permute-done | bytes 26912 | tf_op jit(solution)/shard_map/ppermute | solution.py:322
  29.3 0.0 copy-start.7
  29.3 0.3 collective-permute-start.1
  29.6 0.0 copy-done.13
  29.6 0.0 collective-permute-start.4
  29.6 0.1 dynamic_slice.10
  29.7 1.1 %collective-permute-done.4 = f32[64]{0:T(128)S(1)} collective-permute-done((f32[64]{0:T(128)S(1)}, f32[64]{0:T(128)S(1)}, u32[]{:S(2)}, u32[]{:S(2)}) %collective-permute-start.4) | collective-permute-done | bytes 288 | tf_op jit(solution)/shard_map/ppermute | solution.py:324
  30.7 0.1 dynamic_slice.11
  30.8 2.8 %collective-permute-done.1.b2 = bf16[2,32,420]{2,1,0:T(8,128)(2,1)S(1)} collective-permute-done((bf16[2,32,420]{2,1,0:T(8,128)(2,1)S(1)}, bf16[2,32,420]{2,1,0:T(8,128)(2,1)S(1)}, u32[]{:S(2)}, u32[]{:S(2)}) %collective-permute-start.1) | collective-permute-done | bytes 53792 | tf_op jit(solution)/shard_map/ppermute | solution.py:322
  33.7 0.0 copy-start.8
  33.7 0.7 pad_maximum_fusion
  34.3 0.9 %collective-permute-start.2 = (bf16[4,32,420]{2,1,0:T(8,128)(2,1)}, bf16[4,32,420]{2,1,0:T(8,128)(2,1)S(1)}, u32[]{:S(2)}, u32[]{:S(2)}) collective-permute-start(bf16[4,32,420]{2,1,0:T(8,128)(2,1)} %pad_maximum_fusion), channel_id=1, source_target_pairs={{0,2},{2,0},{4,6},{6,4},{8,10},{10,8},{12,14},{14,12},{1,3},{3,1},... | collective-permute-start | bytes 322568 | tf_op jit(solution)/shard_map/ppermute | solution.py:322
  35.2 0.1 pad_maximum_fusion.3
  35.3 0.7 broadcast_in_dim.14
  36.0 1.4 %broadcast_in_dim_reshape.8.noise = f32[128,1]{1,0:T(8,128)} reshape(f32[16,8]{1,0:T(8,128)} %broadcast_in_dim.14) | data formatting | bytes 1024 | tf_op jit(solution)/shard_map/broadcast_in_dim;reshape | solution.py:328
  37.4 2.1 %collective-permute-done.2.b3 = bf16[4,32,420]{2,1,0:T(8,128)(2,1)S(1)} collective-permute-done((bf16[4,32,420]{2,1,0:T(8,128)(2,1)}, bf16[4,32,420]{2,1,0:T(8,128)(2,1)S(1)}, u32[]{:S(2)}, u32[]{:S(2)}) %collective-permute-start.2) | collective-permute-done | bytes 107552 | tf_op jit(solution)/shard_map/ppermute | solution.py:322
  39.5 0.0 copy-start.9
  39.5 0.0 collective-permute-done.3.other
  39.5 0.0 copy-start.6
  39.5 0.0 copy-done.2
  39.5 0.0 copy-done.4
  39.5 0.0 copy-done.7
  39.5 0.0 copy-done.8
  39.6 0.6 copy-done.9
  40.2 0.2 copy-done.6
  40.4 10.4 %bins.1 = bf16[8,32,420]{2,1,0:T(8,128)(2,1)} custom-call(s32[1]{0:T(128)} %bitcast.index_ref, bf16[1,32,420]{2,1,0:T(8,128)(2,1)} %bitcast.15, bf16[1,32,420]{2,1,0:T(8,128)(2,1)} %copy-done.7, bf16[2,32,420]{2,1,0:T(8,128)(2,1)} %copy-done.8, bf16[4,32,420]{2,1,0:T(8,128)(2,1)} %copy-done.9, bf16[8,2,4,8,512]{4,3,2,1,0:T(8,128)(2,1)} %copy-done.2, ...), custom_call_target="tpu_custom_call" | custom-call | tf_op jit(solution)/shard_map/bins/pallas_call | solution.py:333
  50.8 3.4 %all-to-all-start.1 = ((bf16[8,32,420]{2,1,0:T(8,128)(2,1)}), bf16[8,32,420]{2,1,0:T(8,128)(2,1)S(1)}, u32[]{:S(2)}, u32[]{:S(2)}) async-start(bf16[8,32,420]{2,1,0:T(8,128)(2,1)} %bins.1), calls=%async_computation.1 | async-start | bytes 524288 | tf_op jit(solution)/shard_map/all_to_all | solution.py:349
  54.2 0.7 broadcast_in_dim.15
  54.9 0.7 broadcast_in_dim_reshape.9.prior
  55.6 0.0 copy-start.12
  55.6 0.0 collective-permute-done.5.basis_other
  55.6 6.8 %all-to-all-done.1.parts = bf16[8,32,420]{2,1,0:T(8,128)(2,1)S(1)} async-done(((bf16[8,32,420]{2,1,0:T(8,128)(2,1)}), bf16[8,32,420]{2,1,0:T(8,128)(2,1)S(1)}, u32[]{:S(2)}, u32[]{:S(2)}) %all-to-all-start.1) | async-done | bytes 215072 | tf_op jit(solution)/shard_map/all_to_all | solution.py:349
  62.4 0.0 copy-start.3
  62.4 0.7 copy-done.3
  63.1 3.4 %coeff.1 = (f32[8,1680]{1,0:T(8,128)}, bf16[8,8,1024]{2,1,0:T(8,128)(2,1)}) custom-call(bf16[8,32,420]{2,1,0:T(8,128)(2,1)} %copy-done.3, f32[32,1]{1,0:T(8,128)} %broadcast_in_dim_reshape.9.prior, bf16[1680,512]{1,0:T(8,128)(2,1)} %basis_own.3, bf16[1680,512]{1,0:T(8,128)(2,1)} %collective-permute-done.5.basis_other), custom_call_target="tpu_custom_call" | custom-call | tf_op jit(solution)/shard_map/coeff/pallas_call | solution.py:351
  66.5 3.4 %all-to-all-start.2 = ((bf16[8,8,1024]{2,1,0:T(8,128)(2,1)}), bf16[8,8,1024]{2,1,0:T(8,128)(2,1)S(1)}, u32[]{:S(2)}, u32[]{:S(2)}) async-start(bf16[8,8,1024]{2,1,0:T(8,128)(2,1)} %get-tuple-element.7), calls=%async_computation.2 | async-start | bytes 262144 | tf_op jit(solution)/shard_map/all_to_all | solution.py:363
  69.9 0.0 copy-done.12
  69.9 0.1 collective-permute-start.6
  69.9 1.1 %collective-permute-done.6 = f32[512]{0:T(512)S(1)} collective-permute-done((f32[512]{0:T(512)S(1)}, f32[512]{0:T(512)S(1)}, u32[]{:S(2)}, u32[]{:S(2)}) %collective-permute-start.6) | collective-permute-done | bytes 2080 | tf_op jit(solution)/shard_map/ppermute | solution.py:330
  71.1 0.6 pad_maximum_fusion.2
  71.7 5.4 %all-to-all-done.2.parts = bf16[8,8,1024]{2,1,0:T(8,128)(2,1)S(1)} async-done(((bf16[8,8,1024]{2,1,0:T(8,128)(2,1)}), bf16[8,8,1024]{2,1,0:T(8,128)(2,1)S(1)}, u32[]{:S(2)}, u32[]{:S(2)}) %all-to-all-start.2) | async-done | bytes 131104 | tf_op jit(solution)/shard_map/all_to_all | solution.py:363
  77.1 0.0 copy-start.5
  77.1 0.7 copy-done.5
  77.8 3.8 %deflate.1 = f32[8,4,420]{2,1,0:T(4,128)} custom-call(bf16[8,8,1024]{2,1,0:T(8,128)(2,1)} %copy-done.5, f32[1,1024]{1,0:T(1,128)} %bitcast.16, f32[8,1680]{1,0:T(8,128)} %get-tuple-element.8.flat, bf16[1680,512]{1,0:T(8,128)(2,1)} %basis_own.3, bf16[1680,512]{1,0:T(8,128)(2,1)} %collective-permute-done.5.basis_other), custom_call_target="tpu_custom_call" | custom-call | tf_op jit(solution)/shard_map/deflate/pallas_call | solution.py:364
  81.5 2.1 %all_gather.3 = f32[16,4,420]{2,1,0:T(4,128)S(1)} all-gather(f32[8,4,420]{2,1,0:T(4,128)} %deflate.1), channel_id=1, replica_groups=mesh['grp'=2,'pts'=8,'sen'=2] {'sen'}, dimensions={0}, use_global_device_ids=true | all-gather | bytes 161280 | tf_op jit(solution)/shard_map/all_gather | solution.py:371
  83.6 0.7 copy.24
  (3 shorter events, 0.1 us)
Async XLA Ops:
  0.0 1.0 %copy-start = (bf16[2,4,64,421]{3,2,1,0:T(8,128)(2,1)S(1)}, bf16[2,4,64,421]{3,2,1,0:T(8,128)(2,1)}, u32[]{:S(2)}) copy-start(bf16[2,4,64,421]{3,2,1,0:T(8,128)(2,1)} %param.9) | copy-start | bytes 1293316
  0.0 9.2 %copy-start.1 = (bf16[1680,512]{1,0:T(8,128)(2,1)S(1)}, bf16[1680,512]{1,0:T(8,128)(2,1)}, u32[]{:S(2)}) copy-start(bf16[1680,512]{1,0:T(8,128)(2,1)} %basis_own.3) | copy-start | bytes 5160964
  0.0 23.7 %copy-start.11 = (f32[4]{0:T(128)S(1)}, f32[4]{0:T(128)}, u32[]{:S(2)}) copy-start(f32[4]{0:T(128)} %param.11) | copy-start | bytes 52
  0.0 23.7 %copy-start.10 = (bf16[16,4,420]{2,1,0:T(4,128)(2,1)S(1)}, bf16[16,4,420]{2,1,0:T(4,128)(2,1)}, u32[]{:S(2)}) copy-start(bf16[16,4,420]{2,1,0:T(4,128)(2,1)} %param.8) | copy-start | bytes 161284
  0.0 29.6 %copy-start.13 = (f32[64]{0:T(128)S(1)}, f32[64]{0:T(128)}, u32[]{:S(2)}) copy-start(f32[64]{0:T(128)} %param.10) | copy-start | bytes 772
  1.9 21.8 %all-to-all-start = ((bf16[8,2,4,8,512]{4,3,2,1,0:T(8,128)(2,1)}), bf16[8,2,4,8,512]{4,3,2,1,0:T(8,128)(2,1)S(1)}, u32[]{:S(2)}, u32[]{:S(2)}) async-start(bf16[8,2,4,8,512]{4,3,2,1,0:T(8,128)(2,1)} %pad.4), calls=%async_computation | async-start | bytes 1048576 | tf_op jit(solution)/shard_map/all_to_all | solution.py:312
  9.2 46.4 %collective-permute-start.5 = (bf16[1680,512]{1,0:T(8,128)(2,1)S(1)}, bf16[1680,512]{1,0:T(8,128)(2,1)}, u32[]{:S(2)}, u32[]{:S(2)}) collective-permute-start(bf16[1680,512]{1,0:T(8,128)(2,1)S(1)} %copy-done.1), channel_id=1, source_target_pairs={{0,1},{1,0},{2,3},{3,2},{4,5},{5,4},{6,7},{7,6},{8,9},{9,8},{10,11... | collective-permute-start | bytes 5160968 | tf_op jit(solution)/shard_map/ppermute | solution.py:329
  23.7 15.8 %copy-start.2 = (bf16[8,2,4,8,512]{4,3,2,1,0:T(8,128)(2,1)}, bf16[8,2,4,8,512]{4,3,2,1,0:T(8,128)(2,1)S(1)}, u32[]{:S(2)}) copy-start(bf16[8,2,4,8,512]{4,3,2,1,0:T(8,128)(2,1)S(1)} %all-to-all-done.own) | copy-start | bytes 1572868
  23.7 15.8 %collective-permute-start.3 = (bf16[8,2,4,8,512]{4,3,2,1,0:T(8,128)(2,1)S(1)}, bf16[8,2,4,8,512]{4,3,2,1,0:T(8,128)(2,1)S(1)}, u32[]{:S(2)}, u32[]{:S(2)}) collective-permute-start(bf16[8,2,4,8,512]{4,3,2,1,0:T(8,128)(2,1)S(1)} %all-to-all-done.own), channel_id=1, source_target_pairs={{0,1},{1,0},{2,3},{3,2},{4,5},{5,4},{6,7},{7,6},{8,9},{9,8},{10,11... | collective-permute-start | bytes 1572872 | tf_op jit(solution)/shard_map/ppermute | solution.py:313
  23.8 15.7 %copy-start.4 = (bf16[4,8,420]{2,1,0:T(8,128)(2,1)}, bf16[4,8,420]{2,1,0:T(8,128)(2,1)S(1)}, u32[]{:S(2)}) copy-start(bf16[4,8,420]{2,1,0:T(8,128)(2,1)S(1)} %copy.22) | copy-start | bytes 80644
  23.8 5.5 %collective-permute-start = (bf16[1,32,420]{2,1,0:T(8,128)(2,1)S(1)}, bf16[1,32,420]{2,1,0:T(8,128)(2,1)S(1)}, u32[]{:S(2)}, u32[]{:S(2)}) collective-permute-start(bf16[1,32,420]{2,1,0:T(8,128)(2,1)S(1)} %bitcast.12), channel_id=1, source_target_pairs={{0,8},{2,10},{4,12},{6,14},{8,0},{10,2},{12,4},{14,6},{1,9},{3,11}... | collective-permute-start | bytes 80648 | tf_op jit(solution)/shard_map/ppermute | solution.py:322
  29.3 10.2 %copy-start.7 = (bf16[1,32,420]{2,1,0:T(8,128)(2,1)}, bf16[1,32,420]{2,1,0:T(8,128)(2,1)S(1)}, u32[]{:S(2)}) copy-start(bf16[1,32,420]{2,1,0:T(8,128)(2,1)S(1)} %collective-permute-done.b1) | copy-start | bytes 80644
  29.3 4.3 %collective-permute-start.1 = (bf16[2,32,420]{2,1,0:T(8,128)(2,1)S(1)}, bf16[2,32,420]{2,1,0:T(8,128)(2,1)S(1)}, u32[]{:S(2)}, u32[]{:S(2)}) collective-permute-start(bf16[2,32,420]{2,1,0:T(8,128)(2,1)S(1)} %pad_maximum_fusion.1), channel_id=1, source_target_pairs={{0,4},{2,6},{4,0},{6,2},{8,12},{10,14},{12,8},{14,10},{1,5},{3,7},... | collective-permute-start | bytes 161288 | tf_op jit(solution)/shard_map/ppermute | solution.py:322
  29.6 1.2 %collective-permute-start.4 = (f32[64]{0:T(128)S(1)}, f32[64]{0:T(128)S(1)}, u32[]{:S(2)}, u32[]{:S(2)}) collective-permute-start(f32[64]{0:T(128)S(1)} %copy-done.13), channel_id=1, source_target_pairs={{0,1},{1,0},{2,3},{3,2},{4,5},{5,4},{6,7},{7,6},{8,9},{9,8},{10,11... | collective-permute-start | bytes 776 | tf_op jit(solution)/shard_map/ppermute | solution.py:324
  33.7 5.9 %copy-start.8 = (bf16[2,32,420]{2,1,0:T(8,128)(2,1)}, bf16[2,32,420]{2,1,0:T(8,128)(2,1)S(1)}, u32[]{:S(2)}) copy-start(bf16[2,32,420]{2,1,0:T(8,128)(2,1)S(1)} %collective-permute-done.1.b2) | copy-start | bytes 161284
  34.3 5.2 %collective-permute-start.2 = (bf16[4,32,420]{2,1,0:T(8,128)(2,1)}, bf16[4,32,420]{2,1,0:T(8,128)(2,1)S(1)}, u32[]{:S(2)}, u32[]{:S(2)}) collective-permute-start(bf16[4,32,420]{2,1,0:T(8,128)(2,1)} %pad_maximum_fusion), channel_id=1, source_target_pairs={{0,2},{2,0},{4,6},{6,4},{8,10},{10,8},{12,14},{14,12},{1,3},{3,1},... | collective-permute-start | bytes 322568 | tf_op jit(solution)/shard_map/ppermute | solution.py:322
  39.5 0.7 copy-start.9
  39.5 0.8 %copy-start.6 = (bf16[8,2,4,8,512]{4,3,2,1,0:T(8,128)(2,1)}, bf16[8,2,4,8,512]{4,3,2,1,0:T(8,128)(2,1)S(1)}, u32[]{:S(2)}) copy-start(bf16[8,2,4,8,512]{4,3,2,1,0:T(8,128)(2,1)S(1)} %collective-permute-done.3.other) | copy-start | bytes 1572868
  50.8 11.6 %all-to-all-start.1 = ((bf16[8,32,420]{2,1,0:T(8,128)(2,1)}), bf16[8,32,420]{2,1,0:T(8,128)(2,1)S(1)}, u32[]{:S(2)}, u32[]{:S(2)}) async-start(bf16[8,32,420]{2,1,0:T(8,128)(2,1)} %bins.1), calls=%async_computation.1 | async-start | bytes 524288 | tf_op jit(solution)/shard_map/all_to_all | solution.py:349
  55.6 14.2 %copy-start.12 = (f32[512]{0:T(512)S(1)}, f32[512]{0:T(512)}, u32[]{:S(2)}) copy-start(f32[512]{0:T(512)} %param.13) | copy-start | bytes 6148
  62.4 0.7 copy-start.3
  66.5 10.7 %all-to-all-start.2 = ((bf16[8,8,1024]{2,1,0:T(8,128)(2,1)}), bf16[8,8,1024]{2,1,0:T(8,128)(2,1)S(1)}, u32[]{:S(2)}, u32[]{:S(2)}) async-start(bf16[8,8,1024]{2,1,0:T(8,128)(2,1)} %get-tuple-element.7), calls=%async_computation.2 | async-start | bytes 262144 | tf_op jit(solution)/shard_map/all_to_all | solution.py:363
  69.9 1.2 %collective-permute-start.6 = (f32[512]{0:T(512)S(1)}, f32[512]{0:T(512)S(1)}, u32[]{:S(2)}, u32[]{:S(2)}) collective-permute-start(f32[512]{0:T(512)S(1)} %copy-done.12), channel_id=1, source_target_pairs={{0,1},{1,0},{2,3},{3,2},{4,5},{5,4},{6,7},{7,6},{8,9},{9,8},{10,11... | collective-permute-start | bytes 6152 | tf_op jit(solution)/shard_map/ppermute | solution.py:330
  77.1 0.7 copy-start.5

commit v2 on v0

--- a/solution.py
+++ b/solution.py
@@ -1,9 +1,16 @@
+import functools
 import math
 
 import jax
 import jax.numpy as jnp
+import numpy as np
 from jax import lax
+from jax.experimental import pallas as pl
+from jax.experimental.pallas import tpu as pltpu
 from jax.sharding import PartitionSpec as P
+
+LANES = 128
+ROWS = 8
 
 
 def tables(steps_count):
@@ -117,6 +124,416 @@
     return (flat - correction).reshape(probe_count, point_count, steps_count)
 
 
+def round_up(value, step):
+    return (value + step - 1) // step * step
+
+
+def packed_tables(steps_count, wide):
+    bins_count = steps_count + 1
+    turns = np.arange(steps_count)[:, None] * np.arange(bins_count)[None, :] % (2 * steps_count)
+    angle = turns.astype(np.float64) * (math.pi / steps_count)
+    table = np.zeros((wide, 2 * wide), np.float32)
+    table[:steps_count, :bins_count] = np.cos(angle)
+    table[:steps_count, wide : wide + bins_count] = -np.sin(angle)
+    weights = np.zeros((1, wide), np.float32)
+    weights[0, :bins_count] = 2.0 / (2.0 * steps_count)
+    weights[0, 0] = weights[0, steps_count] = 1.0 / (2.0 * steps_count)
+    return jnp.asarray(table.astype(jnp.bfloat16)), jnp.asarray(weights)
+
+
+NT = (((1,), (1,)), ((), ()))
+
+
+class Packing:
+    def __init__(self, rows, length):
+        self.full = length // LANES
+        self.tail = length % LANES
+        self.slots = LANES // self.tail
+        self.first_tail = rows * self.full
+        self.tiles = self.first_tail + -(-rows // self.slots)
+
+    def place(self, row):
+        return self.first_tail + row // self.slots, row % self.slots * self.tail
+
+
+def turned(tile, lanes):
+    lanes = lanes % LANES
+    return pltpu.roll(tile, lanes, axis=tile.ndim - 1) if lanes else tile
+
+
+def store_packed(out_tile, packing, row, value, merged):
+    for t in range(packing.full):
+        lanes = slice(t * LANES, (t + 1) * LANES)
+        out_tile(row * packing.full + t, value[..., lanes].astype(jnp.bfloat16))
+    tile, lane = packing.place(row)
+    tail = value[..., packing.full * LANES : (packing.full + 1) * LANES]
+    where = lax.broadcasted_iota(jnp.int32, tail.shape, tail.ndim - 1)
+    tail = turned(jnp.where(where < packing.tail, tail, 0.0), lane)
+    merged[tile] = merged[tile] + tail if tile in merged else tail
+
+
+def store_tails(out_tile, merged):
+    for tile, value in merged.items():
+        out_tile(tile, value.astype(jnp.bfloat16))
+
+
+def pack_kernel(
+    core, prior_far, kernel, probes, out, prior, kernel_here, probes_here, sems, *, packing
+):
+    f32 = jnp.float32
+    width, _, sens, _ = out.shape
+    half, points, _ = probes_here.shape
+    edge = packing.full * LANES
+    mine = pl.multiple_of(core[0] * half, half)
+    copies = [pltpu.make_async_copy(probes.at[pl.ds(mine, half)], probes_here, sems.at[0])]
+    for row in range(2 * points):
+        at = (row // points, row % points)
+        copies.append(
+            pltpu.make_async_copy(kernel.at[at], kernel_here.at[at], sems.at[row + 1])
+        )
+    copies.append(pltpu.make_async_copy(prior_far, prior, sems.at[2 * points + 1]))
+    for copy in copies:
+        copy.start()
+
+    def out_tile(tile, value):
+        out[:, tile] = value
+
+    def padded(value):
+        missing = jnp.zeros((value.shape[0], edge + LANES - value.shape[1]), f32)
+        return jnp.concatenate([value, missing], axis=1)
+
+    merged = {}
+    copies[-1].wait()
+    copies[0].wait()
+    scaled = probes_here[...].astype(f32)
+    for p in range(points):
+        value = padded(scaled[:, p, :] * prior[p])
+        value = jnp.broadcast_to(value[None], (width, sens, edge + LANES))
+        store_packed(out_tile, packing, 2 * points + p, value, merged)
+    for row in range(2 * points):
+        copies[row + 1].wait()
+        value = padded(kernel_here[row // points, row % points].astype(f32))
+        store_packed(out_tile, packing, row, value.reshape(width, sens, edge + LANES), merged)
+    store_tails(out_tile, merged)
+
+
+def unpack(source, j, row, packing):
+    f32 = jnp.float32
+    tiles = [source[j, row * packing.full + t].astype(f32) for t in range(packing.full)]
+    tile, lane = packing.place(row)
+    tiles.append(turned(source[j, tile].astype(f32), -lane))
+    return tiles
+
+
+def widen(source, kern, *, packing, width, points):
+    def step(j, carry):
+        for p in range(points):
+            real = unpack(source, j, p, packing)
+            imag = unpack(source, j, points + p, packing)
+            for t, (a, b) in enumerate(zip(real, imag)):
+                lanes = slice(t * LANES, (t + 1) * LANES)
+                kern[0, j * points + p, :, lanes] = a
+                kern[1, j * points + p, :, lanes] = a + b
+                kern[2, j * points + p, :, lanes] = a - b
+        return carry
+
+    lax.fori_loop(0, width, step, 0)
+
+
+def forward_sum(kern, spec, weights, data, base, *, width, points, sens, probes_half, wide):
+    f32 = jnp.float32
+
+    def tile_step(ft, carry):
+        lanes = pl.ds(pl.multiple_of(ft * LANES, LANES), LANES)
+        shifted = pl.ds(pl.multiple_of(wide + ft * LANES, LANES), LANES)
+
+        def source(j, acc):
+            acc = list(acc)
+            for p in range(points):
+                q = j * points + p
+                at = pl.ds(pl.multiple_of(q * probes_half, ROWS), probes_half)
+                both = spec[0, at, lanes]
+                imag = spec[1, at, lanes]
+                real = spec[2, at, lanes]
+                for s in range(sens):
+                    row = slice(s, s + 1)
+                    acc[3 * s] += kern[0, q, row, lanes] * both
+                    acc[3 * s + 1] += kern[1, q, row, lanes] * imag
+                    acc[3 * s + 2] += kern[2, q, row, lanes] * real
+            return tuple(acc)
+
+        zero = jnp.zeros((probes_half, LANES), f32)
+        acc = lax.fori_loop(0, width, source, (zero,) * (3 * sens))
+        factor = weights[:, lanes]
+        for s in range(sens):
+            at = slice(base + s * probes_half, base + (s + 1) * probes_half)
+            data[at, lanes] = (acc[3 * s] - acc[3 * s + 1]) * factor
+            data[at, shifted] = (acc[3 * s] - acc[3 * s + 2]) * factor
+        return carry
+
+    lax.fori_loop(0, wide // LANES, tile_step, 0)
+
+
+def own_kernel(own, table, weights, spec, kern, data, rows, *, sizes, packing):
+    width, points, half = sizes["width"], sizes["points"], sizes["probes_half"]
+    wide = sizes["wide"]
+    for j in range(width):
+        for p in range(points):
+            at = slice((j * points + p) * half, (j * points + p + 1) * half)
+            for t, tile in enumerate(unpack(own, j, 2 * points + p, packing)):
+                rows[at, t * LANES : (t + 1) * LANES] = tile
+    got = jnp.dot(rows[...].astype(jnp.bfloat16), table[...], preferred_element_type=jnp.float32)
+    real = got[:, :wide]
+    imag = got[:, wide:]
+    spec[0] = real + imag
+    spec[1] = imag
+    spec[2] = real
+    widen(own, kern, packing=packing, width=width, points=points)
+    forward_sum(kern, spec, weights, data, 0, **sizes)
+
+
+def bins_kernel(
+    index, noise_own, noise_other, other, spec, kern_own, data_own, table, weights, out,
+    kern, data, wdata, adjoint,
+    *, sizes, packing, packing_back,
+):
+    width, points, sens = sizes["width"], sizes["points"], sizes["sens"]
+    probes_half, wide = sizes["probes_half"], sizes["wide"]
+    tiles = wide // LANES
+    f32 = jnp.float32
+    half_rows = sens * probes_half
+    widen(other, kern, packing=packing, width=width, points=points)
+    forward_sum(kern, spec, weights, data, half_rows, **sizes)
+    data[:half_rows] = data_own[...]
+    table_v = table[...]
+    observed = lax.dot_general(
+        data[...].astype(jnp.bfloat16), table_v, NT, preferred_element_type=f32
+    )
+    first = index[0] * sens
+    scales = [noise_own[first + s] for s in range(sens)]
+    scales += [noise_other[first + s] for s in range(sens)]
+    residual = jnp.concatenate(
+        [
+            (observed[s * probes_half : (s + 1) * probes_half] * scale)
+            for s, scale in enumerate(scales)
+        ],
+        axis=0,
+    ).astype(jnp.bfloat16)
+    weighted = jnp.dot(residual, table_v, preferred_element_type=f32)
+    weight_rows = weights[...]
+    real = weighted[:, :wide] * weight_rows
+    imag = weighted[:, wide:] * weight_rows
+    wdata[0] = real + imag
+    wdata[1] = imag
+    wdata[2] = real
+
+    def adjoint_tile(step, carry):
+        j = step // tiles
+        ft = step % tiles
+        lanes = pl.ds(pl.multiple_of(ft * LANES, LANES), LANES)
+        shifted = pl.ds(pl.multiple_of(wide + ft * LANES, LANES), LANES)
+        zero = jnp.zeros((probes_half, LANES), f32)
+        acc = [zero] * (3 * points)
+        for half, source in ((0, kern_own), (1, kern)):
+            for s in range(sens):
+                at = slice(half * half_rows + s * probes_half, half * half_rows + (s + 1) * probes_half)
+                both = wdata[0, at, lanes]
+                imag = wdata[1, at, lanes]
+                real = wdata[2, at, lanes]
+                row = slice(s, s + 1)
+                for p in range(points):
+                    q = j * points + p
+                    acc[3 * p] += source[0, q, row, lanes] * both
+                    acc[3 * p + 1] += source[2, q, row, lanes] * imag
+                    acc[3 * p + 2] += source[1, q, row, lanes] * real
+        for p in range(points):
+            at = pl.ds(pl.multiple_of((j * points + p) * probes_half, ROWS), probes_half)
+            adjoint[at, lanes] = acc[3 * p] - acc[3 * p + 1]
+            adjoint[at, shifted] = acc[3 * p] - acc[3 * p + 2]
+        return carry
+
+    lax.fori_loop(0, width * tiles, adjoint_tile, 0)
+    back = lax.dot_general(
+        adjoint[...].astype(jnp.bfloat16), table_v, NT, preferred_element_type=f32
+    )
+    back = back.reshape(width, points, probes_half, wide)
+
+    def out_tile(tile, value):
+        out[:, tile] = value
+
+    merged = {}
+    for p in range(points):
+        store_packed(out_tile, packing_back, p, back[:, p], merged)
+    store_tails(out_tile, merged)
+
+
+def summed(parts):
+    total = parts[0].astype(jnp.float32)
+    for j in range(1, parts.shape[0]):
+        total += parts[j].astype(jnp.float32)
+    return total
+
+
+def coeff_kernel(prior, parts, basis_own, basis_other, flat, coeff, *, points, steps, rank, packing):
+    f32 = jnp.float32
+    total = summed(parts)
+    for p in range(points):
+        tiles = [total[p * packing.full + t] for t in range(packing.full)]
+        tile, lane = packing.place(p)
+        tiles.append(turned(total[tile], -lane))
+        piece = jnp.concatenate(tiles, axis=1) * prior[p]
+        flat[:, p * steps : (p + 1) * steps] = piece[:, :steps]
+    low = flat[...].astype(jnp.bfloat16)
+    own = jnp.dot(low, basis_own[...], preferred_element_type=f32).astype(jnp.bfloat16)
+    other = jnp.dot(low, basis_other[...], preferred_element_type=f32).astype(jnp.bfloat16)
+    for j in range(coeff.shape[0]):
+        coeff[j, :, :rank] = own
+        coeff[j, :, rank:] = other
+
+
+def deflate_kernel(
+    core, parts_own, parts_other, deflation_own, deflation_other, flat_own, flat_other,
+    basis_own, basis_other, out,
+    *, points, steps, rank,
+):
+    f32 = jnp.float32
+    bf16 = jnp.bfloat16
+    own = summed(parts_own)
+    other = summed(parts_other)
+    half = own.shape[0]
+    here = jnp.concatenate([own[:, :rank], other[:, rank:]], axis=0) * deflation_own[...]
+    there = jnp.concatenate([own[:, rank:], other[:, :rank]], axis=0) * deflation_other[...]
+    correction = lax.dot_general(here.astype(bf16), basis_own[...], NT, preferred_element_type=f32)
+    correction += lax.dot_general(there.astype(bf16), basis_other[...], NT, preferred_element_type=f32)
+    result = jnp.concatenate([flat_own[...], flat_other[...]], axis=0) - correction
+    mine = core[0] * half
+    for p in range(points):
+        piece = result[:, p * steps : (p + 1) * steps]
+        out[pl.ds(mine, half), p, :] = piece[:half]
+        out[pl.ds(half - mine, half), p, :] = piece[half:]
+
+
+def kept(space, *values):
+    return [pltpu.with_memory_space_constraint(value, space) for value in values]
+
+
+def in_vmem(count):
+    return [pl.BlockSpec(memory_space=pltpu.VMEM) for _ in range(count)]
+
+
+def in_smem(count):
+    return [pl.BlockSpec(memory_space=pltpu.SMEM) for _ in range(count)]
+
+
+def limit(mib):
+    return pltpu.CompilerParams(vmem_limit_bytes=mib * 1024 * 1024)
+
+
+def local_split(probes, kernel, noise_weight, prior_scale, basis, deflation):
+    bf16 = jnp.bfloat16
+    f32 = jnp.float32
+    probe_count, points, steps = probes.shape
+    bins_count = steps + 1
+    width = lax.axis_size("pts")
+    sens = noise_weight.shape[0] // width
+    half = probe_count // 2
+    rank = basis.shape[1]
+    wide = round_up(bins_count, LANES)
+    me = jnp.full((1,), lax.axis_index("pts"), jnp.int32)
+    core_index = lax.axis_index("sen")
+    core = jnp.full((1,), core_index, jnp.int32)
+
+    def swap(value):
+        return lax.ppermute(value, "sen", [(0, 1), (1, 0)])
+
+    def exchange(value):
+        return lax.all_to_all(value, "pts", split_axis=0, concat_axis=0, tiled=False)
+
+    table, weights = packed_tables(steps, wide)
+    sizes = dict(width=width, points=points, sens=sens, probes_half=half, wide=wide)
+    all_rows = width * points * half
+
+    packing = Packing(3 * points, bins_count)
+    packing_back = Packing(points, steps)
+    in_hbm = pl.BlockSpec(memory_space=pltpu.HBM)
+    send = pl.pallas_call(
+        functools.partial(pack_kernel, packing=packing),
+        out_shape=pltpu.VMEM((width, packing.tiles, sens, LANES), bf16),
+        in_specs=in_smem(1) + [in_hbm] * 3,
+        out_specs=in_vmem(1)[0],
+        scratch_shapes=[
+            pltpu.SMEM(prior_scale.shape, f32),
+            pltpu.VMEM(kernel.shape, bf16),
+            pltpu.VMEM((half, points, steps), bf16),
+            pltpu.SemaphoreType.DMA((2 * points + 2,)),
+        ],
+        compiler_params=limit(8),
+        name="pack",
+    )(core, *kept(pltpu.HBM, prior_scale, kernel, probes))
+    own = exchange(send)
+    noise_other = swap(noise_weight)
+    deflation_other = swap(deflation)
+    basis_other = swap(basis)
+    basis, basis_other = kept(pltpu.VMEM, basis, basis_other)
+    other = swap(own)
+    other, basis_other, noise_other, deflation_other = lax.optimization_barrier(
+        (other, basis_other, noise_other, deflation_other)
+    )
+    spec, kern_own, data_own = pl.pallas_call(
+        functools.partial(own_kernel, sizes=sizes, packing=packing),
+        out_shape=(
+            jax.ShapeDtypeStruct((3, all_rows, wide), f32),
+            jax.ShapeDtypeStruct((3, width * points, sens, wide), f32),
+            jax.ShapeDtypeStruct((sens * half, 2 * wide), f32),
+        ),
+        in_specs=in_vmem(3),
+        out_specs=tuple(in_vmem(3)),
+        scratch_shapes=[pltpu.VMEM((all_rows, wide), f32)],
+        compiler_params=limit(10),
+        name="own",
+    )(own, table, weights)
+    back = pl.pallas_call(
+        functools.partial(bins_kernel, sizes=sizes, packing=packing, packing_back=packing_back),
+        out_shape=pltpu.VMEM((width, packing_back.tiles, half, LANES), bf16),
+        in_specs=in_smem(3) + in_vmem(6),
+        out_specs=in_vmem(1)[0],
+        scratch_shapes=[
+            pltpu.VMEM((3, width * points, sens, wide), f32),
+            pltpu.VMEM((2 * sens * half, 2 * wide), f32),
+            pltpu.VMEM((3, 2 * sens * half, wide), f32),
+            pltpu.VMEM((all_rows, 2 * wide), f32),
+        ],
+        compiler_params=limit(20),
+        name="bins",
+    )(me, noise_weight, noise_other, other, spec, kern_own, data_own, table, weights)
+    parts = exchange(back)
+    flat, coeff = pl.pallas_call(
+        functools.partial(coeff_kernel, points=points, steps=steps, rank=rank, packing=packing_back),
+        out_shape=(
+            jax.ShapeDtypeStruct((half, points * steps), f32),
+            jax.ShapeDtypeStruct((width, half, 2 * rank), bf16),
+        ),
+        in_specs=in_smem(1) + in_vmem(3),
+        out_specs=tuple(in_vmem(2)),
+        compiler_params=limit(12),
+        name="coeff",
+    )(prior_scale, parts, basis, basis_other)
+    flat_other = swap(flat)
+    coeff_parts = exchange(coeff)
+    coeff_other = swap(coeff_parts)
+    return pl.pallas_call(
+        functools.partial(deflate_kernel, points=points, steps=steps, rank=rank),
+        out_shape=jax.ShapeDtypeStruct((probe_count, points, steps), f32),
+        in_specs=in_smem(1) + in_vmem(8),
+        out_specs=in_vmem(1)[0],
+        compiler_params=limit(12),
+        name="deflate",
+    )(
+        core, coeff_parts, coeff_other, deflation[None, :], deflation_other[None, :],
+        flat, flat_other, basis, basis_other,
+    )
+
+
 def solution(mesh):
     placed = (
         P(None, ("grp", "pts"), None),
@@ -126,6 +543,15 @@
         P("pts", "sen"),
         P("sen"),
     )
+
+    def body(*args):
+        width = mesh.shape["pts"]
+        split = mesh.shape["sen"] == 2 and width > 1
+        whole_tiles = args[2].shape[0] == width * ROWS and args[0].shape[0] == 2 * ROWS
+        if not (split and whole_tiles):
+            return local(*args)
+        return local_split(*args)
+
     return jax.shard_map(
-        local, mesh=mesh, in_specs=placed, out_specs=P(None, ("grp", "pts"), None), check_vma=False
-    )
+        body, mesh=mesh, in_specs=placed, out_specs=P(None, ("grp", "pts"), None), check_vma=False
+    )

time: 195 us -> 66.9 us (0.34)
  local copies, waits for them, and re-layouts: 71.9 us -> 1.25 us
  blocking collectives: 62.9 us -> 23 us
  matrix products: 19.2 us -> 0 us
  Pallas kernels: 0 us -> 15.5 us
  other arithmetic: 12.7 us -> 0 us
  waiting for transfers between devices: 10.7 us -> 18.2 us
  starting transfers between devices: 15.8 us -> 8.47 us
    psum x3 -> x0, blocking collectives: 41 us -> none  [the longest x1 33.8 us: local(): coeff = lax.psum(coeff, 'pts')]
    unnamed x38 -> x14, local copies, waits for them, and re-layouts: 27.4 us -> 1.25 us
    dot_general x14 -> x0, matrix products: 19.2 us -> none  [the longest x1 2.58 us: local(): observed = jnp.dot(data_rows, inverse.T, precision=highest)]
    pallas_call x0 -> x5, Pallas kernels: none -> 15.5 us  [the longest x1 6.76 us: local_split(): pl.pallas_call(functools.partial(bins_kernel, sizes=sizes, packing=packin...]
    reshape x8 -> x0, local copies, waits for them, and re-layouts: 13.1 us -> none  [the longest x2 5.18 us: local(): spectrum.reshape(probe_count, point_count, 2, bins_count)]
    all_to_all x7 -> x0, local copies, waits for them, and re-layouts: 11.5 us -> none  [the longest x2 3.68 us: local(): lax.all_to_all(adj_bins.astype(jnp.bfloat16), 'pts', split_axis=1, concat...]
    another operation x7 -> x0, local copies, waits for them, and re-layouts: 9.83 us -> none  [the longest x4 7.36 us: local(): jnp.stack([data_real, data_imag], axis=2)]
    slice x7 -> x0, local copies, waits for them, and re-layouts: 9.73 us -> none  [the longest x2 4.22 us: local(): bin_kern_imag = kern_bins[1]]
  transfers between devices with their start and end apart: 3 -> 7, of which waited for: 3 -> 2; matrix products, arithmetic and copies ran while one was open for 8% -> 0% of each run, Pallas kernels for 0% -> 5%
where the time goes in v2:
time: 66.9 us; the launch traced here: 66.5 us
  blocking collectives  23 us (34%)
  waiting for transfers between devices  18.2 us (27%)
  Pallas kernels  15.5 us (23%)
  starting transfers between devices  8.47 us (13%)
  local copies, waits for them, and re-layouts  1.25 us (2%)
    all_to_all x2, blocking collectives, exchange(): lax.all_to_all(value, 'pts', split_axis=0, concat_axis=0, tiled=False)  23 us
    all_to_all x1, waiting for transfers between devices, exchange(): lax.all_to_all(value, 'pts', split_axis=0, concat_axis=0, tiled=False)  17.3 us
    all_to_all x1, starting transfers between devices, exchange(): lax.all_to_all(value, 'pts', split_axis=0, concat_axis=0, tiled=False)  7.31 us
    pallas_call x1, Pallas kernels, local_split(): pl.pallas_call(functools.partial(bins_kernel, sizes=sizes, packing=packin...  6.76 us
    pallas_call x1, Pallas kernels, local_split(): pl.pallas_call(functools.partial(own_kernel, sizes=sizes, packing=packing...  3.47 us
    pallas_call x1, Pallas kernels, local_split(): pl.pallas_call(functools.partial(pack_kernel, packing=packing), out_shape...  2.37 us
    pallas_call x1, Pallas kernels, local_split(): pl.pallas_call(functools.partial(deflate_kernel, points=points, steps=ste...  1.77 us
  transfers between devices with their start and end apart: 7, of which 2 were waited for; matrix products, arithmetic and copies ran while one was open for 0% of the time, Pallas kernels for 5%

profile of v2, /device:TPU:0, one launch (start us, length us, event | category | flops | bytes accessed | tf_op | source)
XLA Modules:
  0.0 66.5 jit_solution(9767471322007647800)
XLA Ops:
  0.0 0.0 copy-start.3
  0.0 0.0 copy-start
  0.0 0.0 copy-start.4
  0.0 0.0 copy-start.6
  0.0 2.4 %pack.1 = bf16[8,40,8,128]{3,2,1,0:T(8,128)(2,1)} custom-call(s32[1]{0:T(128)} %bitcast.core, f32[4]{0:T(128)} %prior.1, bf16[2,4,64,421]{3,2,1,0:T(8,128)(2,1)} %kernel.1, bf16[16,4,420]{2,1,0:T(4,128)(2,1)} %probes.1), custom_call_target="tpu_custom_call" | custom-call | tf_op jit(solution)/shard_map/pack/pallas_call | solution.py:459
  2.4 7.3 %all-to-all-start = ((bf16[8,40,8,128]{3,2,1,0:T(8,128)(2,1)}), bf16[8,40,8,128]{3,2,1,0:T(8,128)(2,1)}, u32[]{:S(2)}, u32[]{:S(2)}) async-start(bf16[8,40,8,128]{3,2,1,0:T(8,128)(2,1)} %pack.1), calls=%async_computation | async-start | bytes 1310720 | tf_op jit(solution)/shard_map/all_to_all | solution.py:450
  9.7 0.0 copy-done
  9.7 0.1 collective-permute-start.1
  9.8 17.3 %all-to-all-done.own = bf16[8,40,8,128]{3,2,1,0:T(8,128)(2,1)} async-done(((bf16[8,40,8,128]{3,2,1,0:T(8,128)(2,1)}), bf16[8,40,8,128]{3,2,1,0:T(8,128)(2,1)}, u32[]{:S(2)}, u32[]{:S(2)}) %all-to-all-start) | async-done | bytes 655392 | tf_op jit(solution)/shard_map/all_to_all | solution.py:450
  27.1 0.0 collective-permute-start
  27.1 0.0 copy-done.4
  27.1 0.5 collective-permute-start.3
  27.6 0.0 copy-done.6
  27.6 0.1 collective-permute-start.2
  27.7 0.0 copy-done.3
  27.7 0.0 copy-start.1
  27.7 1.2 %copy-done.1 = bf16[512,1024]{1,0:T(8,128)(2,1)S(1)} copy-done((bf16[512,1024]{1,0:T(8,128)(2,1)S(1)}, bf16[512,1024]{1,0:T(8,128)(2,1)}, u32[]{:S(2)}) %copy-start.1) | copy-done | bytes 1048600
  28.9 0.0 copy-start.2
  28.9 3.5 %own.1 = (f32[3,256,512]{2,1,0:T(8,128)S(1)}, f32[3,32,8,512]{3,2,1,0:T(8,128)S(1)}, f32[64,1024]{1,0:T(8,128)S(1)}) custom-call(bf16[8,40,8,128]{3,2,1,0:T(8,128)(2,1)} %all-to-all-done.own, bf16[512,1024]{1,0:T(8,128)(2,1)S(1)} %copy-done.1, f32[1,512]{1,0:T(1,128)S(1)} %copy-done.3), custom_call_target="tpu_custom_call" | custom-call | tf_op jit(solution)/shard_map/own/pallas_call | solution.py:482
  32.4 0.0 collective-permute-done.2.noise_other
  32.4 0.0 collective-permute-done.3
  32.4 0.0 collective-permute-done.1.basis_other
  32.4 0.0 collective-permute-done.other
  32.4 0.0 copy-done.2
  32.5 0.0 copy-start.5
  32.5 6.8 %bins.1 = bf16[8,14,8,128]{3,2,1,0:T(8,128)(2,1)S(1)} custom-call(s32[1]{0:T(128)} %bitcast.1.index, f32[64]{0:T(128)S(1)} %copy-done.6, f32[64]{0:T(128)S(1)} %collective-permute-done.2.noise_other, bf16[8,40,8,128]{3,2,1,0:T(8,128)(2,1)} %collective-permute-done.other, f32[3,256,512]{2,1,0:T(8,128)S(1)} %get-tuple-element.16.spec, ...), custom_call_target="tpu_custom_call" | custom-call | tf_op jit(solution)/shard_map/bins/pallas_call | solution.py:495
  39.2 12.5 %all_to_all.15.parts = bf16[8,14,8,128]{3,2,1,0:T(8,128)(2,1)S(1)} all-to-all(bf16[8,14,8,128]{3,2,1,0:T(8,128)(2,1)S(1)} %bins.1), channel_id=1, replica_groups=mesh['grp'=2,'pts'=8,'sen'=2] {'pts'}, dimensions={0} | all-to-all | bytes 458752 | tf_op jit(solution)/shard_map/all_to_all | solution.py:450
  51.7 0.0 copy-done.5
  51.7 1.1 %coeff.1 = (f32[8,1680]{1,0:T(8,128)S(1)}, bf16[8,8,1024]{2,1,0:T(8,128)(2,1)S(1)}) custom-call(f32[4]{0:T(128)S(1)} %copy-done.5, bf16[8,14,8,128]{3,2,1,0:T(8,128)(2,1)S(1)} %all_to_all.15.parts, bf16[1680,512]{1,0:T(8,128)(2,1)S(1)} %copy-done, bf16[1680,512]{1,0:T(8,128)(2,1)S(1)} %collective-permute-done.1.basis_other), custom_call_target="tpu_custom_call" | custom-call | tf_op jit(solution)/shard_map/coeff/pallas_call | solution.py:510
  52.8 10.5 %all_to_all.16.parts_own = bf16[8,8,1024]{2,1,0:T(8,128)(2,1)S(1)} all-to-all(bf16[8,8,1024]{2,1,0:T(8,128)(2,1)S(1)} %get-tuple-element.20), channel_id=1, replica_groups=mesh['grp'=2,'pts'=8,'sen'=2] {'pts'}, dimensions={0} | all-to-all | bytes 262144 | tf_op jit(solution)/shard_map/all_to_all | solution.py:450
  63.3 0.0 collective-permute-start.4
  63.3 0.5 collective-permute-start.5
  63.8 0.9 %collective-permute-done.5.flat_other = f32[8,1680]{1,0:T(8,128)S(1)} collective-permute-done((f32[8,1680]{1,0:T(8,128)S(1)}, f32[8,1680]{1,0:T(8,128)S(1)}, u32[]{:S(2)}, u32[]{:S(2)}) %collective-permute-start.5) | collective-permute-done | bytes 53792 | tf_op jit(solution)/shard_map/ppermute | solution.py:447
  64.8 0.0 collective-permute-done.4.parts_other
  64.8 1.8 %deflate.1 = f32[16,4,420]{2,1,0:T(4,128)} custom-call(s32[1]{0:T(128)} %bitcast.core, bf16[8,8,1024]{2,1,0:T(8,128)(2,1)S(1)} %all_to_all.16.parts_own, bf16[8,8,1024]{2,1,0:T(8,128)(2,1)S(1)} %collective-permute-done.4.parts_other, f32[1,512]{1,0:T(1,128)S(1)} %bitcast.4, f32[1,512]{1,0:T(1,128)S(1)} %bitcast.5, f32[8,1680]{1,0:T(8,128)S(1)} %get-tuple-element.22.flat_own, ...), custom_call_target="tpu_custom_call" | custom-call | tf_op jit(solution)/shard_map/deflate/pallas_call | solution.py:524
Async XLA Ops:
  0.0 27.7 %copy-start.3 = (f32[1,512]{1,0:T(1,128)S(1)}, f32[1,512]{1,0:T(1,128)}, u32[]{:S(2)}) copy-start(f32[1,512]{1,0:T(1,128)} %constant.13.clone.weights) | copy-start | bytes 6148
  0.0 9.7 %copy-start = (bf16[1680,512]{1,0:T(8,128)(2,1)S(1)}, bf16[1680,512]{1,0:T(8,128)(2,1)}, u32[]{:S(2)}) copy-start(bf16[1680,512]{1,0:T(8,128)(2,1)} %basis_own.3) | copy-start | bytes 5160964
  0.0 27.1 %copy-start.4 = (f32[512]{0:T(512)S(1)}, f32[512]{0:T(512)}, u32[]{:S(2)}) copy-start(f32[512]{0:T(512)} %param.13) | copy-start | bytes 6148
  0.0 27.6 %copy-start.6 = (f32[64]{0:T(128)S(1)}, f32[64]{0:T(128)}, u32[]{:S(2)}) copy-start(f32[64]{0:T(128)} %noise_own.1) | copy-start | bytes 772
  2.4 24.7 %all-to-all-start = ((bf16[8,40,8,128]{3,2,1,0:T(8,128)(2,1)}), bf16[8,40,8,128]{3,2,1,0:T(8,128)(2,1)}, u32[]{:S(2)}, u32[]{:S(2)}) async-start(bf16[8,40,8,128]{3,2,1,0:T(8,128)(2,1)} %pack.1), calls=%async_computation | async-start | bytes 1310720 | tf_op jit(solution)/shard_map/all_to_all | solution.py:450
  9.7 22.7 %collective-permute-start.1 = (bf16[1680,512]{1,0:T(8,128)(2,1)S(1)}, bf16[1680,512]{1,0:T(8,128)(2,1)S(1)}, u32[]{:S(2)}, u32[]{:S(2)}) collective-permute-start(bf16[1680,512]{1,0:T(8,128)(2,1)S(1)} %copy-done), channel_id=1, source_target_pairs={{0,1},{1,0},{2,3},{3,2},{4,5},{5,4},{6,7},{7,6},{8,9},{9,8},{10,11... | collective-permute-start | bytes 5160968 | tf_op jit(solution)/shard_map/ppermute | solution.py:447
  27.1 5.3 %collective-permute-start = (bf16[8,40,8,128]{3,2,1,0:T(8,128)(2,1)}, bf16[8,40,8,128]{3,2,1,0:T(8,128)(2,1)}, u32[]{:S(2)}, u32[]{:S(2)}) collective-permute-start(bf16[8,40,8,128]{3,2,1,0:T(8,128)(2,1)} %all-to-all-done.own), channel_id=1, source_target_pairs={{0,1},{1,0},{2,3},{3,2},{4,5},{5,4},{6,7},{7,6},{8,9},{9,8},{10,11... | collective-permute-start | bytes 1966088 | tf_op jit(solution)/shard_map/ppermute | solution.py:447
  27.1 5.3 %collective-permute-start.3 = (f32[512]{0:T(512)S(1)}, f32[512]{0:T(512)S(1)}, u32[]{:S(2)}, u32[]{:S(2)}) collective-permute-start(f32[512]{0:T(512)S(1)} %copy-done.4), channel_id=1, source_target_pairs={{0,1},{1,0},{2,3},{3,2},{4,5},{5,4},{6,7},{7,6},{8,9},{9,8},{10,11... | collective-permute-start | bytes 6152 | tf_op jit(solution)/shard_map/ppermute | solution.py:447
  27.6 4.8 %collective-permute-start.2 = (f32[64]{0:T(128)S(1)}, f32[64]{0:T(128)S(1)}, u32[]{:S(2)}, u32[]{:S(2)}) collective-permute-start(f32[64]{0:T(128)S(1)} %copy-done.6), channel_id=1, source_target_pairs={{0,1},{1,0},{2,3},{3,2},{4,5},{5,4},{6,7},{7,6},{8,9},{9,8},{10,11... | collective-permute-start | bytes 776 | tf_op jit(solution)/shard_map/ppermute | solution.py:447
  27.7 1.2 %copy-start.1 = (bf16[512,1024]{1,0:T(8,128)(2,1)S(1)}, bf16[512,1024]{1,0:T(8,128)(2,1)}, u32[]{:S(2)}) copy-start(bf16[512,1024]{1,0:T(8,128)(2,1)} %constant.12.clone.table) | copy-start | bytes 3145732
  28.9 3.5 %copy-start.2 = (bf16[512,1024]{1,0:T(8,128)(2,1)S(1)}, bf16[512,1024]{1,0:T(8,128)(2,1)}, u32[]{:S(2)}) copy-start(bf16[512,1024]{1,0:T(8,128)(2,1)} %constant.12.clone.table) | copy-start | bytes 3145732
  32.5 19.2 %copy-start.5 = (f32[4]{0:T(128)S(1)}, f32[4]{0:T(128)}, u32[]{:S(2)}) copy-start(f32[4]{0:T(128)} %prior.1) | copy-start | bytes 52
  63.3 1.4 %collective-permute-start.4 = (bf16[8,8,1024]{2,1,0:T(8,128)(2,1)S(1)}, bf16[8,8,1024]{2,1,0:T(8,128)(2,1)S(1)}, u32[]{:S(2)}, u32[]{:S(2)}) collective-permute-start(bf16[8,8,1024]{2,1,0:T(8,128)(2,1)S(1)} %all_to_all.16.parts_own), channel_id=1, source_target_pairs={{0,1},{1,0},{2,3},{3,2},{4,5},{5,4},{6,7},{7,6},{8,9},{9,8},{10,11... | collective-permute-start | bytes 393224 | tf_op jit(solution)/shard_map/ppermute | solution.py:447
  63.3 1.4 %collective-permute-start.5 = (f32[8,1680]{1,0:T(8,128)S(1)}, f32[8,1680]{1,0:T(8,128)S(1)}, u32[]{:S(2)}, u32[]{:S(2)}) collective-permute-start(f32[8,1680]{1,0:T(8,128)S(1)} %get-tuple-element.22.flat_own), channel_id=1, source_target_pairs={{0,1},{1,0},{2,3},{3,2},{4,5},{5,4},{6,7},{7,6},{8,9},{9,8},{10,11... | collective-permute-start | bytes 161288 | tf_op jit(solution)/shard_map/ppermute | solution.py:447

commit v3 on v2

--- a/solution.py
+++ b/solution.py
@@ -177,110 +177,78 @@
         out_tile(tile, value.astype(jnp.bfloat16))
 
 
-def pack_kernel(
-    core, prior_far, kernel, probes, out, prior, kernel_here, probes_here, sems, *, packing
-):
+def pack_kernel(index, prior_far, kernel, probes, *refs, order, sens, half, packing):
+    outs = refs[: len(order)]
+    prior, kernel_here, probes_here, sems = refs[len(order) :]
     f32 = jnp.float32
-    width, _, sens, _ = out.shape
-    half, points, _ = probes_here.shape
+    _, points, _ = probes_here.shape
     edge = packing.full * LANES
-    mine = pl.multiple_of(core[0] * half, half)
-    copies = [pltpu.make_async_copy(probes.at[pl.ds(mine, half)], probes_here, sems.at[0])]
-    for row in range(2 * points):
-        at = (row // points, row % points)
+    me = index[0]
+    mine = pl.multiple_of(index[1] * half, half)
+    copies = [
+        pltpu.make_async_copy(probes.at[pl.ds(mine, half)], probes_here, sems.at[0]),
+        pltpu.make_async_copy(prior_far, prior, sems.at[1]),
+    ]
+    for slot, relative in enumerate(order):
+        rows = pl.ds(pl.multiple_of((me ^ relative) * sens, sens), sens)
         copies.append(
-            pltpu.make_async_copy(kernel.at[at], kernel_here.at[at], sems.at[row + 1])
+            pltpu.make_async_copy(
+                kernel.at[:, :, rows, :], kernel_here.at[slot], sems.at[2 + slot]
+            )
         )
-    copies.append(pltpu.make_async_copy(prior_far, prior, sems.at[2 * points + 1]))
     for copy in copies:
         copy.start()
-
-    def out_tile(tile, value):
-        out[:, tile] = value
 
     def padded(value):
         missing = jnp.zeros((value.shape[0], edge + LANES - value.shape[1]), f32)
         return jnp.concatenate([value, missing], axis=1)
 
-    merged = {}
-    copies[-1].wait()
     copies[0].wait()
+    copies[1].wait()
     scaled = probes_here[...].astype(f32)
-    for p in range(points):
-        value = padded(scaled[:, p, :] * prior[p])
-        value = jnp.broadcast_to(value[None], (width, sens, edge + LANES))
-        store_packed(out_tile, packing, 2 * points + p, value, merged)
-    for row in range(2 * points):
-        copies[row + 1].wait()
-        value = padded(kernel_here[row // points, row % points].astype(f32))
-        store_packed(out_tile, packing, row, value.reshape(width, sens, edge + LANES), merged)
-    store_tails(out_tile, merged)
-
-
-def unpack(source, j, row, packing):
+    scaled = [padded(scaled[:, p, :] * prior[p]) for p in range(points)]
+    for slot, out in enumerate(outs):
+        copies[2 + slot].wait()
+
+        def out_tile(tile, value, out=out):
+            out[tile] = value
+
+        merged = {}
+        for row in range(2 * points):
+            value = padded(kernel_here[slot, row // points, row % points].astype(f32))
+            store_packed(out_tile, packing, row, value, merged)
+        for p in range(points):
+            store_packed(out_tile, packing, 2 * points + p, scaled[p], merged)
+        store_tails(out_tile, merged)
+
+
+def unpack(source, row, packing):
     f32 = jnp.float32
-    tiles = [source[j, row * packing.full + t].astype(f32) for t in range(packing.full)]
+    tiles = [source[row * packing.full + t].astype(f32) for t in range(packing.full)]
     tile, lane = packing.place(row)
-    tiles.append(turned(source[j, tile].astype(f32), -lane))
+    tiles.append(turned(source[tile].astype(f32), -lane))
     return tiles
 
 
-def widen(source, kern, *, packing, width, points):
-    def step(j, carry):
+def widen(sources, kern, *, packing, points, sens):
+    for b, pair in enumerate(sources):
+        for half, source in enumerate(pair):
+            at = slice(half * sens, (half + 1) * sens)
+            for p in range(points):
+                real = unpack(source, p, packing)
+                imag = unpack(source, points + p, packing)
+                for t, (x, y) in enumerate(zip(real, imag)):
+                    lanes = slice(t * LANES, (t + 1) * LANES)
+                    kern[0, b * points + p, at, lanes] = x
+                    kern[1, b * points + p, at, lanes] = x + y
+                    kern[2, b * points + p, at, lanes] = x - y
+
+
+def spectra(sources, table, spec, rows, *, packing, points, half, wide):
+    for b, (own, _) in enumerate(sources):
         for p in range(points):
-            real = unpack(source, j, p, packing)
-            imag = unpack(source, j, points + p, packing)
-            for t, (a, b) in enumerate(zip(real, imag)):
-                lanes = slice(t * LANES, (t + 1) * LANES)
-                kern[0, j * points + p, :, lanes] = a
-                kern[1, j * points + p, :, lanes] = a + b
-                kern[2, j * points + p, :, lanes] = a - b
-        return carry
-
-    lax.fori_loop(0, width, step, 0)
-
-
-def forward_sum(kern, spec, weights, data, base, *, width, points, sens, probes_half, wide):
-    f32 = jnp.float32
-
-    def tile_step(ft, carry):
-        lanes = pl.ds(pl.multiple_of(ft * LANES, LANES), LANES)
-        shifted = pl.ds(pl.multiple_of(wide + ft * LANES, LANES), LANES)
-
-        def source(j, acc):
-            acc = list(acc)
-            for p in range(points):
-                q = j * points + p
-                at = pl.ds(pl.multiple_of(q * probes_half, ROWS), probes_half)
-                both = spec[0, at, lanes]
-                imag = spec[1, at, lanes]
-                real = spec[2, at, lanes]
-                for s in range(sens):
-                    row = slice(s, s + 1)
-                    acc[3 * s] += kern[0, q, row, lanes] * both
-                    acc[3 * s + 1] += kern[1, q, row, lanes] * imag
-                    acc[3 * s + 2] += kern[2, q, row, lanes] * real
-            return tuple(acc)
-
-        zero = jnp.zeros((probes_half, LANES), f32)
-        acc = lax.fori_loop(0, width, source, (zero,) * (3 * sens))
-        factor = weights[:, lanes]
-        for s in range(sens):
-            at = slice(base + s * probes_half, base + (s + 1) * probes_half)
-            data[at, lanes] = (acc[3 * s] - acc[3 * s + 1]) * factor
-            data[at, shifted] = (acc[3 * s] - acc[3 * s + 2]) * factor
-        return carry
-
-    lax.fori_loop(0, wide // LANES, tile_step, 0)
-
-
-def own_kernel(own, table, weights, spec, kern, data, rows, *, sizes, packing):
-    width, points, half = sizes["width"], sizes["points"], sizes["probes_half"]
-    wide = sizes["wide"]
-    for j in range(width):
-        for p in range(points):
-            at = slice((j * points + p) * half, (j * points + p + 1) * half)
-            for t, tile in enumerate(unpack(own, j, 2 * points + p, packing)):
+            at = slice((b * points + p) * half, (b * points + p + 1) * half)
+            for t, tile in enumerate(unpack(own, 2 * points + p, packing)):
                 rows[at, t * LANES : (t + 1) * LANES] = tile
     got = jnp.dot(rows[...].astype(jnp.bfloat16), table[...], preferred_element_type=jnp.float32)
     real = got[:, :wide]
@@ -288,83 +256,133 @@
     spec[0] = real + imag
     spec[1] = imag
     spec[2] = real
-    widen(own, kern, packing=packing, width=width, points=points)
-    forward_sum(kern, spec, weights, data, 0, **sizes)
+
+
+def forward_sum(kern, spec, data, earlier, *, points, sens, half, wide):
+    f32 = jnp.float32
+    blocks = kern.shape[1] // points
+
+    def tile_step(ft, carry):
+        lanes = pl.ds(pl.multiple_of(ft * LANES, LANES), LANES)
+        shifted = pl.ds(pl.multiple_of(wide + ft * LANES, LANES), LANES)
+        for first in range(0, 2 * sens, sens):
+
+            def source(b, acc, first=first):
+                acc = list(acc)
+                for p in range(points):
+                    q = b * points + p
+                    at = pl.ds(pl.multiple_of(q * half, ROWS), half)
+                    both = spec[0, at, lanes]
+                    imag = spec[1, at, lanes]
+                    real = spec[2, at, lanes]
+                    for s in range(sens):
+                        row = slice(first + s, first + s + 1)
+                        acc[3 * s] += kern[0, q, row, lanes] * both
+                        acc[3 * s + 1] += kern[1, q, row, lanes] * imag
+                        acc[3 * s + 2] += kern[2, q, row, lanes] * real
+                return tuple(acc)
+
+            zero = jnp.zeros((half, LANES), f32)
+            acc = lax.fori_loop(0, blocks, source, (zero,) * (3 * sens))
+            for s in range(sens):
+                at = slice((first + s) * half, (first + s + 1) * half)
+                real = acc[3 * s] - acc[3 * s + 1]
+                imag = acc[3 * s] - acc[3 * s + 2]
+                if earlier is not None:
+                    real += earlier[at, lanes]
+                    imag += earlier[at, shifted]
+                data[at, lanes] = real
+                data[at, shifted] = imag
+        return carry
+
+    lax.fori_loop(0, wide // LANES, tile_step, 0)
+
+
+def paired(refs, count):
+    return list(zip(refs[:count], refs[count : 2 * count]))
+
+
+def first_kernel(table, *refs, count, points, sens, half, wide, packing):
+    sources = paired(refs, count)
+    kern, data, spec, rows = refs[2 * count :]
+    spectra(sources, table, spec, rows, packing=packing, points=points, half=half, wide=wide)
+    widen(sources, kern, packing=packing, points=points, sens=sens)
+    forward_sum(kern, spec, data, None, points=points, sens=sens, half=half, wide=wide)
 
 
 def bins_kernel(
-    index, noise_own, noise_other, other, spec, kern_own, data_own, table, weights, out,
-    kern, data, wdata, adjoint,
-    *, sizes, packing, packing_back,
+    index, noise_own, noise_other, table, weights, kern_first, data_first, *refs,
+    orders, points, sens, half, wide, packing, packing_back,
 ):
-    width, points, sens = sizes["width"], sizes["points"], sizes["sens"]
-    probes_half, wide = sizes["probes_half"], sizes["wide"]
+    count = len(orders[1])
+    sources = paired(refs, count)
+    out, kern, spec, rows, data, wdata, adjoint = refs[2 * count :]
     tiles = wide // LANES
     f32 = jnp.float32
-    half_rows = sens * probes_half
-    widen(other, kern, packing=packing, width=width, points=points)
-    forward_sum(kern, spec, weights, data, half_rows, **sizes)
-    data[:half_rows] = data_own[...]
+    bf16 = jnp.bfloat16
+    spectra(sources, table, spec, rows, packing=packing, points=points, half=half, wide=wide)
+    widen(sources, kern, packing=packing, points=points, sens=sens)
+    forward_sum(kern, spec, data, data_first, points=points, sens=sens, half=half, wide=wide)
     table_v = table[...]
-    observed = lax.dot_general(
-        data[...].astype(jnp.bfloat16), table_v, NT, preferred_element_type=f32
-    )
-    first = index[0] * sens
-    scales = [noise_own[first + s] for s in range(sens)]
-    scales += [noise_other[first + s] for s in range(sens)]
+    weight_rows = weights[...]
+    scaled = jnp.concatenate(
+        [data[:, :wide] * weight_rows, data[:, wide:] * weight_rows], axis=1
+    ).astype(bf16)
+    observed = lax.dot_general(scaled, table_v, NT, preferred_element_type=f32)
+    mine = index[0] * sens
+    scales = [noise_own[mine + s] for s in range(sens)]
+    scales += [noise_other[mine + s] for s in range(sens)]
     residual = jnp.concatenate(
-        [
-            (observed[s * probes_half : (s + 1) * probes_half] * scale)
-            for s, scale in enumerate(scales)
-        ],
-        axis=0,
-    ).astype(jnp.bfloat16)
+        [observed[s * half : (s + 1) * half] * scale for s, scale in enumerate(scales)], axis=0
+    ).astype(bf16)
     weighted = jnp.dot(residual, table_v, preferred_element_type=f32)
-    weight_rows = weights[...]
     real = weighted[:, :wide] * weight_rows
     imag = weighted[:, wide:] * weight_rows
     wdata[0] = real + imag
     wdata[1] = imag
     wdata[2] = real
 
-    def adjoint_tile(step, carry):
-        j = step // tiles
-        ft = step % tiles
-        lanes = pl.ds(pl.multiple_of(ft * LANES, LANES), LANES)
-        shifted = pl.ds(pl.multiple_of(wide + ft * LANES, LANES), LANES)
-        zero = jnp.zeros((probes_half, LANES), f32)
-        acc = [zero] * (3 * points)
-        for half, source in ((0, kern_own), (1, kern)):
-            for s in range(sens):
-                at = slice(half * half_rows + s * probes_half, half * half_rows + (s + 1) * probes_half)
+    base = 0
+    for source, order in ((kern_first, orders[0]), (kern, orders[1])):
+
+        def adjoint_tile(step, carry, source=source, base=base):
+            b = step // tiles
+            ft = step % tiles
+            lanes = pl.ds(pl.multiple_of(ft * LANES, LANES), LANES)
+            shifted = pl.ds(pl.multiple_of(wide + ft * LANES, LANES), LANES)
+            zero = jnp.zeros((half, LANES), f32)
+            acc = [zero] * (3 * points)
+            for s in range(2 * sens):
+                at = slice(s * half, (s + 1) * half)
                 both = wdata[0, at, lanes]
                 imag = wdata[1, at, lanes]
                 real = wdata[2, at, lanes]
                 row = slice(s, s + 1)
                 for p in range(points):
-                    q = j * points + p
+                    q = b * points + p
                     acc[3 * p] += source[0, q, row, lanes] * both
                     acc[3 * p + 1] += source[2, q, row, lanes] * imag
                     acc[3 * p + 2] += source[1, q, row, lanes] * real
+            for p in range(points):
+                at = pl.ds(pl.multiple_of((base + b * points + p) * half, ROWS), half)
+                adjoint[at, lanes] = acc[3 * p] - acc[3 * p + 1]
+                adjoint[at, shifted] = acc[3 * p] - acc[3 * p + 2]
+            return carry
+
+        lax.fori_loop(0, len(order) * tiles, adjoint_tile, 0)
+        base += len(order) * points
+    back = lax.dot_general(adjoint[...].astype(bf16), table_v, NT, preferred_element_type=f32)
+    for b, relative in enumerate(orders[0] + orders[1]):
+        there = index[0] ^ relative
+
+        def out_tile(tile, value, there=there):
+            out[there, tile] = value
+
+        merged = {}
         for p in range(points):
-            at = pl.ds(pl.multiple_of((j * points + p) * probes_half, ROWS), probes_half)
-            adjoint[at, lanes] = acc[3 * p] - acc[3 * p + 1]
-            adjoint[at, shifted] = acc[3 * p] - acc[3 * p + 2]
-        return carry
-
-    lax.fori_loop(0, width * tiles, adjoint_tile, 0)
-    back = lax.dot_general(
-        adjoint[...].astype(jnp.bfloat16), table_v, NT, preferred_element_type=f32
-    )
-    back = back.reshape(width, points, probes_half, wide)
-
-    def out_tile(tile, value):
-        out[:, tile] = value
-
-    merged = {}
-    for p in range(points):
-        store_packed(out_tile, packing_back, p, back[:, p], merged)
-    store_tails(out_tile, merged)
+            at = slice((b * points + p) * half, (b * points + p + 1) * half)
+            store_packed(out_tile, packing_back, p, back[at], merged)
+        store_tails(out_tile, merged)
 
 
 def summed(parts):
@@ -413,6 +431,18 @@
         out[pl.ds(half - mine, half), p, :] = piece[half:]
 
 
+def split_order(width):
+    far = list(range(width // 2, width))
+    near = list(range(width // 4, width // 2)) + list(range(1, width // 4))
+    return [0] + far, near
+
+
+def stage_kernel(far, near, sem):
+    copy = pltpu.make_async_copy(far, near, sem)
+    copy.start()
+    copy.wait()
+
+
 def kept(space, *values):
     return [pltpu.with_memory_space_constraint(value, space) for value in values]
 
@@ -450,62 +480,90 @@
         return lax.all_to_all(value, "pts", split_axis=0, concat_axis=0, tiled=False)
 
     table, weights = packed_tables(steps, wide)
-    sizes = dict(width=width, points=points, sens=sens, probes_half=half, wide=wide)
-    all_rows = width * points * half
-
     packing = Packing(3 * points, bins_count)
     packing_back = Packing(points, steps)
+    sizes = dict(points=points, sens=sens, half=half, wide=wide, packing=packing)
+    orders = split_order(width)
+    order = orders[0] + orders[1]
+    places = jnp.stack([me[0], core[0]])
+    chunk = jax.ShapeDtypeStruct((packing.tiles, sens, LANES), bf16)
     in_hbm = pl.BlockSpec(memory_space=pltpu.HBM)
-    send = pl.pallas_call(
-        functools.partial(pack_kernel, packing=packing),
-        out_shape=pltpu.VMEM((width, packing.tiles, sens, LANES), bf16),
+    sent = pl.pallas_call(
+        functools.partial(pack_kernel, order=order, sens=sens, half=half, packing=packing),
+        out_shape=(chunk,) * width,
         in_specs=in_smem(1) + [in_hbm] * 3,
-        out_specs=in_vmem(1)[0],
+        out_specs=tuple(in_vmem(width)),
         scratch_shapes=[
             pltpu.SMEM(prior_scale.shape, f32),
-            pltpu.VMEM(kernel.shape, bf16),
+            pltpu.VMEM((width, 2, points, sens, bins_count), bf16),
             pltpu.VMEM((half, points, steps), bf16),
-            pltpu.SemaphoreType.DMA((2 * points + 2,)),
+            pltpu.SemaphoreType.DMA((2 + width,)),
         ],
         compiler_params=limit(8),
         name="pack",
-    )(core, *kept(pltpu.HBM, prior_scale, kernel, probes))
-    own = exchange(send)
+    )(places, *kept(pltpu.HBM, prior_scale, kernel, probes))
+    blocks = {}
+    others = {}
+    for relative, value in zip(order, sent):
+        if relative:
+            value = lax.ppermute(value, "pts", [(i, i ^ relative) for i in range(width)])
+        blocks[relative] = value
+        others[relative] = swap(value)
     noise_other = swap(noise_weight)
     deflation_other = swap(deflation)
     basis_other = swap(basis)
-    basis, basis_other = kept(pltpu.VMEM, basis, basis_other)
-    other = swap(own)
-    other, basis_other, noise_other, deflation_other = lax.optimization_barrier(
-        (other, basis_other, noise_other, deflation_other)
-    )
-    spec, kern_own, data_own = pl.pallas_call(
-        functools.partial(own_kernel, sizes=sizes, packing=packing),
+
+    def scratch(count):
+        return [
+            pltpu.VMEM((3, count * points * half, wide), f32),
+            pltpu.VMEM((count * points * half, wide), f32),
+        ]
+
+    def ready(part):
+        return [blocks[r] for r in part] + [others[r] for r in part]
+
+    table = pl.pallas_call(
+        stage_kernel,
+        out_shape=pltpu.VMEM(table.shape, bf16),
+        in_specs=[in_hbm],
+        out_specs=in_vmem(1)[0],
+        scratch_shapes=[pltpu.SemaphoreType.DMA],
+        compiler_params=limit(2),
+        name="stage",
+    )(*kept(pltpu.HBM, table))
+    count = len(orders[0])
+    kern_first, data_first = pl.pallas_call(
+        functools.partial(first_kernel, count=count, **sizes),
         out_shape=(
-            jax.ShapeDtypeStruct((3, all_rows, wide), f32),
-            jax.ShapeDtypeStruct((3, width * points, sens, wide), f32),
-            jax.ShapeDtypeStruct((sens * half, 2 * wide), f32),
+            jax.ShapeDtypeStruct((3, count * points, 2 * sens, wide), f32),
+            jax.ShapeDtypeStruct((2 * sens * half, 2 * wide), f32),
         ),
-        in_specs=in_vmem(3),
-        out_specs=tuple(in_vmem(3)),
-        scratch_shapes=[pltpu.VMEM((all_rows, wide), f32)],
-        compiler_params=limit(10),
-        name="own",
-    )(own, table, weights)
+        in_specs=in_vmem(1 + 2 * count),
+        out_specs=tuple(in_vmem(2)),
+        scratch_shapes=scratch(count),
+        compiler_params=limit(12),
+        name="first",
+    )(table, *ready(orders[0]))
+    count = len(orders[1])
     back = pl.pallas_call(
-        functools.partial(bins_kernel, sizes=sizes, packing=packing, packing_back=packing_back),
-        out_shape=pltpu.VMEM((width, packing_back.tiles, half, LANES), bf16),
-        in_specs=in_smem(3) + in_vmem(6),
+        functools.partial(bins_kernel, orders=orders, packing_back=packing_back, **sizes),
+        out_shape=jax.ShapeDtypeStruct((width, packing_back.tiles, half, LANES), bf16),
+        in_specs=in_smem(3) + in_vmem(4 + 2 * count),
         out_specs=in_vmem(1)[0],
-        scratch_shapes=[
-            pltpu.VMEM((3, width * points, sens, wide), f32),
+        scratch_shapes=[pltpu.VMEM((3, count * points, 2 * sens, wide), f32)]
+        + scratch(count)
+        + [
             pltpu.VMEM((2 * sens * half, 2 * wide), f32),
             pltpu.VMEM((3, 2 * sens * half, wide), f32),
-            pltpu.VMEM((all_rows, 2 * wide), f32),
+            pltpu.VMEM((width * points * half, 2 * wide), f32),
         ],
         compiler_params=limit(20),
         name="bins",
-    )(me, noise_weight, noise_other, other, spec, kern_own, data_own, table, weights)
+    )(me, noise_weight, noise_other, table, weights, kern_first, data_first, *ready(orders[1]))
+    back, basis_other, deflation_other = lax.optimization_barrier(
+        (back, basis_other, deflation_other)
+    )
+    basis, basis_other = kept(pltpu.VMEM, basis, basis_other)
     parts = exchange(back)
     flat, coeff = pl.pallas_call(
         functools.partial(coeff_kernel, points=points, steps=steps, rank=rank, packing=packing_back),
@@ -546,7 +604,7 @@
 
     def body(*args):
         width = mesh.shape["pts"]
-        split = mesh.shape["sen"] == 2 and width > 1
+        split = mesh.shape["sen"] == 2 and width == ROWS
         whole_tiles = args[2].shape[0] == width * ROWS and args[0].shape[0] == 2 * ROWS
         if not (split and whole_tiles):
             return local(*args)

time: 66.9 us -> 66.4 us (level)
  starting transfers between devices: 8.47 us -> 16 us
  waiting for transfers between devices: 18.2 us -> 11.1 us
  blocking collectives: 23 us -> 25 us
  Pallas kernels: 15.5 us -> 13.8 us
  local copies, waits for them, and re-layouts: 1.25 us -> 0.02 us
    all_to_all x1 -> x0, waiting for transfers between devices: 17.3 us -> none  [exchange(): lax.all_to_all(value, 'pts', split_axis=0, concat_axis=0, tiled=False)]
    ppermute x0 -> x7, starting transfers between devices: none -> 13.1 us  [local_split(): lax.ppermute(value, 'pts', [(i, i ^ relative) for i in range(width)])]
    ppermute x0 -> x7, waiting for transfers between devices: none -> 8.63 us  [local_split(): lax.ppermute(value, 'pts', [(i, i ^ relative) for i in range(width)])]
    all_to_all x1 -> x0, starting transfers between devices: 7.31 us -> none  [exchange(): lax.all_to_all(value, 'pts', split_axis=0, concat_axis=0, tiled=False)]
    all_to_all x2, blocking collectives: 23 us -> 25 us  [exchange(): lax.all_to_all(value, 'pts', split_axis=0, concat_axis=0, tiled=False)]
    pallas_call x3 -> x4, Pallas kernels: 12.6 us -> 10.9 us  [the longest x1 5.65 us: local_split(): pl.pallas_call(functools.partial(bins_kernel, orders=orders, packing_back...]
    ppermute x6 -> x13, starting transfers between devices: 1.16 us -> 2.86 us  [swap(): return lax.ppermute(value, 'sen', [(0, 1), (1, 0)])]
    ppermute x6 -> x13, waiting for transfers between devices: 0.93 us -> 2.48 us  [swap(): return lax.ppermute(value, 'sen', [(0, 1), (1, 0)])]
  transfers between devices with their start and end apart: 7 -> 20, of which waited for: 2 -> 6; matrix products, arithmetic and copies ran while one was open for 0% -> 0% of each run, Pallas kernels for 5% -> 16%
where the time goes in v3:
time: 66.4 us; the launch traced here: 66.1 us
  blocking collectives  25 us (38%)
  starting transfers between devices  16 us (24%)
  Pallas kernels  13.8 us (21%)
  waiting for transfers between devices  11.1 us (17%)
    all_to_all x2, blocking collectives, exchange(): lax.all_to_all(value, 'pts', split_axis=0, concat_axis=0, tiled=False)  25 us
    ppermute x7, starting transfers between devices, local_split(): lax.ppermute(value, 'pts', [(i, i ^ relative) for i in range(width)])  13.1 us
    ppermute x7, waiting for transfers between devices, local_split(): lax.ppermute(value, 'pts', [(i, i ^ relative) for i in range(width)])  8.63 us
    pallas_call x1, Pallas kernels, local_split(): pl.pallas_call(functools.partial(bins_kernel, orders=orders, packing_back...  5.65 us
    ppermute x13, starting transfers between devices, swap(): return lax.ppermute(value, 'sen', [(0, 1), (1, 0)])  2.86 us
    ppermute x13, waiting for transfers between devices, swap(): return lax.ppermute(value, 'sen', [(0, 1), (1, 0)])  2.48 us
    pallas_call x1, Pallas kernels, local_split(): pl.pallas_call(functools.partial(pack_kernel, order=order, sens=sens, hal...  2.15 us
    pallas_call x1, Pallas kernels, local_split(): pl.pallas_call(functools.partial(first_kernel, count=count, **sizes), out...  1.85 us
  transfers between devices with their start and end apart: 20, of which 6 were waited for; matrix products, arithmetic and copies ran while one was open for 0% of the time, Pallas kernels for 16%

profile of v3, /device:TPU:0, one launch (start us, length us, event | category | flops | bytes accessed | tf_op | source)
XLA Modules:
  0.0 66.1 jit_solution(3041992060920737676)
XLA Ops:
  0.0 0.5 collective-permute-start.16
  0.5 0.1 pad_add_fusion.index
  0.6 2.1 %pack.1 = (bf16[40,8,128]{2,1,0:T(8,128)(2,1)S(1)}, bf16[40,8,128]{2,1,0:T(8,128)(2,1)S(1)}, bf16[40,8,128]{2,1,0:T(8,128)(2,1)S(1)}, bf16[40,8,128]{2,1,0:T(8,1...) custom-call(s32[2]{0:T(128)S(1)} %pad_add_fusion.index, ...), custom_call_target="tpu_custom_call" | custom-call | tf_op jit(solution)/shard_map/pack/pallas_call | solution.py:491
  2.7 3.6 %collective-permute-start.1 = (bf16[40,8,128]{2,1,0:T(8,128)(2,1)S(1)}, bf16[40,8,128]{2,1,0:T(8,128)(2,1)S(1)}, u32[]{:S(2)}, u32[]{:S(2)}) collective-permute-start(bf16[40,8,128]{2,1,0:T(8,128)(2,1)S(1)} %get-tuple-element.21), channel_id=1, source_target_pairs={{0,8},{2,10},{4,12},{6,14},{8,0},{10,2},{12,4},{14,6},{1,9},{3,11}... | collective-permute-start | bytes 245768 | tf_op jit(solution)/shard_map/ppermute | solution.py:509
  6.4 1.3 %collective-permute-start.2 = (bf16[40,8,128]{2,1,0:T(8,128)(2,1)S(1)}, bf16[40,8,128]{2,1,0:T(8,128)(2,1)S(1)}, u32[]{:S(2)}, u32[]{:S(2)}) collective-permute-start(bf16[40,8,128]{2,1,0:T(8,128)(2,1)S(1)} %get-tuple-element.22), channel_id=1, source_target_pairs={{0,10},{2,8},{4,14},{6,12},{8,2},{10,0},{12,6},{14,4},{1,11},{3,9}... | collective-permute-start | bytes 245768 | tf_op jit(solution)/shard_map/ppermute | solution.py:509
  7.6 3.6 %collective-permute-start.3 = (bf16[40,8,128]{2,1,0:T(8,128)(2,1)S(1)}, bf16[40,8,128]{2,1,0:T(8,128)(2,1)S(1)}, u32[]{:S(2)}, u32[]{:S(2)}) collective-permute-start(bf16[40,8,128]{2,1,0:T(8,128)(2,1)S(1)} %get-tuple-element.23), channel_id=1, source_target_pairs={{0,12},{2,14},{4,8},{6,10},{8,4},{10,6},{12,0},{14,2},{1,13},{3,15... | collective-permute-start | bytes 245768 | tf_op jit(solution)/shard_map/ppermute | solution.py:509
  11.2 0.0 collective-permute-start
  11.2 1.3 %collective-permute-done.noise_other = f32[64]{0:T(128)S(1)} collective-permute-done((f32[64]{0:T(128)}, f32[64]{0:T(128)S(1)}, u32[]{:S(2)}, u32[]{:S(2)}) %collective-permute-start) | collective-permute-done | bytes 288 | tf_op jit(solution)/shard_map/ppermute | solution.py:477
  12.5 0.0 collective-permute-start.4
  12.5 0.0 collective-permute-done.1.refs_1_
  12.5 0.2 collective-permute-start.5
  12.7 5.2 %collective-permute-done.2.refs_2_ = bf16[40,8,128]{2,1,0:T(8,128)(2,1)S(1)} collective-permute-done((bf16[40,8,128]{2,1,0:T(8,128)(2,1)S(1)}, bf16[40,8,128]{2,1,0:T(8,128)(2,1)S(1)}, u32[]{:S(2)}, u32[]{:S(2)}) %collective-permute-start.2) | collective-permute-done | bytes 81952 | tf_op jit(solution)/shard_map/ppermute | solution.py:509
  17.9 1.1 %collective-permute-start.10 = (bf16[40,8,128]{2,1,0:T(8,128)(2,1)S(1)}, bf16[40,8,128]{2,1,0:T(8,128)(2,1)S(1)}, u32[]{:S(2)}, u32[]{:S(2)}) collective-permute-start(bf16[40,8,128]{2,1,0:T(8,128)(2,1)S(1)} %get-tuple-element.27), channel_id=1, source_target_pairs={{0,4},{2,6},{4,0},{6,2},{8,12},{10,14},{12,8},{14,10},{1,5},{3,7},... | collective-permute-start | bytes 245768 | tf_op jit(solution)/shard_map/ppermute | solution.py:509
  19.0 0.0 collective-permute-done.3.refs_3_
  19.0 3.0 %collective-permute-start.11 = (bf16[40,8,128]{2,1,0:T(8,128)(2,1)S(1)}, bf16[40,8,128]{2,1,0:T(8,128)(2,1)S(1)}, u32[]{:S(2)}, u32[]{:S(2)}) collective-permute-start(bf16[40,8,128]{2,1,0:T(8,128)(2,1)S(1)} %get-tuple-element.28), channel_id=1, source_target_pairs={{0,6},{2,4},{4,2},{6,0},{8,14},{10,12},{12,10},{14,8},{1,7},{3,5},... | collective-permute-start | bytes 245768 | tf_op jit(solution)/shard_map/ppermute | solution.py:509
  22.0 0.0 collective-permute-done.4.refs_4_
  22.0 0.0 copy-start.2
  22.0 0.0 copy-start.4
  22.0 0.5 collective-permute-start.12
  22.6 0.0 collective-permute-done.5.refs_5_
  22.6 0.0 collective-permute-start.6
  22.6 0.0 collective-permute-done.10.refs_0_
  22.6 0.5 collective-permute-start.7
  23.1 1.4 %collective-permute-done.11.refs_1_ = bf16[40,8,128]{2,1,0:T(8,128)(2,1)S(1)} collective-permute-done((bf16[40,8,128]{2,1,0:T(8,128)(2,1)S(1)}, bf16[40,8,128]{2,1,0:T(8,128)(2,1)S(1)}, u32[]{:S(2)}, u32[]{:S(2)}) %collective-permute-start.11) | collective-permute-done | bytes 81952 | tf_op jit(solution)/shard_map/ppermute | solution.py:509
  24.5 0.0 collective-permute-start.8
  24.5 2.0 %collective-permute-done.12.refs_2_ = bf16[40,8,128]{2,1,0:T(8,128)(2,1)S(1)} collective-permute-done((bf16[40,8,128]{2,1,0:T(8,128)(2,1)S(1)}, bf16[40,8,128]{2,1,0:T(8,128)(2,1)S(1)}, u32[]{:S(2)}, u32[]{:S(2)}) %collective-permute-start.12) | collective-permute-done | bytes 81952 | tf_op jit(solution)/shard_map/ppermute | solution.py:509
  26.5 0.0 collective-permute-start.9
  26.5 0.0 collective-permute-done.6.refs_6_
  26.5 0.5 collective-permute-start.13
  27.0 0.0 collective-permute-done.7.refs_7_
  27.0 0.1 collective-permute-start.14
  27.1 0.0 collective-permute-done.8.refs_8_
  27.1 0.4 collective-permute-start.15
  27.5 0.2 collective-permute-done.9.refs_9_
  27.7 0.2 collective-permute-start.17
  27.9 1.2 %stage.1.table = bf16[512,1024]{1,0:T(8,128)(2,1)S(1)} custom-call(bf16[512,1024]{1,0:T(8,128)(2,1)} %constant.12.clone.far), custom_call_target="tpu_custom_call" | custom-call | tf_op jit(solution)/shard_map/stage/pallas_call | solution.py:525
  29.1 1.8 %first.1 = (f32[3,20,16,512]{3,2,1,0:T(8,128)S(1)}, f32[128,1024]{1,0:T(8,128)S(1)}) custom-call(bf16[512,1024]{1,0:T(8,128)(2,1)S(1)} %stage.1.table, bf16[40,8,128]{2,1,0:T(8,128)(2,1)S(1)} %get-tuple-element.20.refs_0_, bf16[40,8,128]{2,1,0:T(8,128)(2,1)S(1)} %collective-permute-done.1.refs_1_, bf16[40,8,128]{2,1,0:T(8,128)(2,1)S(1)} %collective-permute-done.2.refs_2_, ...), custom_call_target="tpu_custom_call" | custom-call | tf_op jit(solution)/shard_map/first/pallas_call | solution.py:535
  31.0 0.0 collective-permute-done.13.refs_3_
  31.0 0.0 collective-permute-done.14.refs_4_
  31.0 0.0 collective-permute-done.15.refs_5_
  31.0 0.0 copy-done.2
  31.0 0.0 copy-done.4
  31.0 0.0 copy-start
  31.1 0.0 copy-start.3
  31.1 5.6 %bins.1 = bf16[8,14,8,128]{3,2,1,0:T(8,128)(2,1)S(1)} custom-call(s32[1]{0:T(128)} %bitcast.1.index, f32[64]{0:T(128)S(1)} %copy-done.4, f32[64]{0:T(128)S(1)} %collective-permute-done.noise_other, bf16[512,1024]{1,0:T(8,128)(2,1)S(1)} %stage.1.table, f32[1,512]{1,0:T(1,128)S(1)} %copy-done.2, f32[3,20,16,512]{3,2,1,0:T(8,128)S(1)} %get-tuple-element.25.kern_first, ...), custom_call_target="tpu_custom_call" | custom-call | tf_op jit(solution)/shard_map/bins/pallas_call | solution.py:548
  36.7 0.0 collective-permute-done.17
  36.7 0.0 collective-permute-done.16.basis_other
  36.7 14.5 %all_to_all.10.parts = bf16[8,14,8,128]{3,2,1,0:T(8,128)(2,1)S(1)} all-to-all(bf16[8,14,8,128]{3,2,1,0:T(8,128)(2,1)S(1)} %bins.1), channel_id=1, replica_groups=mesh['grp'=2,'pts'=8,'sen'=2] {'pts'}, dimensions={0} | all-to-all | bytes 458752 | tf_op jit(solution)/shard_map/all_to_all | solution.py:480
  51.3 0.0 copy-done
  51.3 0.0 copy-done.3
  51.3 0.0 copy-start.1
  51.3 1.1 %coeff.1 = (f32[8,1680]{1,0:T(8,128)S(1)}, bf16[8,8,1024]{2,1,0:T(8,128)(2,1)S(1)}) custom-call(f32[4]{0:T(128)S(1)} %copy-done.3, bf16[8,14,8,128]{3,2,1,0:T(8,128)(2,1)S(1)} %all_to_all.10.parts, bf16[1680,512]{1,0:T(8,128)(2,1)S(1)} %copy-done, bf16[1680,512]{1,0:T(8,128)(2,1)S(1)} %collective-permute-done.16.basis_other), custom_call_target="tpu_custom_call" | custom-call | tf_op jit(solution)/shard_map/coeff/pallas_call | solution.py:568
  52.4 10.5 %all_to_all.11.parts_own = bf16[8,8,1024]{2,1,0:T(8,128)(2,1)S(1)} all-to-all(bf16[8,8,1024]{2,1,0:T(8,128)(2,1)S(1)} %get-tuple-element.32), channel_id=1, replica_groups=mesh['grp'=2,'pts'=8,'sen'=2] {'pts'}, dimensions={0} | all-to-all | bytes 262144 | tf_op jit(solution)/shard_map/all_to_all | solution.py:480
  62.9 0.0 collective-permute-start.18
  62.9 0.5 collective-permute-start.19
  63.4 0.9 %collective-permute-done.19.flat_other = f32[8,1680]{1,0:T(8,128)S(1)} collective-permute-done((f32[8,1680]{1,0:T(8,128)S(1)}, f32[8,1680]{1,0:T(8,128)S(1)}, u32[]{:S(2)}, u32[]{:S(2)}) %collective-permute-start.19) | collective-permute-done | bytes 53792 | tf_op jit(solution)/shard_map/ppermute | solution.py:477
  64.3 0.0 collective-permute-done.18.parts_other
  64.3 0.0 copy-done.1
  64.3 1.8 %deflate.1 = f32[16,4,420]{2,1,0:T(4,128)} custom-call(s32[1]{0:T(128)} %bitcast.core, bf16[8,8,1024]{2,1,0:T(8,128)(2,1)S(1)} %all_to_all.11.parts_own, bf16[8,8,1024]{2,1,0:T(8,128)(2,1)S(1)} %collective-permute-done.18.parts_other, f32[1,512]{1,0:T(1,128)S(1)} %bitcast.4, f32[1,512]{1,0:T(1,128)S(1)} %bitcast.5, ...), custom_call_target="tpu_custom_call" | custom-call | tf_op jit(solution)/shard_map/deflate/pallas_call | solution.py:582
Async XLA Ops:
  0.0 36.7 %collective-permute-start.16 = (bf16[1680,512]{1,0:T(8,128)(2,1)}, bf16[1680,512]{1,0:T(8,128)(2,1)S(1)}, u32[]{:S(2)}, u32[]{:S(2)}) collective-permute-start(bf16[1680,512]{1,0:T(8,128)(2,1)} %basis_own.3), channel_id=1, source_target_pairs={{0,1},{1,0},{2,3},{3,2},{4,5},{5,4},{6,7},{7,6},{8,9},{9,8},{10,11... | collective-permute-start | bytes 5160968 | tf_op jit(solution)/shard_map/ppermute | solution.py:477
  2.7 9.8 %collective-permute-start.1 = (bf16[40,8,128]{2,1,0:T(8,128)(2,1)S(1)}, bf16[40,8,128]{2,1,0:T(8,128)(2,1)S(1)}, u32[]{:S(2)}, u32[]{:S(2)}) collective-permute-start(bf16[40,8,128]{2,1,0:T(8,128)(2,1)S(1)} %get-tuple-element.21), channel_id=1, source_target_pairs={{0,8},{2,10},{4,12},{6,14},{8,0},{10,2},{12,4},{14,6},{1,9},{3,11}... | collective-permute-start | bytes 245768 | tf_op jit(solution)/shard_map/ppermute | solution.py:509
  6.4 11.6 %collective-permute-start.2 = (bf16[40,8,128]{2,1,0:T(8,128)(2,1)S(1)}, bf16[40,8,128]{2,1,0:T(8,128)(2,1)S(1)}, u32[]{:S(2)}, u32[]{:S(2)}) collective-permute-start(bf16[40,8,128]{2,1,0:T(8,128)(2,1)S(1)} %get-tuple-element.22), channel_id=1, source_target_pairs={{0,10},{2,8},{4,14},{6,12},{8,2},{10,0},{12,6},{14,4},{1,11},{3,9}... | collective-permute-start | bytes 245768 | tf_op jit(solution)/shard_map/ppermute | solution.py:509
  7.6 11.4 %collective-permute-start.3 = (bf16[40,8,128]{2,1,0:T(8,128)(2,1)S(1)}, bf16[40,8,128]{2,1,0:T(8,128)(2,1)S(1)}, u32[]{:S(2)}, u32[]{:S(2)}) collective-permute-start(bf16[40,8,128]{2,1,0:T(8,128)(2,1)S(1)} %get-tuple-element.23), channel_id=1, source_target_pairs={{0,12},{2,14},{4,8},{6,10},{8,4},{10,6},{12,0},{14,2},{1,13},{3,15... | collective-permute-start | bytes 245768 | tf_op jit(solution)/shard_map/ppermute | solution.py:509
  11.2 1.3 %collective-permute-start = (f32[64]{0:T(128)}, f32[64]{0:T(128)S(1)}, u32[]{:S(2)}, u32[]{:S(2)}) collective-permute-start(f32[64]{0:T(128)} %noise_own.1), channel_id=1, source_target_pairs={{0,1},{1,0},{2,3},{3,2},{4,5},{5,4},{6,7},{7,6},{8,9},{9,8},{10,11... | collective-permute-start | bytes 776 | tf_op jit(solution)/shard_map/ppermute | solution.py:477
  12.5 9.5 %collective-permute-start.4 = (bf16[40,8,128]{2,1,0:T(8,128)(2,1)S(1)}, bf16[40,8,128]{2,1,0:T(8,128)(2,1)S(1)}, u32[]{:S(2)}, u32[]{:S(2)}) collective-permute-start(bf16[40,8,128]{2,1,0:T(8,128)(2,1)S(1)} %get-tuple-element.24), channel_id=1, source_target_pairs={{0,14},{2,12},{4,10},{6,8},{8,6},{10,4},{12,2},{14,0},{1,15},{3,13... | collective-permute-start | bytes 245768 | tf_op jit(solution)/shard_map/ppermute | solution.py:509
  12.5 10.0 %collective-permute-start.5 = (bf16[40,8,128]{2,1,0:T(8,128)(2,1)S(1)}, bf16[40,8,128]{2,1,0:T(8,128)(2,1)S(1)}, u32[]{:S(2)}, u32[]{:S(2)}) collective-permute-start(bf16[40,8,128]{2,1,0:T(8,128)(2,1)S(1)} %get-tuple-element.20.refs_0_), channel_id=1, source_target_pairs={{0,1},{1,0},{2,3},{3,2},{4,5},{5,4},{6,7},{7,6},{8,9},{9,8},{10,11... | collective-permute-start | bytes 245768 | tf_op jit(solution)/shard_map/ppermute | solution.py:477
  17.9 4.6 %collective-permute-start.10 = (bf16[40,8,128]{2,1,0:T(8,128)(2,1)S(1)}, bf16[40,8,128]{2,1,0:T(8,128)(2,1)S(1)}, u32[]{:S(2)}, u32[]{:S(2)}) collective-permute-start(bf16[40,8,128]{2,1,0:T(8,128)(2,1)S(1)} %get-tuple-element.27), channel_id=1, source_target_pairs={{0,4},{2,6},{4,0},{6,2},{8,12},{10,14},{12,8},{14,10},{1,5},{3,7},... | collective-permute-start | bytes 245768 | tf_op jit(solution)/shard_map/ppermute | solution.py:509
  19.0 5.5 %collective-permute-start.11 = (bf16[40,8,128]{2,1,0:T(8,128)(2,1)S(1)}, bf16[40,8,128]{2,1,0:T(8,128)(2,1)S(1)}, u32[]{:S(2)}, u32[]{:S(2)}) collective-permute-start(bf16[40,8,128]{2,1,0:T(8,128)(2,1)S(1)} %get-tuple-element.28), channel_id=1, source_target_pairs={{0,6},{2,4},{4,2},{6,0},{8,14},{10,12},{12,10},{14,8},{1,7},{3,5},... | collective-permute-start | bytes 245768 | tf_op jit(solution)/shard_map/ppermute | solution.py:509
  22.0 9.0 %copy-start.2 = (f32[1,512]{1,0:T(1,128)S(1)}, f32[1,512]{1,0:T(1,128)}, u32[]{:S(2)}) copy-start(f32[1,512]{1,0:T(1,128)} %constant.13.clone.weights) | copy-start | bytes 6148
  22.0 9.0 %copy-start.4 = (f32[64]{0:T(128)S(1)}, f32[64]{0:T(128)}, u32[]{:S(2)}) copy-start(f32[64]{0:T(128)} %noise_own.1) | copy-start | bytes 772
  22.0 4.4 %collective-permute-start.12 = (bf16[40,8,128]{2,1,0:T(8,128)(2,1)S(1)}, bf16[40,8,128]{2,1,0:T(8,128)(2,1)S(1)}, u32[]{:S(2)}, u32[]{:S(2)}) collective-permute-start(bf16[40,8,128]{2,1,0:T(8,128)(2,1)S(1)} %get-tuple-element.29), channel_id=1, source_target_pairs={{0,2},{2,0},{4,6},{6,4},{8,10},{10,8},{12,14},{14,12},{1,3},{3,1},... | collective-permute-start | bytes 245768 | tf_op jit(solution)/shard_map/ppermute | solution.py:509
  22.6 3.9 %collective-permute-start.6 = (bf16[40,8,128]{2,1,0:T(8,128)(2,1)S(1)}, bf16[40,8,128]{2,1,0:T(8,128)(2,1)S(1)}, u32[]{:S(2)}, u32[]{:S(2)}) collective-permute-start(bf16[40,8,128]{2,1,0:T(8,128)(2,1)S(1)} %collective-permute-done.1.refs_1_), channel_id=1, source_target_pairs={{0,1},{1,0},{2,3},{3,2},{4,5},{5,4},{6,7},{7,6},{8,9},{9,8},{10,11... | collective-permute-start | bytes 245768 | tf_op jit(solution)/shard_map/ppermute | solution.py:477
  22.6 4.4 %collective-permute-start.7 = (bf16[40,8,128]{2,1,0:T(8,128)(2,1)S(1)}, bf16[40,8,128]{2,1,0:T(8,128)(2,1)S(1)}, u32[]{:S(2)}, u32[]{:S(2)}) collective-permute-start(bf16[40,8,128]{2,1,0:T(8,128)(2,1)S(1)} %collective-permute-done.2.refs_2_), channel_id=1, source_target_pairs={{0,1},{1,0},{2,3},{3,2},{4,5},{5,4},{6,7},{7,6},{8,9},{9,8},{10,11... | collective-permute-start | bytes 245768 | tf_op jit(solution)/shard_map/ppermute | solution.py:477
  24.5 2.6 %collective-permute-start.8 = (bf16[40,8,128]{2,1,0:T(8,128)(2,1)S(1)}, bf16[40,8,128]{2,1,0:T(8,128)(2,1)S(1)}, u32[]{:S(2)}, u32[]{:S(2)}) collective-permute-start(bf16[40,8,128]{2,1,0:T(8,128)(2,1)S(1)} %collective-permute-done.3.refs_3_), channel_id=1, source_target_pairs={{0,1},{1,0},{2,3},{3,2},{4,5},{5,4},{6,7},{7,6},{8,9},{9,8},{10,11... | collective-permute-start | bytes 245768 | tf_op jit(solution)/shard_map/ppermute | solution.py:477
  26.5 1.3 %collective-permute-start.9 = (bf16[40,8,128]{2,1,0:T(8,128)(2,1)S(1)}, bf16[40,8,128]{2,1,0:T(8,128)(2,1)S(1)}, u32[]{:S(2)}, u32[]{:S(2)}) collective-permute-start(bf16[40,8,128]{2,1,0:T(8,128)(2,1)S(1)} %collective-permute-done.4.refs_4_), channel_id=1, source_target_pairs={{0,1},{1,0},{2,3},{3,2},{4,5},{5,4},{6,7},{7,6},{8,9},{9,8},{10,11... | collective-permute-start | bytes 245768 | tf_op jit(solution)/shard_map/ppermute | solution.py:477
  26.5 4.5 %collective-permute-start.13 = (bf16[40,8,128]{2,1,0:T(8,128)(2,1)S(1)}, bf16[40,8,128]{2,1,0:T(8,128)(2,1)S(1)}, u32[]{:S(2)}, u32[]{:S(2)}) collective-permute-start(bf16[40,8,128]{2,1,0:T(8,128)(2,1)S(1)} %collective-permute-done.10.refs_0_), channel_id=1, source_target_pairs={{0,1},{1,0},{2,3},{3,2},{4,5},{5,4},{6,7},{7,6},{8,9},{9,8},{10,11... | collective-permute-start | bytes 245768 | tf_op jit(solution)/shard_map/ppermute | solution.py:477
  27.0 4.0 %collective-permute-start.14 = (bf16[40,8,128]{2,1,0:T(8,128)(2,1)S(1)}, bf16[40,8,128]{2,1,0:T(8,128)(2,1)S(1)}, u32[]{:S(2)}, u32[]{:S(2)}) collective-permute-start(bf16[40,8,128]{2,1,0:T(8,128)(2,1)S(1)} %collective-permute-done.11.refs_1_), channel_id=1, source_target_pairs={{0,1},{1,0},{2,3},{3,2},{4,5},{5,4},{6,7},{7,6},{8,9},{9,8},{10,11... | collective-permute-start | bytes 245768 | tf_op jit(solution)/shard_map/ppermute | solution.py:477
  27.1 4.0 %collective-permute-start.15 = (bf16[40,8,128]{2,1,0:T(8,128)(2,1)S(1)}, bf16[40,8,128]{2,1,0:T(8,128)(2,1)S(1)}, u32[]{:S(2)}, u32[]{:S(2)}) collective-permute-start(bf16[40,8,128]{2,1,0:T(8,128)(2,1)S(1)} %collective-permute-done.12.refs_2_), channel_id=1, source_target_pairs={{0,1},{1,0},{2,3},{3,2},{4,5},{5,4},{6,7},{7,6},{8,9},{9,8},{10,11... | collective-permute-start | bytes 245768 | tf_op jit(solution)/shard_map/ppermute | solution.py:477
  27.7 9.0 %collective-permute-start.17 = (f32[512]{0:T(512)}, f32[512]{0:T(512)S(1)}, u32[]{:S(2)}, u32[]{:S(2)}) collective-permute-start(f32[512]{0:T(512)} %param.13), channel_id=1, source_target_pairs={{0,1},{1,0},{2,3},{3,2},{4,5},{5,4},{6,7},{7,6},{8,9},{9,8},{10,11... | collective-permute-start | bytes 6152 | tf_op jit(solution)/shard_map/ppermute | solution.py:477
  31.0 20.2 %copy-start = (bf16[1680,512]{1,0:T(8,128)(2,1)S(1)}, bf16[1680,512]{1,0:T(8,128)(2,1)}, u32[]{:S(2)}) copy-start(bf16[1680,512]{1,0:T(8,128)(2,1)} %basis_own.3) | copy-start | bytes 5160964
  31.1 20.2 %copy-start.3 = (f32[4]{0:T(128)S(1)}, f32[4]{0:T(128)}, u32[]{:S(2)}) copy-start(f32[4]{0:T(128)} %prior.1) | copy-start | bytes 52
  51.3 13.1 %copy-start.1 = (f32[512]{0:T(512)S(1)}, f32[512]{0:T(512)}, u32[]{:S(2)}) copy-start(f32[512]{0:T(512)} %param.13) | copy-start | bytes 6148
  62.9 1.4 %collective-permute-start.18 = (bf16[8,8,1024]{2,1,0:T(8,128)(2,1)S(1)}, bf16[8,8,1024]{2,1,0:T(8,128)(2,1)S(1)}, u32[]{:S(2)}, u32[]{:S(2)}) collective-permute-start(bf16[8,8,1024]{2,1,0:T(8,128)(2,1)S(1)} %all_to_all.11.parts_own), channel_id=1, source_target_pairs={{0,1},{1,0},{2,3},{3,2},{4,5},{5,4},{6,7},{7,6},{8,9},{9,8},{10,11... | collective-permute-start | bytes 393224 | tf_op jit(solution)/shard_map/ppermute | solution.py:477
  62.9 1.4 %collective-permute-start.19 = (f32[8,1680]{1,0:T(8,128)S(1)}, f32[8,1680]{1,0:T(8,128)S(1)}, u32[]{:S(2)}, u32[]{:S(2)}) collective-permute-start(f32[8,1680]{1,0:T(8,128)S(1)} %get-tuple-element.34.flat_own), channel_id=1, source_target_pairs={{0,1},{1,0},{2,3},{3,2},{4,5},{5,4},{6,7},{7,6},{8,9},{9,8},{10,11... | collective-permute-start | bytes 161288 | tf_op jit(solution)/shard_map/ppermute | solution.py:477

commit v4 on v3

--- a/solution.py
+++ b/solution.py
@@ -161,15 +161,19 @@
     return pltpu.roll(tile, lanes, axis=tile.ndim - 1) if lanes else tile
 
 
-def store_packed(out_tile, packing, row, value, merged):
-    for t in range(packing.full):
-        lanes = slice(t * LANES, (t + 1) * LANES)
-        out_tile(row * packing.full + t, value[..., lanes].astype(jnp.bfloat16))
+def add_tail(packing, row, value, merged):
     tile, lane = packing.place(row)
     tail = value[..., packing.full * LANES : (packing.full + 1) * LANES]
     where = lax.broadcasted_iota(jnp.int32, tail.shape, tail.ndim - 1)
     tail = turned(jnp.where(where < packing.tail, tail, 0.0), lane)
     merged[tile] = merged[tile] + tail if tile in merged else tail
+
+
+def store_packed(out_tile, packing, row, value, merged):
+    for t in range(packing.full):
+        lanes = slice(t * LANES, (t + 1) * LANES)
+        out_tile(row * packing.full + t, value[..., lanes].astype(jnp.bfloat16))
+    add_tail(packing, row, value, merged)
 
 
 def store_tails(out_tile, merged):
@@ -206,19 +210,22 @@
     copies[0].wait()
     copies[1].wait()
     scaled = probes_here[...].astype(f32)
-    scaled = [padded(scaled[:, p, :] * prior[p]) for p in range(points)]
+    tiles = {}
+    tails = {}
+    for p in range(points):
+        store_packed(tiles.__setitem__, packing, 2 * points + p, padded(scaled[:, p, :] * prior[p]), tails)
     for slot, out in enumerate(outs):
         copies[2 + slot].wait()
 
         def out_tile(tile, value, out=out):
             out[tile] = value
 
-        merged = {}
+        merged = dict(tails)
+        for tile, value in tiles.items():
+            out_tile(tile, value)
         for row in range(2 * points):
             value = padded(kernel_here[slot, row // points, row % points].astype(f32))
             store_packed(out_tile, packing, row, value, merged)
-        for p in range(points):
-            store_packed(out_tile, packing, 2 * points + p, scaled[p], merged)
         store_tails(out_tile, merged)
 
 
@@ -432,9 +439,7 @@
 
 
 def split_order(width):
-    far = list(range(width // 2, width))
-    near = list(range(width // 4, width // 2)) + list(range(1, width // 4))
-    return [0] + far, near
+    return list(range(width // 2)), list(range(width // 2, width))
 
 
 def stage_kernel(far, near, sem):

time: 66.4 us -> 65.6 us (0.988)
  waiting for transfers between devices: 11.1 us -> 9.56 us
    ppermute x7, waiting for transfers between devices: 8.63 us -> 7.08 us  [local_split(): lax.ppermute(value, 'pts', [(i, i ^ relative) for i in range(width)])]
  transfers between devices with their start and end apart: 20 -> 20, of which waited for: 6 -> 5; matrix products, arithmetic and copies ran while one was open for 0% -> 0% of each run, Pallas kernels for 16% -> 17%
where the time goes in v4:
time: 65.6 us; the launch traced here: 65.3 us
  blocking collectives  25.5 us (39%)
  starting transfers between devices  16.2 us (25%)
  Pallas kernels  13.8 us (21%)
  waiting for transfers between devices  9.56 us (15%)
    all_to_all x2, blocking collectives, exchange(): lax.all_to_all(value, 'pts', split_axis=0, concat_axis=0, tiled=False)  25.5 us
    ppermute x7, starting transfers between devices, local_split(): lax.ppermute(value, 'pts', [(i, i ^ relative) for i in range(width)])  13.4 us
    ppermute x7, waiting for transfers between devices, local_split(): lax.ppermute(value, 'pts', [(i, i ^ relative) for i in range(width)])  7.08 us
    pallas_call x1, Pallas kernels, local_split(): pl.pallas_call(functools.partial(bins_kernel, orders=orders, packing_back...  5.98 us
    ppermute x13, starting transfers between devices, swap(): return lax.ppermute(value, 'sen', [(0, 1), (1, 0)])  2.86 us
    ppermute x13, waiting for transfers between devices, swap(): return lax.ppermute(value, 'sen', [(0, 1), (1, 0)])  2.48 us
    pallas_call x1, Pallas kernels, local_split(): pl.pallas_call(functools.partial(pack_kernel, order=order, sens=sens, hal...  2.18 us
    pallas_call x1, Pallas kernels, local_split(): pl.pallas_call(functools.partial(deflate_kernel, points=points, steps=ste...  1.76 us
  transfers between devices with their start and end apart: 20, of which 5 were waited for; matrix products, arithmetic and copies ran while one was open for 0% of the time, Pallas kernels for 17%

profile of v4, /device:TPU:0, one launch (start us, length us, event | category | flops | bytes accessed | tf_op | source)
XLA Modules:
  0.0 65.3 jit_solution(13924624811024413365)
XLA Ops:
  0.0 0.5 collective-permute-start.16
  0.5 0.1 pad_add_fusion.index
  0.6 2.2 %pack.1 = (bf16[40,8,128]{2,1,0:T(8,128)(2,1)S(1)}, bf16[40,8,128]{2,1,0:T(8,128)(2,1)S(1)}, bf16[40,8,128]{2,1,0:T(8,128)(2,1)S(1)}, bf16[40,8,128]{2,1,0:T(8,1...) custom-call(s32[2]{0:T(128)S(1)} %pad_add_fusion.index, ...), custom_call_target="tpu_custom_call" | custom-call | tf_op jit(solution)/shard_map/pack/pallas_call | solution.py:496
  2.8 2.5 %collective-permute-start.1 = (bf16[40,8,128]{2,1,0:T(8,128)(2,1)S(1)}, bf16[40,8,128]{2,1,0:T(8,128)(2,1)S(1)}, u32[]{:S(2)}, u32[]{:S(2)}) collective-permute-start(bf16[40,8,128]{2,1,0:T(8,128)(2,1)S(1)} %get-tuple-element.21), channel_id=1, source_target_pairs={{0,2},{2,0},{4,6},{6,4},{8,10},{10,8},{12,14},{14,12},{1,3},{3,1},... | collective-permute-start | bytes 245768 | tf_op jit(solution)/shard_map/ppermute | solution.py:514
  5.3 1.6 %collective-permute-start.2 = (bf16[40,8,128]{2,1,0:T(8,128)(2,1)S(1)}, bf16[40,8,128]{2,1,0:T(8,128)(2,1)S(1)}, u32[]{:S(2)}, u32[]{:S(2)}) collective-permute-start(bf16[40,8,128]{2,1,0:T(8,128)(2,1)S(1)} %get-tuple-element.22), channel_id=1, source_target_pairs={{0,4},{2,6},{4,0},{6,2},{8,12},{10,14},{12,8},{14,10},{1,5},{3,7},... | collective-permute-start | bytes 245768 | tf_op jit(solution)/shard_map/ppermute | solution.py:514
  6.9 0.0 collective-permute-start.3
  6.9 0.0 collective-permute-start
  6.9 1.3 %collective-permute-done.noise_other = f32[64]{0:T(128)S(1)} collective-permute-done((f32[64]{0:T(128)}, f32[64]{0:T(128)S(1)}, u32[]{:S(2)}, u32[]{:S(2)}) %collective-permute-start) | collective-permute-done | bytes 288 | tf_op jit(solution)/shard_map/ppermute | solution.py:482
  8.2 0.2 collective-permute-start.4
  8.3 0.1 collective-permute-done.1.refs_1_
  8.4 2.9 %collective-permute-start.8 = (bf16[40,8,128]{2,1,0:T(8,128)(2,1)S(1)}, bf16[40,8,128]{2,1,0:T(8,128)(2,1)S(1)}, u32[]{:S(2)}, u32[]{:S(2)}) collective-permute-start(bf16[40,8,128]{2,1,0:T(8,128)(2,1)S(1)} %get-tuple-element.26), channel_id=1, source_target_pairs={{0,8},{2,10},{4,12},{6,14},{8,0},{10,2},{12,4},{14,6},{1,9},{3,11}... | collective-permute-start | bytes 245768 | tf_op jit(solution)/shard_map/ppermute | solution.py:514
  11.4 0.0 collective-permute-done.2.refs_2_
  11.4 1.3 %collective-permute-start.9 = (bf16[40,8,128]{2,1,0:T(8,128)(2,1)S(1)}, bf16[40,8,128]{2,1,0:T(8,128)(2,1)S(1)}, u32[]{:S(2)}, u32[]{:S(2)}) collective-permute-start(bf16[40,8,128]{2,1,0:T(8,128)(2,1)S(1)} %get-tuple-element.27), channel_id=1, source_target_pairs={{0,10},{2,8},{4,14},{6,12},{8,2},{10,0},{12,6},{14,4},{1,11},{3,9}... | collective-permute-start | bytes 245768 | tf_op jit(solution)/shard_map/ppermute | solution.py:514
  12.6 0.0 collective-permute-done.3.refs_3_
  12.6 3.6 %collective-permute-start.10 = (bf16[40,8,128]{2,1,0:T(8,128)(2,1)S(1)}, bf16[40,8,128]{2,1,0:T(8,128)(2,1)S(1)}, u32[]{:S(2)}, u32[]{:S(2)}) collective-permute-start(bf16[40,8,128]{2,1,0:T(8,128)(2,1)S(1)} %get-tuple-element.28), channel_id=1, source_target_pairs={{0,12},{2,14},{4,8},{6,10},{8,4},{10,6},{12,0},{14,2},{1,13},{3,15... | collective-permute-start | bytes 245768 | tf_op jit(solution)/shard_map/ppermute | solution.py:514
  16.2 0.0 collective-permute-done.4.refs_4_
  16.2 0.0 copy-start.2
  16.2 0.0 copy-start.4
  16.2 1.4 %collective-permute-start.11 = (bf16[40,8,128]{2,1,0:T(8,128)(2,1)S(1)}, bf16[40,8,128]{2,1,0:T(8,128)(2,1)S(1)}, u32[]{:S(2)}, u32[]{:S(2)}) collective-permute-start(bf16[40,8,128]{2,1,0:T(8,128)(2,1)S(1)} %get-tuple-element.29), channel_id=1, source_target_pairs={{0,14},{2,12},{4,10},{6,8},{8,6},{10,4},{12,2},{14,0},{1,15},{3,13... | collective-permute-start | bytes 245768 | tf_op jit(solution)/shard_map/ppermute | solution.py:514
  17.7 0.0 collective-permute-done.8.refs_0_
  17.7 0.0 collective-permute-start.5
  17.7 7.0 %collective-permute-done.9.refs_1_ = bf16[40,8,128]{2,1,0:T(8,128)(2,1)S(1)} collective-permute-done((bf16[40,8,128]{2,1,0:T(8,128)(2,1)S(1)}, bf16[40,8,128]{2,1,0:T(8,128)(2,1)S(1)}, u32[]{:S(2)}, u32[]{:S(2)}) %collective-permute-start.9) | collective-permute-done | bytes 81952 | tf_op jit(solution)/shard_map/ppermute | solution.py:514
  24.7 0.0 collective-permute-start.6
  24.7 0.0 collective-permute-done.10.refs_2_
  24.7 0.5 collective-permute-start.7
  25.2 0.0 collective-permute-done.11.refs_3_
  25.2 0.1 collective-permute-start.12
  25.3 0.0 collective-permute-done.5.refs_5_
  25.3 0.4 collective-permute-start.13
  25.7 0.2 collective-permute-done.6.refs_6_
  26.0 0.2 collective-permute-start.14
  26.1 0.0 collective-permute-done.7.refs_7_
  26.1 0.4 collective-permute-start.15
  26.5 0.0 collective-permute-done.12.refs_4_
  26.5 0.2 collective-permute-start.17
  26.6 1.2 %stage.1.table = bf16[512,1024]{1,0:T(8,128)(2,1)S(1)} custom-call(bf16[512,1024]{1,0:T(8,128)(2,1)} %constant.12.clone.far), custom_call_target="tpu_custom_call" | custom-call | tf_op jit(solution)/shard_map/stage/pallas_call | solution.py:530
  27.9 1.5 %first.1 = (f32[3,16,16,512]{3,2,1,0:T(8,128)S(1)}, f32[128,1024]{1,0:T(8,128)S(1)}) custom-call(bf16[512,1024]{1,0:T(8,128)(2,1)S(1)} %stage.1.table, bf16[40,8,128]{2,1,0:T(8,128)(2,1)S(1)} %get-tuple-element.20.refs_0_, bf16[40,8,128]{2,1,0:T(8,128)(2,1)S(1)} %collective-permute-done.1.refs_1_, bf16[40,8,128]{2,1,0:T(8,128)(2,1)S(1)} %collective-permute-done.2.refs_2_, ...), custom_call_target="tpu_custom_call" | custom-call | tf_op jit(solution)/shard_map/first/pallas_call | solution.py:540
  29.4 0.0 collective-permute-done.13.refs_5_
  29.4 0.0 collective-permute-done.14.refs_6_
  29.4 0.0 collective-permute-done.15.refs_7_
  29.4 0.0 copy-done.2
  29.5 0.0 copy-done.4
  29.5 0.0 copy-start
  29.5 0.0 copy-start.3
  29.5 6.0 %bins.1 = bf16[8,14,8,128]{3,2,1,0:T(8,128)(2,1)S(1)} custom-call(s32[1]{0:T(128)} %bitcast.1.index, f32[64]{0:T(128)S(1)} %copy-done.4, f32[64]{0:T(128)S(1)} %collective-permute-done.noise_other, bf16[512,1024]{1,0:T(8,128)(2,1)S(1)} %stage.1.table, f32[1,512]{1,0:T(1,128)S(1)} %copy-done.2, f32[3,16,16,512]{3,2,1,0:T(8,128)S(1)} %get-tuple-element.24.kern_first, ...), custom_call_target="tpu_custom_call" | custom-call | tf_op jit(solution)/shard_map/bins/pallas_call | solution.py:553
  35.5 0.0 collective-permute-done.17
  35.5 0.0 collective-permute-done.16.basis_other
  35.5 15.0 %all_to_all.10.parts = bf16[8,14,8,128]{3,2,1,0:T(8,128)(2,1)S(1)} all-to-all(bf16[8,14,8,128]{3,2,1,0:T(8,128)(2,1)S(1)} %bins.1), channel_id=1, replica_groups=mesh['grp'=2,'pts'=8,'sen'=2] {'pts'}, dimensions={0} | all-to-all | bytes 458752 | tf_op jit(solution)/shard_map/all_to_all | solution.py:485
  50.5 0.0 copy-done
  50.5 0.0 copy-done.3
  50.5 0.0 copy-start.1
  50.5 1.1 %coeff.1 = (f32[8,1680]{1,0:T(8,128)S(1)}, bf16[8,8,1024]{2,1,0:T(8,128)(2,1)S(1)}) custom-call(f32[4]{0:T(128)S(1)} %copy-done.3, bf16[8,14,8,128]{3,2,1,0:T(8,128)(2,1)S(1)} %all_to_all.10.parts, bf16[1680,512]{1,0:T(8,128)(2,1)S(1)} %copy-done, bf16[1680,512]{1,0:T(8,128)(2,1)S(1)} %collective-permute-done.16.basis_other), custom_call_target="tpu_custom_call" | custom-call | tf_op jit(solution)/shard_map/coeff/pallas_call | solution.py:573
  51.6 10.5 %all_to_all.11.parts_own = bf16[8,8,1024]{2,1,0:T(8,128)(2,1)S(1)} all-to-all(bf16[8,8,1024]{2,1,0:T(8,128)(2,1)S(1)} %get-tuple-element.32), channel_id=1, replica_groups=mesh['grp'=2,'pts'=8,'sen'=2] {'pts'}, dimensions={0} | all-to-all | bytes 262144 | tf_op jit(solution)/shard_map/all_to_all | solution.py:485
  62.1 0.0 collective-permute-start.18
  62.1 0.5 collective-permute-start.19
  62.6 0.9 %collective-permute-done.19.flat_other = f32[8,1680]{1,0:T(8,128)S(1)} collective-permute-done((f32[8,1680]{1,0:T(8,128)S(1)}, f32[8,1680]{1,0:T(8,128)S(1)}, u32[]{:S(2)}, u32[]{:S(2)}) %collective-permute-start.19) | collective-permute-done | bytes 53792 | tf_op jit(solution)/shard_map/ppermute | solution.py:482
  63.6 0.0 collective-permute-done.18.parts_other
  63.6 0.0 copy-done.1
  63.6 1.8 %deflate.1 = f32[16,4,420]{2,1,0:T(4,128)} custom-call(s32[1]{0:T(128)} %bitcast.core, bf16[8,8,1024]{2,1,0:T(8,128)(2,1)S(1)} %all_to_all.11.parts_own, bf16[8,8,1024]{2,1,0:T(8,128)(2,1)S(1)} %collective-permute-done.18.parts_other, f32[1,512]{1,0:T(1,128)S(1)} %bitcast.4, f32[1,512]{1,0:T(1,128)S(1)} %bitcast.5, ...), custom_call_target="tpu_custom_call" | custom-call | tf_op jit(solution)/shard_map/deflate/pallas_call | solution.py:587
Async XLA Ops:
  0.0 35.5 %collective-permute-start.16 = (bf16[1680,512]{1,0:T(8,128)(2,1)}, bf16[1680,512]{1,0:T(8,128)(2,1)S(1)}, u32[]{:S(2)}, u32[]{:S(2)}) collective-permute-start(bf16[1680,512]{1,0:T(8,128)(2,1)} %basis_own.3), channel_id=1, source_target_pairs={{0,1},{1,0},{2,3},{3,2},{4,5},{5,4},{6,7},{7,6},{8,9},{9,8},{10,11... | collective-permute-start | bytes 5160968 | tf_op jit(solution)/shard_map/ppermute | solution.py:482
  2.8 5.7 %collective-permute-start.1 = (bf16[40,8,128]{2,1,0:T(8,128)(2,1)S(1)}, bf16[40,8,128]{2,1,0:T(8,128)(2,1)S(1)}, u32[]{:S(2)}, u32[]{:S(2)}) collective-permute-start(bf16[40,8,128]{2,1,0:T(8,128)(2,1)S(1)} %get-tuple-element.21), channel_id=1, source_target_pairs={{0,2},{2,0},{4,6},{6,4},{8,10},{10,8},{12,14},{14,12},{1,3},{3,1},... | collective-permute-start | bytes 245768 | tf_op jit(solution)/shard_map/ppermute | solution.py:514
  5.3 6.1 %collective-permute-start.2 = (bf16[40,8,128]{2,1,0:T(8,128)(2,1)S(1)}, bf16[40,8,128]{2,1,0:T(8,128)(2,1)S(1)}, u32[]{:S(2)}, u32[]{:S(2)}) collective-permute-start(bf16[40,8,128]{2,1,0:T(8,128)(2,1)S(1)} %get-tuple-element.22), channel_id=1, source_target_pairs={{0,4},{2,6},{4,0},{6,2},{8,12},{10,14},{12,8},{14,10},{1,5},{3,7},... | collective-permute-start | bytes 245768 | tf_op jit(solution)/shard_map/ppermute | solution.py:514
  6.9 5.7 %collective-permute-start.3 = (bf16[40,8,128]{2,1,0:T(8,128)(2,1)S(1)}, bf16[40,8,128]{2,1,0:T(8,128)(2,1)S(1)}, u32[]{:S(2)}, u32[]{:S(2)}) collective-permute-start(bf16[40,8,128]{2,1,0:T(8,128)(2,1)S(1)} %get-tuple-element.23), channel_id=1, source_target_pairs={{0,6},{2,4},{4,2},{6,0},{8,14},{10,12},{12,10},{14,8},{1,7},{3,5},... | collective-permute-start | bytes 245768 | tf_op jit(solution)/shard_map/ppermute | solution.py:514
  6.9 1.3 %collective-permute-start = (f32[64]{0:T(128)}, f32[64]{0:T(128)S(1)}, u32[]{:S(2)}, u32[]{:S(2)}) collective-permute-start(f32[64]{0:T(128)} %noise_own.1), channel_id=1, source_target_pairs={{0,1},{1,0},{2,3},{3,2},{4,5},{5,4},{6,7},{7,6},{8,9},{9,8},{10,11... | collective-permute-start | bytes 776 | tf_op jit(solution)/shard_map/ppermute | solution.py:482
  8.2 8.1 %collective-permute-start.4 = (bf16[40,8,128]{2,1,0:T(8,128)(2,1)S(1)}, bf16[40,8,128]{2,1,0:T(8,128)(2,1)S(1)}, u32[]{:S(2)}, u32[]{:S(2)}) collective-permute-start(bf16[40,8,128]{2,1,0:T(8,128)(2,1)S(1)} %get-tuple-element.20.refs_0_), channel_id=1, source_target_pairs={{0,1},{1,0},{2,3},{3,2},{4,5},{5,4},{6,7},{7,6},{8,9},{9,8},{10,11... | collective-permute-start | bytes 245768 | tf_op jit(solution)/shard_map/ppermute | solution.py:482
  8.4 9.3 %collective-permute-start.8 = (bf16[40,8,128]{2,1,0:T(8,128)(2,1)S(1)}, bf16[40,8,128]{2,1,0:T(8,128)(2,1)S(1)}, u32[]{:S(2)}, u32[]{:S(2)}) collective-permute-start(bf16[40,8,128]{2,1,0:T(8,128)(2,1)S(1)} %get-tuple-element.26), channel_id=1, source_target_pairs={{0,8},{2,10},{4,12},{6,14},{8,0},{10,2},{12,4},{14,6},{1,9},{3,11}... | collective-permute-start | bytes 245768 | tf_op jit(solution)/shard_map/ppermute | solution.py:514
  11.4 13.3 %collective-permute-start.9 = (bf16[40,8,128]{2,1,0:T(8,128)(2,1)S(1)}, bf16[40,8,128]{2,1,0:T(8,128)(2,1)S(1)}, u32[]{:S(2)}, u32[]{:S(2)}) collective-permute-start(bf16[40,8,128]{2,1,0:T(8,128)(2,1)S(1)} %get-tuple-element.27), channel_id=1, source_target_pairs={{0,10},{2,8},{4,14},{6,12},{8,2},{10,0},{12,6},{14,4},{1,11},{3,9}... | collective-permute-start | bytes 245768 | tf_op jit(solution)/shard_map/ppermute | solution.py:514
  12.6 12.1 %collective-permute-start.10 = (bf16[40,8,128]{2,1,0:T(8,128)(2,1)S(1)}, bf16[40,8,128]{2,1,0:T(8,128)(2,1)S(1)}, u32[]{:S(2)}, u32[]{:S(2)}) collective-permute-start(bf16[40,8,128]{2,1,0:T(8,128)(2,1)S(1)} %get-tuple-element.28), channel_id=1, source_target_pairs={{0,12},{2,14},{4,8},{6,10},{8,4},{10,6},{12,0},{14,2},{1,13},{3,15... | collective-permute-start | bytes 245768 | tf_op jit(solution)/shard_map/ppermute | solution.py:514
  16.2 13.2 %copy-start.2 = (f32[1,512]{1,0:T(1,128)S(1)}, f32[1,512]{1,0:T(1,128)}, u32[]{:S(2)}) copy-start(f32[1,512]{1,0:T(1,128)} %constant.13.clone.weights) | copy-start | bytes 6148
  16.2 13.2 %copy-start.4 = (f32[64]{0:T(128)S(1)}, f32[64]{0:T(128)}, u32[]{:S(2)}) copy-start(f32[64]{0:T(128)} %noise_own.1) | copy-start | bytes 772
  16.2 9.0 %collective-permute-start.11 = (bf16[40,8,128]{2,1,0:T(8,128)(2,1)S(1)}, bf16[40,8,128]{2,1,0:T(8,128)(2,1)S(1)}, u32[]{:S(2)}, u32[]{:S(2)}) collective-permute-start(bf16[40,8,128]{2,1,0:T(8,128)(2,1)S(1)} %get-tuple-element.29), channel_id=1, source_target_pairs={{0,14},{2,12},{4,10},{6,8},{8,6},{10,4},{12,2},{14,0},{1,15},{3,13... | collective-permute-start | bytes 245768 | tf_op jit(solution)/shard_map/ppermute | solution.py:514
  17.7 7.6 %collective-permute-start.5 = (bf16[40,8,128]{2,1,0:T(8,128)(2,1)S(1)}, bf16[40,8,128]{2,1,0:T(8,128)(2,1)S(1)}, u32[]{:S(2)}, u32[]{:S(2)}) collective-permute-start(bf16[40,8,128]{2,1,0:T(8,128)(2,1)S(1)} %collective-permute-done.1.refs_1_), channel_id=1, source_target_pairs={{0,1},{1,0},{2,3},{3,2},{4,5},{5,4},{6,7},{7,6},{8,9},{9,8},{10,11... | collective-permute-start | bytes 245768 | tf_op jit(solution)/shard_map/ppermute | solution.py:482
  24.7 1.3 %collective-permute-start.6 = (bf16[40,8,128]{2,1,0:T(8,128)(2,1)S(1)}, bf16[40,8,128]{2,1,0:T(8,128)(2,1)S(1)}, u32[]{:S(2)}, u32[]{:S(2)}) collective-permute-start(bf16[40,8,128]{2,1,0:T(8,128)(2,1)S(1)} %collective-permute-done.2.refs_2_), channel_id=1, source_target_pairs={{0,1},{1,0},{2,3},{3,2},{4,5},{5,4},{6,7},{7,6},{8,9},{9,8},{10,11... | collective-permute-start | bytes 245768 | tf_op jit(solution)/shard_map/ppermute | solution.py:482
  24.7 1.4 %collective-permute-start.7 = (bf16[40,8,128]{2,1,0:T(8,128)(2,1)S(1)}, bf16[40,8,128]{2,1,0:T(8,128)(2,1)S(1)}, u32[]{:S(2)}, u32[]{:S(2)}) collective-permute-start(bf16[40,8,128]{2,1,0:T(8,128)(2,1)S(1)} %collective-permute-done.3.refs_3_), channel_id=1, source_target_pairs={{0,1},{1,0},{2,3},{3,2},{4,5},{5,4},{6,7},{7,6},{8,9},{9,8},{10,11... | collective-permute-start | bytes 245768 | tf_op jit(solution)/shard_map/ppermute | solution.py:482
  25.2 1.3 %collective-permute-start.12 = (bf16[40,8,128]{2,1,0:T(8,128)(2,1)S(1)}, bf16[40,8,128]{2,1,0:T(8,128)(2,1)S(1)}, u32[]{:S(2)}, u32[]{:S(2)}) collective-permute-start(bf16[40,8,128]{2,1,0:T(8,128)(2,1)S(1)} %collective-permute-done.8.refs_0_), channel_id=1, source_target_pairs={{0,1},{1,0},{2,3},{3,2},{4,5},{5,4},{6,7},{7,6},{8,9},{9,8},{10,11... | collective-permute-start | bytes 245768 | tf_op jit(solution)/shard_map/ppermute | solution.py:482
  25.3 4.1 %collective-permute-start.13 = (bf16[40,8,128]{2,1,0:T(8,128)(2,1)S(1)}, bf16[40,8,128]{2,1,0:T(8,128)(2,1)S(1)}, u32[]{:S(2)}, u32[]{:S(2)}) collective-permute-start(bf16[40,8,128]{2,1,0:T(8,128)(2,1)S(1)} %collective-permute-done.9.refs_1_), channel_id=1, source_target_pairs={{0,1},{1,0},{2,3},{3,2},{4,5},{5,4},{6,7},{7,6},{8,9},{9,8},{10,11... | collective-permute-start | bytes 245768 | tf_op jit(solution)/shard_map/ppermute | solution.py:482
  26.0 3.5 %collective-permute-start.14 = (bf16[40,8,128]{2,1,0:T(8,128)(2,1)S(1)}, bf16[40,8,128]{2,1,0:T(8,128)(2,1)S(1)}, u32[]{:S(2)}, u32[]{:S(2)}) collective-permute-start(bf16[40,8,128]{2,1,0:T(8,128)(2,1)S(1)} %collective-permute-done.10.refs_2_), channel_id=1, source_target_pairs={{0,1},{1,0},{2,3},{3,2},{4,5},{5,4},{6,7},{7,6},{8,9},{9,8},{10,11... | collective-permute-start | bytes 245768 | tf_op jit(solution)/shard_map/ppermute | solution.py:482
  26.1 3.3 %collective-permute-start.15 = (bf16[40,8,128]{2,1,0:T(8,128)(2,1)S(1)}, bf16[40,8,128]{2,1,0:T(8,128)(2,1)S(1)}, u32[]{:S(2)}, u32[]{:S(2)}) collective-permute-start(bf16[40,8,128]{2,1,0:T(8,128)(2,1)S(1)} %collective-permute-done.11.refs_3_), channel_id=1, source_target_pairs={{0,1},{1,0},{2,3},{3,2},{4,5},{5,4},{6,7},{7,6},{8,9},{9,8},{10,11... | collective-permute-start | bytes 245768 | tf_op jit(solution)/shard_map/ppermute | solution.py:482
  26.5 9.0 %collective-permute-start.17 = (f32[512]{0:T(512)}, f32[512]{0:T(512)S(1)}, u32[]{:S(2)}, u32[]{:S(2)}) collective-permute-start(f32[512]{0:T(512)} %param.13), channel_id=1, source_target_pairs={{0,1},{1,0},{2,3},{3,2},{4,5},{5,4},{6,7},{7,6},{8,9},{9,8},{10,11... | collective-permute-start | bytes 6152 | tf_op jit(solution)/shard_map/ppermute | solution.py:482
  29.5 21.0 %copy-start = (bf16[1680,512]{1,0:T(8,128)(2,1)S(1)}, bf16[1680,512]{1,0:T(8,128)(2,1)}, u32[]{:S(2)}) copy-start(bf16[1680,512]{1,0:T(8,128)(2,1)} %basis_own.3) | copy-start | bytes 5160964
  29.5 21.0 %copy-start.3 = (f32[4]{0:T(128)S(1)}, f32[4]{0:T(128)}, u32[]{:S(2)}) copy-start(f32[4]{0:T(128)} %prior.1) | copy-start | bytes 52
  50.5 13.1 %copy-start.1 = (f32[512]{0:T(512)S(1)}, f32[512]{0:T(512)}, u32[]{:S(2)}) copy-start(f32[512]{0:T(512)} %param.13) | copy-start | bytes 6148
  62.1 1.4 %collective-permute-start.18 = (bf16[8,8,1024]{2,1,0:T(8,128)(2,1)S(1)}, bf16[8,8,1024]{2,1,0:T(8,128)(2,1)S(1)}, u32[]{:S(2)}, u32[]{:S(2)}) collective-permute-start(bf16[8,8,1024]{2,1,0:T(8,128)(2,1)S(1)} %all_to_all.11.parts_own), channel_id=1, source_target_pairs={{0,1},{1,0},{2,3},{3,2},{4,5},{5,4},{6,7},{7,6},{8,9},{9,8},{10,11... | collective-permute-start | bytes 393224 | tf_op jit(solution)/shard_map/ppermute | solution.py:482
  62.1 1.4 %collective-permute-start.19 = (f32[8,1680]{1,0:T(8,128)S(1)}, f32[8,1680]{1,0:T(8,128)S(1)}, u32[]{:S(2)}, u32[]{:S(2)}) collective-permute-start(f32[8,1680]{1,0:T(8,128)S(1)} %get-tuple-element.34.flat_own), channel_id=1, source_target_pairs={{0,1},{1,0},{2,3},{3,2},{4,5},{5,4},{6,7},{7,6},{8,9},{9,8},{10,11... | collective-permute-start | bytes 161288 | tf_op jit(solution)/shard_map/ppermute | solution.py:482

commit v5 on v4

--- a/solution.py
+++ b/solution.py
@@ -181,7 +181,7 @@
         out_tile(tile, value.astype(jnp.bfloat16))
 
 
-def pack_kernel(index, prior_far, kernel, probes, *refs, order, sens, half, packing):
+def pack_kernel(index, prior_far, kernel, probes, *refs, order, half, packing):
     outs = refs[: len(order)]
     prior, kernel_here, probes_here, sems = refs[len(order) :]
     f32 = jnp.float32
@@ -193,13 +193,9 @@
         pltpu.make_async_copy(probes.at[pl.ds(mine, half)], probes_here, sems.at[0]),
         pltpu.make_async_copy(prior_far, prior, sems.at[1]),
     ]
-    for slot, relative in enumerate(order):
-        rows = pl.ds(pl.multiple_of((me ^ relative) * sens, sens), sens)
-        copies.append(
-            pltpu.make_async_copy(
-                kernel.at[:, :, rows, :], kernel_here.at[slot], sems.at[2 + slot]
-            )
-        )
+    for row in range(2 * points):
+        at = (row // points, row % points)
+        copies.append(pltpu.make_async_copy(kernel.at[at], kernel_here.at[at], sems.at[2 + row]))
     for copy in copies:
         copy.start()
 
@@ -214,8 +210,9 @@
     tails = {}
     for p in range(points):
         store_packed(tiles.__setitem__, packing, 2 * points + p, padded(scaled[:, p, :] * prior[p]), tails)
-    for slot, out in enumerate(outs):
-        copies[2 + slot].wait()
+    for copy in copies[2:]:
+        copy.wait()
+    for relative, out in zip(order, outs):
 
         def out_tile(tile, value, out=out):
             out[tile] = value
@@ -224,7 +221,7 @@
         for tile, value in tiles.items():
             out_tile(tile, value)
         for row in range(2 * points):
-            value = padded(kernel_here[slot, row // points, row % points].astype(f32))
+            value = padded(kernel_here[row // points, row % points, me ^ relative].astype(f32))
             store_packed(out_tile, packing, row, value, merged)
         store_tails(out_tile, merged)
 
@@ -318,12 +315,18 @@
 
 
 def bins_kernel(
-    index, noise_own, noise_other, table, weights, kern_first, data_first, *refs,
+    index, noise_far, noise_other_far, table, weights, kern_first, data_first, *refs,
     orders, points, sens, half, wide, packing, packing_back,
 ):
     count = len(orders[1])
     sources = paired(refs, count)
-    out, kern, spec, rows, data, wdata, adjoint = refs[2 * count :]
+    out, kern, spec, rows, data, wdata, adjoint, noise_own, noise_other, sems = refs[2 * count :]
+    copies = [
+        pltpu.make_async_copy(noise_far, noise_own, sems.at[0]),
+        pltpu.make_async_copy(noise_other_far, noise_other, sems.at[1]),
+    ]
+    for copy in copies:
+        copy.start()
     tiles = wide // LANES
     f32 = jnp.float32
     bf16 = jnp.bfloat16
@@ -336,6 +339,8 @@
         [data[:, :wide] * weight_rows, data[:, wide:] * weight_rows], axis=1
     ).astype(bf16)
     observed = lax.dot_general(scaled, table_v, NT, preferred_element_type=f32)
+    for copy in copies:
+        copy.wait()
     mine = index[0] * sens
     scales = [noise_own[mine + s] for s in range(sens)]
     scales += [noise_other[mine + s] for s in range(sens)]
@@ -350,33 +355,33 @@
     wdata[2] = real
 
     base = 0
+    group = 2 * points
     for source, order in ((kern_first, orders[0]), (kern, orders[1])):
 
         def adjoint_tile(step, carry, source=source, base=base):
-            b = step // tiles
+            first = step // tiles * group
             ft = step % tiles
             lanes = pl.ds(pl.multiple_of(ft * LANES, LANES), LANES)
             shifted = pl.ds(pl.multiple_of(wide + ft * LANES, LANES), LANES)
             zero = jnp.zeros((half, LANES), f32)
-            acc = [zero] * (3 * points)
+            acc = [zero] * (3 * group)
             for s in range(2 * sens):
                 at = slice(s * half, (s + 1) * half)
                 both = wdata[0, at, lanes]
                 imag = wdata[1, at, lanes]
                 real = wdata[2, at, lanes]
                 row = slice(s, s + 1)
-                for p in range(points):
-                    q = b * points + p
-                    acc[3 * p] += source[0, q, row, lanes] * both
-                    acc[3 * p + 1] += source[2, q, row, lanes] * imag
-                    acc[3 * p + 2] += source[1, q, row, lanes] * real
-            for p in range(points):
-                at = pl.ds(pl.multiple_of((base + b * points + p) * half, ROWS), half)
+                for p in range(group):
+                    acc[3 * p] += source[0, first + p, row, lanes] * both
+                    acc[3 * p + 1] += source[2, first + p, row, lanes] * imag
+                    acc[3 * p + 2] += source[1, first + p, row, lanes] * real
+            for p in range(group):
+                at = pl.ds(pl.multiple_of((base + first + p) * half, ROWS), half)
                 adjoint[at, lanes] = acc[3 * p] - acc[3 * p + 1]
                 adjoint[at, shifted] = acc[3 * p] - acc[3 * p + 2]
             return carry
 
-        lax.fori_loop(0, len(order) * tiles, adjoint_tile, 0)
+        lax.fori_loop(0, len(order) * points // group * tiles, adjoint_tile, 0)
         base += len(order) * points
     back = lax.dot_general(adjoint[...].astype(bf16), table_v, NT, preferred_element_type=f32)
     for b, relative in enumerate(orders[0] + orders[1]):
@@ -399,14 +404,16 @@
     return total
 
 
-def coeff_kernel(prior, parts, basis_own, basis_other, flat, coeff, *, points, steps, rank, packing):
+def coeff_kernel(
+    prior, parts, basis_own, basis_other, flat, coeff, *, points, steps, rank, packing
+):
     f32 = jnp.float32
     total = summed(parts)
     for p in range(points):
         tiles = [total[p * packing.full + t] for t in range(packing.full)]
         tile, lane = packing.place(p)
         tiles.append(turned(total[tile], -lane))
-        piece = jnp.concatenate(tiles, axis=1) * prior[p]
+        piece = jnp.concatenate(tiles, axis=1) * prior[:, p : p + 1]
         flat[:, p * steps : (p + 1) * steps] = piece[:, :steps]
     low = flat[...].astype(jnp.bfloat16)
     own = jnp.dot(low, basis_own[...], preferred_element_type=f32).astype(jnp.bfloat16)
@@ -494,19 +501,19 @@
     chunk = jax.ShapeDtypeStruct((packing.tiles, sens, LANES), bf16)
     in_hbm = pl.BlockSpec(memory_space=pltpu.HBM)
     sent = pl.pallas_call(
-        functools.partial(pack_kernel, order=order, sens=sens, half=half, packing=packing),
+        functools.partial(pack_kernel, order=order, half=half, packing=packing),
         out_shape=(chunk,) * width,
         in_specs=in_smem(1) + [in_hbm] * 3,
         out_specs=tuple(in_vmem(width)),
         scratch_shapes=[
             pltpu.SMEM(prior_scale.shape, f32),
-            pltpu.VMEM((width, 2, points, sens, bins_count), bf16),
+            pltpu.VMEM((2, points, width, sens, bins_count), bf16),
             pltpu.VMEM((half, points, steps), bf16),
-            pltpu.SemaphoreType.DMA((2 + width,)),
+            pltpu.SemaphoreType.DMA((2 + 2 * points,)),
         ],
         compiler_params=limit(8),
         name="pack",
-    )(places, *kept(pltpu.HBM, prior_scale, kernel, probes))
+    )(places, *kept(pltpu.HBM, prior_scale, kernel.reshape(2, points, width, sens, bins_count), probes))
     blocks = {}
     others = {}
     for relative, value in zip(order, sent):
@@ -553,7 +560,7 @@
     back = pl.pallas_call(
         functools.partial(bins_kernel, orders=orders, packing_back=packing_back, **sizes),
         out_shape=jax.ShapeDtypeStruct((width, packing_back.tiles, half, LANES), bf16),
-        in_specs=in_smem(3) + in_vmem(4 + 2 * count),
+        in_specs=in_smem(1) + [in_hbm] * 2 + in_vmem(4 + 2 * count),
         out_specs=in_vmem(1)[0],
         scratch_shapes=[pltpu.VMEM((3, count * points, 2 * sens, wide), f32)]
         + scratch(count)
@@ -561,10 +568,16 @@
             pltpu.VMEM((2 * sens * half, 2 * wide), f32),
             pltpu.VMEM((3, 2 * sens * half, wide), f32),
             pltpu.VMEM((width * points * half, 2 * wide), f32),
+            pltpu.SMEM(noise_weight.shape, f32),
+            pltpu.SMEM(noise_weight.shape, f32),
+            pltpu.SemaphoreType.DMA((2,)),
         ],
         compiler_params=limit(20),
         name="bins",
-    )(me, noise_weight, noise_other, table, weights, kern_first, data_first, *ready(orders[1]))
+    )(
+        me, *kept(pltpu.HBM, noise_weight, noise_other), table, weights, kern_first, data_first,
+        *ready(orders[1]),
+    )
     back, basis_other, deflation_other = lax.optimization_barrier(
         (back, basis_other, deflation_other)
     )
@@ -576,11 +589,11 @@
             jax.ShapeDtypeStruct((half, points * steps), f32),
             jax.ShapeDtypeStruct((width, half, 2 * rank), bf16),
         ),
-        in_specs=in_smem(1) + in_vmem(3),
+        in_specs=in_vmem(4),
         out_specs=tuple(in_vmem(2)),
         compiler_params=limit(12),
         name="coeff",
-    )(prior_scale, parts, basis, basis_other)
+    )(prior_scale[None, :], parts, basis, basis_other)
     flat_other = swap(flat)
     coeff_parts = exchange(coeff)
     coeff_other = swap(coeff_parts)

time: 65.6 us -> 64.1 us (0.977)
  Pallas kernels: 13.8 us -> 12.3 us
    pallas_call x1, Pallas kernels: 5.98 us -> 5.28 us  [local_split(): pl.pallas_call(functools.partial(bins_kernel, orders=orders, packing_back...]
  transfers between devices with their start and end apart: 20 -> 20, of which waited for: 5 -> 5; matrix products, arithmetic and copies ran while one was open for 0% -> 0% of each run, Pallas kernels for 17% -> 16%
where the time goes in v5:
time: 64.1 us; the launch traced here: 63.8 us
  blocking collectives  25.5 us (40%)
  starting transfers between devices  16.2 us (25%)
  Pallas kernels  12.3 us (19%)
  waiting for transfers between devices  9.57 us (15%)
    all_to_all x2, blocking collectives, exchange(): lax.all_to_all(value, 'pts', split_axis=0, concat_axis=0, tiled=False)  25.5 us
    ppermute x7, starting transfers between devices, local_split(): lax.ppermute(value, 'pts', [(i, i ^ relative) for i in range(width)])  13.4 us
    ppermute x7, waiting for transfers between devices, local_split(): lax.ppermute(value, 'pts', [(i, i ^ relative) for i in range(width)])  7.08 us
    pallas_call x1, Pallas kernels, local_split(): pl.pallas_call(functools.partial(bins_kernel, orders=orders, packing_back...  5.28 us
    ppermute x13, starting transfers between devices, swap(): return lax.ppermute(value, 'sen', [(0, 1), (1, 0)])  2.86 us
    ppermute x13, waiting for transfers between devices, swap(): return lax.ppermute(value, 'sen', [(0, 1), (1, 0)])  2.48 us
    pallas_call x1, Pallas kernels, local_split(): pl.pallas_call(functools.partial(pack_kernel, order=order, half=half, pac...  1.85 us
    pallas_call x1, Pallas kernels, local_split(): pl.pallas_call(functools.partial(deflate_kernel, points=points, steps=ste...  1.76 us
  transfers between devices with their start and end apart: 20, of which 5 were waited for; matrix products, arithmetic and copies ran while one was open for 0% of the time, Pallas kernels for 16%

profile of v5, /device:TPU:0, one launch (start us, length us, event | category | flops | bytes accessed | tf_op | source)
XLA Modules:
  0.0 63.8 jit_solution(12744814475540941079)
XLA Ops:
  0.0 0.5 collective-permute-start.16
  0.5 0.1 pad_add_fusion.index
  0.6 1.9 %pack.1 = (bf16[40,8,128]{2,1,0:T(8,128)(2,1)S(1)}, bf16[40,8,128]{2,1,0:T(8,128)(2,1)S(1)}, bf16[40,8,128]{2,1,0:T(8,128)(2,1)S(1)}, bf16[40,8,128]{2,1,0:T(8,1...) custom-call(s32[2]{0:T(128)S(1)} %pad_add_fusion.index, ...), custom_call_target="tpu_custom_call" | custom-call | tf_op jit(solution)/shard_map/pack/pallas_call | solution.py:503
  2.4 2.5 %collective-permute-start.1 = (bf16[40,8,128]{2,1,0:T(8,128)(2,1)S(1)}, bf16[40,8,128]{2,1,0:T(8,128)(2,1)S(1)}, u32[]{:S(2)}, u32[]{:S(2)}) collective-permute-start(bf16[40,8,128]{2,1,0:T(8,128)(2,1)S(1)} %get-tuple-element.21), channel_id=1, source_target_pairs={{0,2},{2,0},{4,6},{6,4},{8,10},{10,8},{12,14},{14,12},{1,3},{3,1},... | collective-permute-start | bytes 245768 | tf_op jit(solution)/shard_map/ppermute | solution.py:521
  5.0 1.6 %collective-permute-start.2 = (bf16[40,8,128]{2,1,0:T(8,128)(2,1)S(1)}, bf16[40,8,128]{2,1,0:T(8,128)(2,1)S(1)}, u32[]{:S(2)}, u32[]{:S(2)}) collective-permute-start(bf16[40,8,128]{2,1,0:T(8,128)(2,1)S(1)} %get-tuple-element.22), channel_id=1, source_target_pairs={{0,4},{2,6},{4,0},{6,2},{8,12},{10,14},{12,8},{14,10},{1,5},{3,7},... | collective-permute-start | bytes 245768 | tf_op jit(solution)/shard_map/ppermute | solution.py:521
  6.5 0.0 collective-permute-start.3
  6.6 0.0 collective-permute-start
  6.6 1.3 %collective-permute-done.noise_other_far = f32[64]{0:T(128)S(1)} collective-permute-done((f32[64]{0:T(128)}, f32[64]{0:T(128)S(1)}, u32[]{:S(2)}, u32[]{:S(2)}) %collective-permute-start) | collective-permute-done | bytes 288 | tf_op jit(solution)/shard_map/ppermute | solution.py:489
  7.8 0.0 copy-start.4
  7.9 0.2 collective-permute-start.4
  8.0 0.1 collective-permute-done.1.refs_1_
  8.1 2.9 %collective-permute-start.8 = (bf16[40,8,128]{2,1,0:T(8,128)(2,1)S(1)}, bf16[40,8,128]{2,1,0:T(8,128)(2,1)S(1)}, u32[]{:S(2)}, u32[]{:S(2)}) collective-permute-start(bf16[40,8,128]{2,1,0:T(8,128)(2,1)S(1)} %get-tuple-element.26), channel_id=1, source_target_pairs={{0,8},{2,10},{4,12},{6,14},{8,0},{10,2},{12,4},{14,6},{1,9},{3,11}... | collective-permute-start | bytes 245768 | tf_op jit(solution)/shard_map/ppermute | solution.py:521
  11.0 0.0 collective-permute-done.2.refs_2_
  11.0 1.3 %collective-permute-start.9 = (bf16[40,8,128]{2,1,0:T(8,128)(2,1)S(1)}, bf16[40,8,128]{2,1,0:T(8,128)(2,1)S(1)}, u32[]{:S(2)}, u32[]{:S(2)}) collective-permute-start(bf16[40,8,128]{2,1,0:T(8,128)(2,1)S(1)} %get-tuple-element.27), channel_id=1, source_target_pairs={{0,10},{2,8},{4,14},{6,12},{8,2},{10,0},{12,6},{14,4},{1,11},{3,9}... | collective-permute-start | bytes 245768 | tf_op jit(solution)/shard_map/ppermute | solution.py:521
  12.3 0.0 collective-permute-done.3.refs_3_
  12.3 3.6 %collective-permute-start.10 = (bf16[40,8,128]{2,1,0:T(8,128)(2,1)S(1)}, bf16[40,8,128]{2,1,0:T(8,128)(2,1)S(1)}, u32[]{:S(2)}, u32[]{:S(2)}) collective-permute-start(bf16[40,8,128]{2,1,0:T(8,128)(2,1)S(1)} %get-tuple-element.28), channel_id=1, source_target_pairs={{0,12},{2,14},{4,8},{6,10},{8,4},{10,6},{12,0},{14,2},{1,13},{3,15... | collective-permute-start | bytes 245768 | tf_op jit(solution)/shard_map/ppermute | solution.py:521
  15.9 0.0 collective-permute-done.4.refs_4_
  15.9 0.0 copy-start.2
  15.9 1.4 %collective-permute-start.11 = (bf16[40,8,128]{2,1,0:T(8,128)(2,1)S(1)}, bf16[40,8,128]{2,1,0:T(8,128)(2,1)S(1)}, u32[]{:S(2)}, u32[]{:S(2)}) collective-permute-start(bf16[40,8,128]{2,1,0:T(8,128)(2,1)S(1)} %get-tuple-element.29), channel_id=1, source_target_pairs={{0,14},{2,12},{4,10},{6,8},{8,6},{10,4},{12,2},{14,0},{1,15},{3,13... | collective-permute-start | bytes 245768 | tf_op jit(solution)/shard_map/ppermute | solution.py:521
  17.4 0.0 collective-permute-done.8.refs_0_
  17.4 0.0 collective-permute-start.5
  17.4 7.0 %collective-permute-done.9.refs_1_ = bf16[40,8,128]{2,1,0:T(8,128)(2,1)S(1)} collective-permute-done((bf16[40,8,128]{2,1,0:T(8,128)(2,1)S(1)}, bf16[40,8,128]{2,1,0:T(8,128)(2,1)S(1)}, u32[]{:S(2)}, u32[]{:S(2)}) %collective-permute-start.9) | collective-permute-done | bytes 81952 | tf_op jit(solution)/shard_map/ppermute | solution.py:521
  24.4 0.0 collective-permute-start.6
  24.4 0.0 collective-permute-done.10.refs_2_
  24.4 0.5 collective-permute-start.7
  24.9 0.0 collective-permute-done.11.refs_3_
  24.9 0.1 collective-permute-start.12
  25.0 0.0 collective-permute-done.5.refs_5_
  25.0 0.4 collective-permute-start.13
  25.4 0.2 collective-permute-done.6.refs_6_
  25.6 0.2 collective-permute-start.14
  25.8 0.0 collective-permute-done.7.refs_7_
  25.8 0.4 collective-permute-start.15
  26.2 0.0 collective-permute-done.12.refs_4_
  26.2 0.2 collective-permute-start.17
  26.3 1.2 %stage.1.table = bf16[512,1024]{1,0:T(8,128)(2,1)S(1)} custom-call(bf16[512,1024]{1,0:T(8,128)(2,1)} %constant.12.clone.far), custom_call_target="tpu_custom_call" | custom-call | tf_op jit(solution)/shard_map/stage/pallas_call | solution.py:537
  27.6 1.5 %first.1 = (f32[3,16,16,512]{3,2,1,0:T(8,128)S(1)}, f32[128,1024]{1,0:T(8,128)S(1)}) custom-call(bf16[512,1024]{1,0:T(8,128)(2,1)S(1)} %stage.1.table, bf16[40,8,128]{2,1,0:T(8,128)(2,1)S(1)} %get-tuple-element.20.refs_0_, bf16[40,8,128]{2,1,0:T(8,128)(2,1)S(1)} %collective-permute-done.1.refs_1_, bf16[40,8,128]{2,1,0:T(8,128)(2,1)S(1)} %collective-permute-done.2.refs_2_, ...), custom_call_target="tpu_custom_call" | custom-call | tf_op jit(solution)/shard_map/first/pallas_call | solution.py:547
  29.1 0.0 copy-done.4
  29.1 0.0 collective-permute-done.13.refs_5_
  29.1 0.0 collective-permute-done.14.refs_6_
  29.1 0.0 collective-permute-done.15.refs_7_
  29.1 0.0 copy-done.2
  29.1 0.0 copy-start
  29.2 0.0 copy-start.3
  29.2 5.3 %bins.1 = bf16[8,14,8,128]{3,2,1,0:T(8,128)(2,1)S(1)} custom-call(s32[1]{0:T(128)} %bitcast.2.index, f32[64]{0:T(128)} %noise_far.1, f32[64]{0:T(128)} %copy-done.4, bf16[512,1024]{1,0:T(8,128)(2,1)S(1)} %stage.1.table, f32[1,512]{1,0:T(1,128)S(1)} %copy-done.2, f32[3,16,16,512]{3,2,1,0:T(8,128)S(1)} %get-tuple-element.24.kern_first, ...), custom_call_target="tpu_custom_call" | custom-call | tf_op jit(solution)/shard_map/bins/pallas_call | solution.py:560
  34.5 0.0 collective-permute-done.17
  34.5 0.0 collective-permute-done.16.basis_other
  34.5 15.0 %all_to_all.10.parts = bf16[8,14,8,128]{3,2,1,0:T(8,128)(2,1)S(1)} all-to-all(bf16[8,14,8,128]{3,2,1,0:T(8,128)(2,1)S(1)} %bins.1), channel_id=1, replica_groups=mesh['grp'=2,'pts'=8,'sen'=2] {'pts'}, dimensions={0} | all-to-all | bytes 458752 | tf_op jit(solution)/shard_map/all_to_all | solution.py:492
  49.5 0.0 copy-done
  49.5 0.0 copy-done.3
  49.5 0.0 copy-start.1
  49.5 0.6 %coeff.1 = (f32[8,1680]{1,0:T(8,128)S(1)}, bf16[8,8,1024]{2,1,0:T(8,128)(2,1)S(1)}) custom-call(f32[1,4]{1,0:T(1,128)S(1)} %bitcast.8, bf16[8,14,8,128]{3,2,1,0:T(8,128)(2,1)S(1)} %all_to_all.10.parts, bf16[1680,512]{1,0:T(8,128)(2,1)S(1)} %copy-done, bf16[1680,512]{1,0:T(8,128)(2,1)S(1)} %collective-permute-done.16.basis_other), custom_call_target="tpu_custom_call" | custom-call | tf_op jit(solution)/shard_map/coeff/pallas_call | solution.py:586
  50.1 10.5 %all_to_all.11.parts_own = bf16[8,8,1024]{2,1,0:T(8,128)(2,1)S(1)} all-to-all(bf16[8,8,1024]{2,1,0:T(8,128)(2,1)S(1)} %get-tuple-element.32), channel_id=1, replica_groups=mesh['grp'=2,'pts'=8,'sen'=2] {'pts'}, dimensions={0} | all-to-all | bytes 262144 | tf_op jit(solution)/shard_map/all_to_all | solution.py:492
  60.6 0.0 collective-permute-start.18
  60.6 0.5 collective-permute-start.19
  61.1 0.9 %collective-permute-done.19.flat_other = f32[8,1680]{1,0:T(8,128)S(1)} collective-permute-done((f32[8,1680]{1,0:T(8,128)S(1)}, f32[8,1680]{1,0:T(8,128)S(1)}, u32[]{:S(2)}, u32[]{:S(2)}) %collective-permute-start.19) | collective-permute-done | bytes 53792 | tf_op jit(solution)/shard_map/ppermute | solution.py:489
  62.0 0.0 collective-permute-done.18.parts_other
  62.1 0.0 copy-done.1
  62.1 1.8 %deflate.1 = f32[16,4,420]{2,1,0:T(4,128)} custom-call(s32[1]{0:T(128)} %bitcast.core, bf16[8,8,1024]{2,1,0:T(8,128)(2,1)S(1)} %all_to_all.11.parts_own, bf16[8,8,1024]{2,1,0:T(8,128)(2,1)S(1)} %collective-permute-done.18.parts_other, f32[1,512]{1,0:T(1,128)S(1)} %bitcast.6, f32[1,512]{1,0:T(1,128)S(1)} %bitcast.7, ...), custom_call_target="tpu_custom_call" | custom-call | tf_op jit(solution)/shard_map/deflate/pallas_call | solution.py:600
Async XLA Ops:
  0.0 34.5 %collective-permute-start.16 = (bf16[1680,512]{1,0:T(8,128)(2,1)}, bf16[1680,512]{1,0:T(8,128)(2,1)S(1)}, u32[]{:S(2)}, u32[]{:S(2)}) collective-permute-start(bf16[1680,512]{1,0:T(8,128)(2,1)} %basis_own.3), channel_id=1, source_target_pairs={{0,1},{1,0},{2,3},{3,2},{4,5},{5,4},{6,7},{7,6},{8,9},{9,8},{10,11... | collective-permute-start | bytes 5160968 | tf_op jit(solution)/shard_map/ppermute | solution.py:489
  2.4 5.7 %collective-permute-start.1 = (bf16[40,8,128]{2,1,0:T(8,128)(2,1)S(1)}, bf16[40,8,128]{2,1,0:T(8,128)(2,1)S(1)}, u32[]{:S(2)}, u32[]{:S(2)}) collective-permute-start(bf16[40,8,128]{2,1,0:T(8,128)(2,1)S(1)} %get-tuple-element.21), channel_id=1, source_target_pairs={{0,2},{2,0},{4,6},{6,4},{8,10},{10,8},{12,14},{14,12},{1,3},{3,1},... | collective-permute-start | bytes 245768 | tf_op jit(solution)/shard_map/ppermute | solution.py:521
  5.0 6.1 %collective-permute-start.2 = (bf16[40,8,128]{2,1,0:T(8,128)(2,1)S(1)}, bf16[40,8,128]{2,1,0:T(8,128)(2,1)S(1)}, u32[]{:S(2)}, u32[]{:S(2)}) collective-permute-start(bf16[40,8,128]{2,1,0:T(8,128)(2,1)S(1)} %get-tuple-element.22), channel_id=1, source_target_pairs={{0,4},{2,6},{4,0},{6,2},{8,12},{10,14},{12,8},{14,10},{1,5},{3,7},... | collective-permute-start | bytes 245768 | tf_op jit(solution)/shard_map/ppermute | solution.py:521
  6.5 5.8 %collective-permute-start.3 = (bf16[40,8,128]{2,1,0:T(8,128)(2,1)S(1)}, bf16[40,8,128]{2,1,0:T(8,128)(2,1)S(1)}, u32[]{:S(2)}, u32[]{:S(2)}) collective-permute-start(bf16[40,8,128]{2,1,0:T(8,128)(2,1)S(1)} %get-tuple-element.23), channel_id=1, source_target_pairs={{0,6},{2,4},{4,2},{6,0},{8,14},{10,12},{12,10},{14,8},{1,7},{3,5},... | collective-permute-start | bytes 245768 | tf_op jit(solution)/shard_map/ppermute | solution.py:521
  6.6 1.3 %collective-permute-start = (f32[64]{0:T(128)}, f32[64]{0:T(128)S(1)}, u32[]{:S(2)}, u32[]{:S(2)}) collective-permute-start(f32[64]{0:T(128)} %noise_far.1), channel_id=1, source_target_pairs={{0,1},{1,0},{2,3},{3,2},{4,5},{5,4},{6,7},{7,6},{8,9},{9,8},{10,11... | collective-permute-start | bytes 776 | tf_op jit(solution)/shard_map/ppermute | solution.py:489
  7.8 21.2 %copy-start.4 = (f32[64]{0:T(128)}, f32[64]{0:T(128)S(1)}, u32[]{:S(2)}) copy-start(f32[64]{0:T(128)S(1)} %collective-permute-done.noise_other_far) | copy-start | bytes 772
  7.9 8.1 %collective-permute-start.4 = (bf16[40,8,128]{2,1,0:T(8,128)(2,1)S(1)}, bf16[40,8,128]{2,1,0:T(8,128)(2,1)S(1)}, u32[]{:S(2)}, u32[]{:S(2)}) collective-permute-start(bf16[40,8,128]{2,1,0:T(8,128)(2,1)S(1)} %get-tuple-element.20.refs_0_), channel_id=1, source_target_pairs={{0,1},{1,0},{2,3},{3,2},{4,5},{5,4},{6,7},{7,6},{8,9},{9,8},{10,11... | collective-permute-start | bytes 245768 | tf_op jit(solution)/shard_map/ppermute | solution.py:489
  8.1 9.3 %collective-permute-start.8 = (bf16[40,8,128]{2,1,0:T(8,128)(2,1)S(1)}, bf16[40,8,128]{2,1,0:T(8,128)(2,1)S(1)}, u32[]{:S(2)}, u32[]{:S(2)}) collective-permute-start(bf16[40,8,128]{2,1,0:T(8,128)(2,1)S(1)} %get-tuple-element.26), channel_id=1, source_target_pairs={{0,8},{2,10},{4,12},{6,14},{8,0},{10,2},{12,4},{14,6},{1,9},{3,11}... | collective-permute-start | bytes 245768 | tf_op jit(solution)/shard_map/ppermute | solution.py:521
  11.0 13.3 %collective-permute-start.9 = (bf16[40,8,128]{2,1,0:T(8,128)(2,1)S(1)}, bf16[40,8,128]{2,1,0:T(8,128)(2,1)S(1)}, u32[]{:S(2)}, u32[]{:S(2)}) collective-permute-start(bf16[40,8,128]{2,1,0:T(8,128)(2,1)S(1)} %get-tuple-element.27), channel_id=1, source_target_pairs={{0,10},{2,8},{4,14},{6,12},{8,2},{10,0},{12,6},{14,4},{1,11},{3,9}... | collective-permute-start | bytes 245768 | tf_op jit(solution)/shard_map/ppermute | solution.py:521
  12.3 12.1 %collective-permute-start.10 = (bf16[40,8,128]{2,1,0:T(8,128)(2,1)S(1)}, bf16[40,8,128]{2,1,0:T(8,128)(2,1)S(1)}, u32[]{:S(2)}, u32[]{:S(2)}) collective-permute-start(bf16[40,8,128]{2,1,0:T(8,128)(2,1)S(1)} %get-tuple-element.28), channel_id=1, source_target_pairs={{0,12},{2,14},{4,8},{6,10},{8,4},{10,6},{12,0},{14,2},{1,13},{3,15... | collective-permute-start | bytes 245768 | tf_op jit(solution)/shard_map/ppermute | solution.py:521
  15.9 13.2 %copy-start.2 = (f32[1,512]{1,0:T(1,128)S(1)}, f32[1,512]{1,0:T(1,128)}, u32[]{:S(2)}) copy-start(f32[1,512]{1,0:T(1,128)} %constant.13.clone.weights) | copy-start | bytes 6148
  15.9 9.0 %collective-permute-start.11 = (bf16[40,8,128]{2,1,0:T(8,128)(2,1)S(1)}, bf16[40,8,128]{2,1,0:T(8,128)(2,1)S(1)}, u32[]{:S(2)}, u32[]{:S(2)}) collective-permute-start(bf16[40,8,128]{2,1,0:T(8,128)(2,1)S(1)} %get-tuple-element.29), channel_id=1, source_target_pairs={{0,14},{2,12},{4,10},{6,8},{8,6},{10,4},{12,2},{14,0},{1,15},{3,13... | collective-permute-start | bytes 245768 | tf_op jit(solution)/shard_map/ppermute | solution.py:521
  17.4 7.6 %collective-permute-start.5 = (bf16[40,8,128]{2,1,0:T(8,128)(2,1)S(1)}, bf16[40,8,128]{2,1,0:T(8,128)(2,1)S(1)}, u32[]{:S(2)}, u32[]{:S(2)}) collective-permute-start(bf16[40,8,128]{2,1,0:T(8,128)(2,1)S(1)} %collective-permute-done.1.refs_1_), channel_id=1, source_target_pairs={{0,1},{1,0},{2,3},{3,2},{4,5},{5,4},{6,7},{7,6},{8,9},{9,8},{10,11... | collective-permute-start | bytes 245768 | tf_op jit(solution)/shard_map/ppermute | solution.py:489
  24.4 1.3 %collective-permute-start.6 = (bf16[40,8,128]{2,1,0:T(8,128)(2,1)S(1)}, bf16[40,8,128]{2,1,0:T(8,128)(2,1)S(1)}, u32[]{:S(2)}, u32[]{:S(2)}) collective-permute-start(bf16[40,8,128]{2,1,0:T(8,128)(2,1)S(1)} %collective-permute-done.2.refs_2_), channel_id=1, source_target_pairs={{0,1},{1,0},{2,3},{3,2},{4,5},{5,4},{6,7},{7,6},{8,9},{9,8},{10,11... | collective-permute-start | bytes 245768 | tf_op jit(solution)/shard_map/ppermute | solution.py:489
  24.4 1.4 %collective-permute-start.7 = (bf16[40,8,128]{2,1,0:T(8,128)(2,1)S(1)}, bf16[40,8,128]{2,1,0:T(8,128)(2,1)S(1)}, u32[]{:S(2)}, u32[]{:S(2)}) collective-permute-start(bf16[40,8,128]{2,1,0:T(8,128)(2,1)S(1)} %collective-permute-done.3.refs_3_), channel_id=1, source_target_pairs={{0,1},{1,0},{2,3},{3,2},{4,5},{5,4},{6,7},{7,6},{8,9},{9,8},{10,11... | collective-permute-start | bytes 245768 | tf_op jit(solution)/shard_map/ppermute | solution.py:489
  24.9 1.3 %collective-permute-start.12 = (bf16[40,8,128]{2,1,0:T(8,128)(2,1)S(1)}, bf16[40,8,128]{2,1,0:T(8,128)(2,1)S(1)}, u32[]{:S(2)}, u32[]{:S(2)}) collective-permute-start(bf16[40,8,128]{2,1,0:T(8,128)(2,1)S(1)} %collective-permute-done.8.refs_0_), channel_id=1, source_target_pairs={{0,1},{1,0},{2,3},{3,2},{4,5},{5,4},{6,7},{7,6},{8,9},{9,8},{10,11... | collective-permute-start | bytes 245768 | tf_op jit(solution)/shard_map/ppermute | solution.py:489
  25.0 4.2 %collective-permute-start.13 = (bf16[40,8,128]{2,1,0:T(8,128)(2,1)S(1)}, bf16[40,8,128]{2,1,0:T(8,128)(2,1)S(1)}, u32[]{:S(2)}, u32[]{:S(2)}) collective-permute-start(bf16[40,8,128]{2,1,0:T(8,128)(2,1)S(1)} %collective-permute-done.9.refs_1_), channel_id=1, source_target_pairs={{0,1},{1,0},{2,3},{3,2},{4,5},{5,4},{6,7},{7,6},{8,9},{9,8},{10,11... | collective-permute-start | bytes 245768 | tf_op jit(solution)/shard_map/ppermute | solution.py:489
  25.6 3.5 %collective-permute-start.14 = (bf16[40,8,128]{2,1,0:T(8,128)(2,1)S(1)}, bf16[40,8,128]{2,1,0:T(8,128)(2,1)S(1)}, u32[]{:S(2)}, u32[]{:S(2)}) collective-permute-start(bf16[40,8,128]{2,1,0:T(8,128)(2,1)S(1)} %collective-permute-done.10.refs_2_), channel_id=1, source_target_pairs={{0,1},{1,0},{2,3},{3,2},{4,5},{5,4},{6,7},{7,6},{8,9},{9,8},{10,11... | collective-permute-start | bytes 245768 | tf_op jit(solution)/shard_map/ppermute | solution.py:489
  25.8 3.3 %collective-permute-start.15 = (bf16[40,8,128]{2,1,0:T(8,128)(2,1)S(1)}, bf16[40,8,128]{2,1,0:T(8,128)(2,1)S(1)}, u32[]{:S(2)}, u32[]{:S(2)}) collective-permute-start(bf16[40,8,128]{2,1,0:T(8,128)(2,1)S(1)} %collective-permute-done.11.refs_3_), channel_id=1, source_target_pairs={{0,1},{1,0},{2,3},{3,2},{4,5},{5,4},{6,7},{7,6},{8,9},{9,8},{10,11... | collective-permute-start | bytes 245768 | tf_op jit(solution)/shard_map/ppermute | solution.py:489
  26.2 8.3 %collective-permute-start.17 = (f32[512]{0:T(512)}, f32[512]{0:T(512)S(1)}, u32[]{:S(2)}, u32[]{:S(2)}) collective-permute-start(f32[512]{0:T(512)} %param.13), channel_id=1, source_target_pairs={{0,1},{1,0},{2,3},{3,2},{4,5},{5,4},{6,7},{7,6},{8,9},{9,8},{10,11... | collective-permute-start | bytes 6152 | tf_op jit(solution)/shard_map/ppermute | solution.py:489
  29.1 20.3 %copy-start = (bf16[1680,512]{1,0:T(8,128)(2,1)S(1)}, bf16[1680,512]{1,0:T(8,128)(2,1)}, u32[]{:S(2)}) copy-start(bf16[1680,512]{1,0:T(8,128)(2,1)} %basis_own.3) | copy-start | bytes 5160964
  29.2 20.3 %copy-start.3 = (f32[4]{0:T(128)S(1)}, f32[4]{0:T(128)}, u32[]{:S(2)}) copy-start(f32[4]{0:T(128)} %prior_far.1) | copy-start | bytes 52
  49.5 12.6 %copy-start.1 = (f32[512]{0:T(512)S(1)}, f32[512]{0:T(512)}, u32[]{:S(2)}) copy-start(f32[512]{0:T(512)} %param.13) | copy-start | bytes 6148
  60.6 1.4 %collective-permute-start.18 = (bf16[8,8,1024]{2,1,0:T(8,128)(2,1)S(1)}, bf16[8,8,1024]{2,1,0:T(8,128)(2,1)S(1)}, u32[]{:S(2)}, u32[]{:S(2)}) collective-permute-start(bf16[8,8,1024]{2,1,0:T(8,128)(2,1)S(1)} %all_to_all.11.parts_own), channel_id=1, source_target_pairs={{0,1},{1,0},{2,3},{3,2},{4,5},{5,4},{6,7},{7,6},{8,9},{9,8},{10,11... | collective-permute-start | bytes 393224 | tf_op jit(solution)/shard_map/ppermute | solution.py:489
  60.6 1.4 %collective-permute-start.19 = (f32[8,1680]{1,0:T(8,128)S(1)}, f32[8,1680]{1,0:T(8,128)S(1)}, u32[]{:S(2)}, u32[]{:S(2)}) collective-permute-start(f32[8,1680]{1,0:T(8,128)S(1)} %get-tuple-element.34.flat_own), channel_id=1, source_target_pairs={{0,1},{1,0},{2,3},{3,2},{4,5},{5,4},{6,7},{7,6},{8,9},{9,8},{10,11... | collective-permute-start | bytes 161288 | tf_op jit(solution)/shard_map/ppermute | solution.py:489

commit v6 on v5

--- a/solution.py
+++ b/solution.py
@@ -446,7 +446,9 @@
 
 
 def split_order(width):
-    return list(range(width // 2)), list(range(width // 2, width))
+    near = list(range(2, width // 2))
+    far = list(range(width // 2, width))
+    return [0, far[0]] + near, far[1:] + [1]
 
 
 def stage_kernel(far, near, sem):
@@ -560,7 +562,7 @@
     back = pl.pallas_call(
         functools.partial(bins_kernel, orders=orders, packing_back=packing_back, **sizes),
         out_shape=jax.ShapeDtypeStruct((width, packing_back.tiles, half, LANES), bf16),
-        in_specs=in_smem(1) + [in_hbm] * 2 + in_vmem(4 + 2 * count),
+        in_specs=in_smem(1) + [in_hbm] + in_vmem(5 + 2 * count),
         out_specs=in_vmem(1)[0],
         scratch_shapes=[pltpu.VMEM((3, count * points, 2 * sens, wide), f32)]
         + scratch(count)
@@ -575,7 +577,7 @@
         compiler_params=limit(20),
         name="bins",
     )(
-        me, *kept(pltpu.HBM, noise_weight, noise_other), table, weights, kern_first, data_first,
+        me, *kept(pltpu.HBM, noise_weight), noise_other, table, weights, kern_first, data_first,
         *ready(orders[1]),
     )
     back, basis_other, deflation_other = lax.optimization_barrier(

time: 64.1 us -> 62.6 us (0.977)
  waiting for transfers between devices: 9.57 us -> 7.84 us
  starting transfers between devices: 16.2 us -> 17.3 us
  blocking collectives: 25.5 us -> 24.7 us
    ppermute x7, waiting for transfers between devices: 7.08 us -> 5.35 us  [local_split(): lax.ppermute(value, 'pts', [(i, i ^ relative) for i in range(width)])]
    all_to_all x2, blocking collectives: 25.5 us -> 24.7 us  [exchange(): lax.all_to_all(value, 'pts', split_axis=0, concat_axis=0, tiled=False)]
    ppermute x7, starting transfers between devices: 13.4 us -> 14 us  [local_split(): lax.ppermute(value, 'pts', [(i, i ^ relative) for i in range(width)])]
where the time goes in v6:
time: 62.6 us; the launch traced here: 62.4 us
  blocking collectives  24.7 us (39%)
  starting transfers between devices  17.3 us (28%)
  Pallas kernels  12.3 us (20%)
  waiting for transfers between devices  7.84 us (13%)
    all_to_all x2, blocking collectives, exchange(): lax.all_to_all(value, 'pts', split_axis=0, concat_axis=0, tiled=False)  24.7 us
    ppermute x7, starting transfers between devices, local_split(): lax.ppermute(value, 'pts', [(i, i ^ relative) for i in range(width)])  14 us
    ppermute x7, waiting for transfers between devices, local_split(): lax.ppermute(value, 'pts', [(i, i ^ relative) for i in range(width)])  5.35 us
    pallas_call x1, Pallas kernels, local_split(): pl.pallas_call(functools.partial(bins_kernel, orders=orders, packing_back...  5.27 us
    ppermute x13, starting transfers between devices, swap(): return lax.ppermute(value, 'sen', [(0, 1), (1, 0)])  3.21 us
    ppermute x13, waiting for transfers between devices, swap(): return lax.ppermute(value, 'sen', [(0, 1), (1, 0)])  2.48 us
    pallas_call x1, Pallas kernels, local_split(): pl.pallas_call(functools.partial(pack_kernel, order=order, half=half, pac...  1.85 us
    pallas_call x1, Pallas kernels, local_split(): pl.pallas_call(functools.partial(deflate_kernel, points=points, steps=ste...  1.77 us
  transfers between devices with their start and end apart: 20, of which 5 were waited for; matrix products, arithmetic and copies ran while one was open for 0% of the time, Pallas kernels for 16%

profile of v6, /device:TPU:0, one launch (start us, length us, event | category | flops | bytes accessed | tf_op | source)
XLA Modules:
  0.0 62.4 jit_solution(10557222644613188950)
XLA Ops:
  0.0 0.5 collective-permute-start.16
  0.5 0.1 pad_add_fusion.index
  0.6 1.9 %pack.1 = (bf16[40,8,128]{2,1,0:T(8,128)(2,1)S(1)}, bf16[40,8,128]{2,1,0:T(8,128)(2,1)S(1)}, bf16[40,8,128]{2,1,0:T(8,128)(2,1)S(1)}, bf16[40,8,128]{2,1,0:T(8,1...) custom-call(s32[2]{0:T(128)S(1)} %pad_add_fusion.index, ...), custom_call_target="tpu_custom_call" | custom-call | tf_op jit(solution)/shard_map/pack/pallas_call | solution.py:505
  2.4 3.6 %collective-permute-start.1 = (bf16[40,8,128]{2,1,0:T(8,128)(2,1)S(1)}, bf16[40,8,128]{2,1,0:T(8,128)(2,1)S(1)}, u32[]{:S(2)}, u32[]{:S(2)}) collective-permute-start(bf16[40,8,128]{2,1,0:T(8,128)(2,1)S(1)} %get-tuple-element.21), channel_id=1, source_target_pairs={{0,8},{2,10},{4,12},{6,14},{8,0},{10,2},{12,4},{14,6},{1,9},{3,11}... | collective-permute-start | bytes 245768 | tf_op jit(solution)/shard_map/ppermute | solution.py:523
  6.1 1.6 %collective-permute-start.2 = (bf16[40,8,128]{2,1,0:T(8,128)(2,1)S(1)}, bf16[40,8,128]{2,1,0:T(8,128)(2,1)S(1)}, u32[]{:S(2)}, u32[]{:S(2)}) collective-permute-start(bf16[40,8,128]{2,1,0:T(8,128)(2,1)S(1)} %get-tuple-element.22), channel_id=1, source_target_pairs={{0,4},{2,6},{4,0},{6,2},{8,12},{10,14},{12,8},{14,10},{1,5},{3,7},... | collective-permute-start | bytes 245768 | tf_op jit(solution)/shard_map/ppermute | solution.py:523
  7.6 1.4 %collective-permute-start.3 = (bf16[40,8,128]{2,1,0:T(8,128)(2,1)S(1)}, bf16[40,8,128]{2,1,0:T(8,128)(2,1)S(1)}, u32[]{:S(2)}, u32[]{:S(2)}) collective-permute-start(bf16[40,8,128]{2,1,0:T(8,128)(2,1)S(1)} %get-tuple-element.23), channel_id=1, source_target_pairs={{0,6},{2,4},{4,2},{6,0},{8,14},{10,12},{12,10},{14,8},{1,7},{3,5},... | collective-permute-start | bytes 245768 | tf_op jit(solution)/shard_map/ppermute | solution.py:523
  9.0 0.0 collective-permute-start
  9.0 1.3 %collective-permute-done.noise_other_far = f32[64]{0:T(128)S(1)} collective-permute-done((f32[64]{0:T(128)}, f32[64]{0:T(128)S(1)}, u32[]{:S(2)}, u32[]{:S(2)}) %collective-permute-start) | collective-permute-done | bytes 288 | tf_op jit(solution)/shard_map/ppermute | solution.py:491
  10.3 0.2 collective-permute-start.4
  10.5 0.6 collective-permute-done.1.refs_1_
  11.0 2.2 %collective-permute-start.8 = (bf16[40,8,128]{2,1,0:T(8,128)(2,1)S(1)}, bf16[40,8,128]{2,1,0:T(8,128)(2,1)S(1)}, u32[]{:S(2)}, u32[]{:S(2)}) collective-permute-start(bf16[40,8,128]{2,1,0:T(8,128)(2,1)S(1)} %get-tuple-element.26), channel_id=1, source_target_pairs={{0,10},{2,8},{4,14},{6,12},{8,2},{10,0},{12,6},{14,4},{1,11},{3,9}... | collective-permute-start | bytes 245768 | tf_op jit(solution)/shard_map/ppermute | solution.py:523
  13.2 0.0 collective-permute-done.2.refs_2_
  13.2 1.8 %collective-permute-start.9 = (bf16[40,8,128]{2,1,0:T(8,128)(2,1)S(1)}, bf16[40,8,128]{2,1,0:T(8,128)(2,1)S(1)}, u32[]{:S(2)}, u32[]{:S(2)}) collective-permute-start(bf16[40,8,128]{2,1,0:T(8,128)(2,1)S(1)} %get-tuple-element.27), channel_id=1, source_target_pairs={{0,12},{2,14},{4,8},{6,10},{8,4},{10,6},{12,0},{14,2},{1,13},{3,15... | collective-permute-start | bytes 245768 | tf_op jit(solution)/shard_map/ppermute | solution.py:523
  15.0 0.0 collective-permute-done.3.refs_3_
  15.0 2.0 %collective-permute-start.10 = (bf16[40,8,128]{2,1,0:T(8,128)(2,1)S(1)}, bf16[40,8,128]{2,1,0:T(8,128)(2,1)S(1)}, u32[]{:S(2)}, u32[]{:S(2)}) collective-permute-start(bf16[40,8,128]{2,1,0:T(8,128)(2,1)S(1)} %get-tuple-element.28), channel_id=1, source_target_pairs={{0,14},{2,12},{4,10},{6,8},{8,6},{10,4},{12,2},{14,0},{1,15},{3,13... | collective-permute-start | bytes 245768 | tf_op jit(solution)/shard_map/ppermute | solution.py:523
  17.0 0.0 collective-permute-done.4.refs_4_
  17.0 0.0 copy-start.2
  17.0 1.5 %collective-permute-start.11 = (bf16[40,8,128]{2,1,0:T(8,128)(2,1)S(1)}, bf16[40,8,128]{2,1,0:T(8,128)(2,1)S(1)}, u32[]{:S(2)}, u32[]{:S(2)}) collective-permute-start(bf16[40,8,128]{2,1,0:T(8,128)(2,1)S(1)} %get-tuple-element.29), channel_id=1, source_target_pairs={{0,2},{2,0},{4,6},{6,4},{8,10},{10,8},{12,14},{14,12},{1,3},{3,1},... | collective-permute-start | bytes 245768 | tf_op jit(solution)/shard_map/ppermute | solution.py:523
  18.5 4.8 %collective-permute-done.8.refs_0_ = bf16[40,8,128]{2,1,0:T(8,128)(2,1)S(1)} collective-permute-done((bf16[40,8,128]{2,1,0:T(8,128)(2,1)S(1)}, bf16[40,8,128]{2,1,0:T(8,128)(2,1)S(1)}, u32[]{:S(2)}, u32[]{:S(2)}) %collective-permute-start.8) | collective-permute-done | bytes 81952 | tf_op jit(solution)/shard_map/ppermute | solution.py:523
  23.3 0.0 collective-permute-start.5
  23.3 0.0 collective-permute-done.9.refs_1_
  23.3 0.5 collective-permute-start.6
  23.8 0.0 collective-permute-done.10.refs_2_
  23.8 0.1 collective-permute-start.7
  23.9 0.0 collective-permute-done.11.refs_3_
  23.9 0.4 collective-permute-start.12
  24.3 0.2 collective-permute-done.5.refs_5_
  24.6 0.2 collective-permute-start.13
  24.7 0.0 collective-permute-done.6.refs_6_
  24.7 0.4 collective-permute-start.14
  25.1 0.0 collective-permute-done.7.refs_7_
  25.1 0.2 collective-permute-start.15
  25.3 0.0 collective-permute-done.12.refs_4_
  25.3 0.4 collective-permute-start.17
  25.6 1.2 %stage.1.table = bf16[512,1024]{1,0:T(8,128)(2,1)S(1)} custom-call(bf16[512,1024]{1,0:T(8,128)(2,1)} %constant.12.clone.far), custom_call_target="tpu_custom_call" | custom-call | tf_op jit(solution)/shard_map/stage/pallas_call | solution.py:539
  26.9 1.5 %first.1 = (f32[3,16,16,512]{3,2,1,0:T(8,128)S(1)}, f32[128,1024]{1,0:T(8,128)S(1)}) custom-call(bf16[512,1024]{1,0:T(8,128)(2,1)S(1)} %stage.1.table, bf16[40,8,128]{2,1,0:T(8,128)(2,1)S(1)} %get-tuple-element.20.refs_0_, bf16[40,8,128]{2,1,0:T(8,128)(2,1)S(1)} %collective-permute-done.1.refs_1_, bf16[40,8,128]{2,1,0:T(8,128)(2,1)S(1)} %collective-permute-done.2.refs_2_, ...), custom_call_target="tpu_custom_call" | custom-call | tf_op jit(solution)/shard_map/first/pallas_call | solution.py:549
  28.4 0.0 collective-permute-done.13.refs_5_
  28.4 0.0 collective-permute-done.14.refs_6_
  28.4 0.0 collective-permute-done.15.refs_7_
  28.4 0.0 copy-done.2
  28.4 0.0 copy-start
  28.4 0.0 copy-start.3
  28.5 5.3 %bins.1 = bf16[8,14,8,128]{3,2,1,0:T(8,128)(2,1)S(1)} custom-call(s32[1]{0:T(128)} %bitcast.2.index, f32[64]{0:T(128)} %noise_far.1, f32[64]{0:T(128)S(1)} %collective-permute-done.noise_other_far, bf16[512,1024]{1,0:T(8,128)(2,1)S(1)} %stage.1.table, f32[1,512]{1,0:T(1,128)S(1)} %copy-done.2, f32[3,16,16,512]{3,2,1,0:T(8,128)S(1)} %get-tuple-element.24.kern_first, ...), custom_call_target="tpu_custom_call" | custom-call | tf_op jit(solution)/shard_map/bins/pallas_call | solution.py:562
  33.7 0.0 collective-permute-done.17
  33.8 0.0 collective-permute-done.16.basis_other
  33.8 14.2 %all_to_all.10.parts = bf16[8,14,8,128]{3,2,1,0:T(8,128)(2,1)S(1)} all-to-all(bf16[8,14,8,128]{3,2,1,0:T(8,128)(2,1)S(1)} %bins.1), channel_id=1, replica_groups=mesh['grp'=2,'pts'=8,'sen'=2] {'pts'}, dimensions={0} | all-to-all | bytes 458752 | tf_op jit(solution)/shard_map/all_to_all | solution.py:494
  48.0 0.0 copy-done
  48.0 0.0 copy-done.3
  48.0 0.0 copy-start.1
  48.0 0.6 %coeff.1 = (f32[8,1680]{1,0:T(8,128)S(1)}, bf16[8,8,1024]{2,1,0:T(8,128)(2,1)S(1)}) custom-call(f32[1,4]{1,0:T(1,128)S(1)} %bitcast.8, bf16[8,14,8,128]{3,2,1,0:T(8,128)(2,1)S(1)} %all_to_all.10.parts, bf16[1680,512]{1,0:T(8,128)(2,1)S(1)} %copy-done, bf16[1680,512]{1,0:T(8,128)(2,1)S(1)} %collective-permute-done.16.basis_other), custom_call_target="tpu_custom_call" | custom-call | tf_op jit(solution)/shard_map/coeff/pallas_call | solution.py:588
  48.7 10.5 %all_to_all.11.parts_own = bf16[8,8,1024]{2,1,0:T(8,128)(2,1)S(1)} all-to-all(bf16[8,8,1024]{2,1,0:T(8,128)(2,1)S(1)} %get-tuple-element.32), channel_id=1, replica_groups=mesh['grp'=2,'pts'=8,'sen'=2] {'pts'}, dimensions={0} | all-to-all | bytes 262144 | tf_op jit(solution)/shard_map/all_to_all | solution.py:494
  59.2 0.0 collective-permute-start.18
  59.2 0.5 collective-permute-start.19
  59.7 0.9 %collective-permute-done.19.flat_other = f32[8,1680]{1,0:T(8,128)S(1)} collective-permute-done((f32[8,1680]{1,0:T(8,128)S(1)}, f32[8,1680]{1,0:T(8,128)S(1)}, u32[]{:S(2)}, u32[]{:S(2)}) %collective-permute-start.19) | collective-permute-done | bytes 53792 | tf_op jit(solution)/shard_map/ppermute | solution.py:491
  60.6 0.0 collective-permute-done.18.parts_other
  60.6 0.0 copy-done.1
  60.6 1.8 %deflate.1 = f32[16,4,420]{2,1,0:T(4,128)} custom-call(s32[1]{0:T(128)} %bitcast.core, bf16[8,8,1024]{2,1,0:T(8,128)(2,1)S(1)} %all_to_all.11.parts_own, bf16[8,8,1024]{2,1,0:T(8,128)(2,1)S(1)} %collective-permute-done.18.parts_other, f32[1,512]{1,0:T(1,128)S(1)} %bitcast.6, f32[1,512]{1,0:T(1,128)S(1)} %bitcast.7, ...), custom_call_target="tpu_custom_call" | custom-call | tf_op jit(solution)/shard_map/deflate/pallas_call | solution.py:602
Async XLA Ops:
  0.0 33.8 %collective-permute-start.16 = (bf16[1680,512]{1,0:T(8,128)(2,1)}, bf16[1680,512]{1,0:T(8,128)(2,1)S(1)}, u32[]{:S(2)}, u32[]{:S(2)}) collective-permute-start(bf16[1680,512]{1,0:T(8,128)(2,1)} %basis_own.3), channel_id=1, source_target_pairs={{0,1},{1,0},{2,3},{3,2},{4,5},{5,4},{6,7},{7,6},{8,9},{9,8},{10,11... | collective-permute-start | bytes 5160968 | tf_op jit(solution)/shard_map/ppermute | solution.py:491
  2.4 8.6 %collective-permute-start.1 = (bf16[40,8,128]{2,1,0:T(8,128)(2,1)S(1)}, bf16[40,8,128]{2,1,0:T(8,128)(2,1)S(1)}, u32[]{:S(2)}, u32[]{:S(2)}) collective-permute-start(bf16[40,8,128]{2,1,0:T(8,128)(2,1)S(1)} %get-tuple-element.21), channel_id=1, source_target_pairs={{0,8},{2,10},{4,12},{6,14},{8,0},{10,2},{12,4},{14,6},{1,9},{3,11}... | collective-permute-start | bytes 245768 | tf_op jit(solution)/shard_map/ppermute | solution.py:523
  6.1 7.1 %collective-permute-start.2 = (bf16[40,8,128]{2,1,0:T(8,128)(2,1)S(1)}, bf16[40,8,128]{2,1,0:T(8,128)(2,1)S(1)}, u32[]{:S(2)}, u32[]{:S(2)}) collective-permute-start(bf16[40,8,128]{2,1,0:T(8,128)(2,1)S(1)} %get-tuple-element.22), channel_id=1, source_target_pairs={{0,4},{2,6},{4,0},{6,2},{8,12},{10,14},{12,8},{14,10},{1,5},{3,7},... | collective-permute-start | bytes 245768 | tf_op jit(solution)/shard_map/ppermute | solution.py:523
  7.6 7.4 %collective-permute-start.3 = (bf16[40,8,128]{2,1,0:T(8,128)(2,1)S(1)}, bf16[40,8,128]{2,1,0:T(8,128)(2,1)S(1)}, u32[]{:S(2)}, u32[]{:S(2)}) collective-permute-start(bf16[40,8,128]{2,1,0:T(8,128)(2,1)S(1)} %get-tuple-element.23), channel_id=1, source_target_pairs={{0,6},{2,4},{4,2},{6,0},{8,14},{10,12},{12,10},{14,8},{1,7},{3,5},... | collective-permute-start | bytes 245768 | tf_op jit(solution)/shard_map/ppermute | solution.py:523
  9.0 1.3 %collective-permute-start = (f32[64]{0:T(128)}, f32[64]{0:T(128)S(1)}, u32[]{:S(2)}, u32[]{:S(2)}) collective-permute-start(f32[64]{0:T(128)} %noise_far.1), channel_id=1, source_target_pairs={{0,1},{1,0},{2,3},{3,2},{4,5},{5,4},{6,7},{7,6},{8,9},{9,8},{10,11... | collective-permute-start | bytes 776 | tf_op jit(solution)/shard_map/ppermute | solution.py:491
  10.3 6.7 %collective-permute-start.4 = (bf16[40,8,128]{2,1,0:T(8,128)(2,1)S(1)}, bf16[40,8,128]{2,1,0:T(8,128)(2,1)S(1)}, u32[]{:S(2)}, u32[]{:S(2)}) collective-permute-start(bf16[40,8,128]{2,1,0:T(8,128)(2,1)S(1)} %get-tuple-element.20.refs_0_), channel_id=1, source_target_pairs={{0,1},{1,0},{2,3},{3,2},{4,5},{5,4},{6,7},{7,6},{8,9},{9,8},{10,11... | collective-permute-start | bytes 245768 | tf_op jit(solution)/shard_map/ppermute | solution.py:491
  11.0 12.3 %collective-permute-start.8 = (bf16[40,8,128]{2,1,0:T(8,128)(2,1)S(1)}, bf16[40,8,128]{2,1,0:T(8,128)(2,1)S(1)}, u32[]{:S(2)}, u32[]{:S(2)}) collective-permute-start(bf16[40,8,128]{2,1,0:T(8,128)(2,1)S(1)} %get-tuple-element.26), channel_id=1, source_target_pairs={{0,10},{2,8},{4,14},{6,12},{8,2},{10,0},{12,6},{14,4},{1,11},{3,9}... | collective-permute-start | bytes 245768 | tf_op jit(solution)/shard_map/ppermute | solution.py:523
  13.2 10.1 %collective-permute-start.9 = (bf16[40,8,128]{2,1,0:T(8,128)(2,1)S(1)}, bf16[40,8,128]{2,1,0:T(8,128)(2,1)S(1)}, u32[]{:S(2)}, u32[]{:S(2)}) collective-permute-start(bf16[40,8,128]{2,1,0:T(8,128)(2,1)S(1)} %get-tuple-element.27), channel_id=1, source_target_pairs={{0,12},{2,14},{4,8},{6,10},{8,4},{10,6},{12,0},{14,2},{1,13},{3,15... | collective-permute-start | bytes 245768 | tf_op jit(solution)/shard_map/ppermute | solution.py:523
  15.0 8.8 %collective-permute-start.10 = (bf16[40,8,128]{2,1,0:T(8,128)(2,1)S(1)}, bf16[40,8,128]{2,1,0:T(8,128)(2,1)S(1)}, u32[]{:S(2)}, u32[]{:S(2)}) collective-permute-start(bf16[40,8,128]{2,1,0:T(8,128)(2,1)S(1)} %get-tuple-element.28), channel_id=1, source_target_pairs={{0,14},{2,12},{4,10},{6,8},{8,6},{10,4},{12,2},{14,0},{1,15},{3,13... | collective-permute-start | bytes 245768 | tf_op jit(solution)/shard_map/ppermute | solution.py:523
  17.0 11.4 %copy-start.2 = (f32[1,512]{1,0:T(1,128)S(1)}, f32[1,512]{1,0:T(1,128)}, u32[]{:S(2)}) copy-start(f32[1,512]{1,0:T(1,128)} %constant.13.clone.weights) | copy-start | bytes 6148
  17.0 6.9 %collective-permute-start.11 = (bf16[40,8,128]{2,1,0:T(8,128)(2,1)S(1)}, bf16[40,8,128]{2,1,0:T(8,128)(2,1)S(1)}, u32[]{:S(2)}, u32[]{:S(2)}) collective-permute-start(bf16[40,8,128]{2,1,0:T(8,128)(2,1)S(1)} %get-tuple-element.29), channel_id=1, source_target_pairs={{0,2},{2,0},{4,6},{6,4},{8,10},{10,8},{12,14},{14,12},{1,3},{3,1},... | collective-permute-start | bytes 245768 | tf_op jit(solution)/shard_map/ppermute | solution.py:523
  23.3 1.3 %collective-permute-start.5 = (bf16[40,8,128]{2,1,0:T(8,128)(2,1)S(1)}, bf16[40,8,128]{2,1,0:T(8,128)(2,1)S(1)}, u32[]{:S(2)}, u32[]{:S(2)}) collective-permute-start(bf16[40,8,128]{2,1,0:T(8,128)(2,1)S(1)} %collective-permute-done.1.refs_1_), channel_id=1, source_target_pairs={{0,1},{1,0},{2,3},{3,2},{4,5},{5,4},{6,7},{7,6},{8,9},{9,8},{10,11... | collective-permute-start | bytes 245768 | tf_op jit(solution)/shard_map/ppermute | solution.py:491
  23.3 1.4 %collective-permute-start.6 = (bf16[40,8,128]{2,1,0:T(8,128)(2,1)S(1)}, bf16[40,8,128]{2,1,0:T(8,128)(2,1)S(1)}, u32[]{:S(2)}, u32[]{:S(2)}) collective-permute-start(bf16[40,8,128]{2,1,0:T(8,128)(2,1)S(1)} %collective-permute-done.2.refs_2_), channel_id=1, source_target_pairs={{0,1},{1,0},{2,3},{3,2},{4,5},{5,4},{6,7},{7,6},{8,9},{9,8},{10,11... | collective-permute-start | bytes 245768 | tf_op jit(solution)/shard_map/ppermute | solution.py:491
  23.8 1.3 %collective-permute-start.7 = (bf16[40,8,128]{2,1,0:T(8,128)(2,1)S(1)}, bf16[40,8,128]{2,1,0:T(8,128)(2,1)S(1)}, u32[]{:S(2)}, u32[]{:S(2)}) collective-permute-start(bf16[40,8,128]{2,1,0:T(8,128)(2,1)S(1)} %collective-permute-done.3.refs_3_), channel_id=1, source_target_pairs={{0,1},{1,0},{2,3},{3,2},{4,5},{5,4},{6,7},{7,6},{8,9},{9,8},{10,11... | collective-permute-start | bytes 245768 | tf_op jit(solution)/shard_map/ppermute | solution.py:491
  23.9 1.4 %collective-permute-start.12 = (bf16[40,8,128]{2,1,0:T(8,128)(2,1)S(1)}, bf16[40,8,128]{2,1,0:T(8,128)(2,1)S(1)}, u32[]{:S(2)}, u32[]{:S(2)}) collective-permute-start(bf16[40,8,128]{2,1,0:T(8,128)(2,1)S(1)} %collective-permute-done.8.refs_0_), channel_id=1, source_target_pairs={{0,1},{1,0},{2,3},{3,2},{4,5},{5,4},{6,7},{7,6},{8,9},{9,8},{10,11... | collective-permute-start | bytes 245768 | tf_op jit(solution)/shard_map/ppermute | solution.py:491
  24.6 3.8 %collective-permute-start.13 = (bf16[40,8,128]{2,1,0:T(8,128)(2,1)S(1)}, bf16[40,8,128]{2,1,0:T(8,128)(2,1)S(1)}, u32[]{:S(2)}, u32[]{:S(2)}) collective-permute-start(bf16[40,8,128]{2,1,0:T(8,128)(2,1)S(1)} %collective-permute-done.9.refs_1_), channel_id=1, source_target_pairs={{0,1},{1,0},{2,3},{3,2},{4,5},{5,4},{6,7},{7,6},{8,9},{9,8},{10,11... | collective-permute-start | bytes 245768 | tf_op jit(solution)/shard_map/ppermute | solution.py:491
  24.7 3.7 %collective-permute-start.14 = (bf16[40,8,128]{2,1,0:T(8,128)(2,1)S(1)}, bf16[40,8,128]{2,1,0:T(8,128)(2,1)S(1)}, u32[]{:S(2)}, u32[]{:S(2)}) collective-permute-start(bf16[40,8,128]{2,1,0:T(8,128)(2,1)S(1)} %collective-permute-done.10.refs_2_), channel_id=1, source_target_pairs={{0,1},{1,0},{2,3},{3,2},{4,5},{5,4},{6,7},{7,6},{8,9},{9,8},{10,11... | collective-permute-start | bytes 245768 | tf_op jit(solution)/shard_map/ppermute | solution.py:491
  25.1 3.3 %collective-permute-start.15 = (bf16[40,8,128]{2,1,0:T(8,128)(2,1)S(1)}, bf16[40,8,128]{2,1,0:T(8,128)(2,1)S(1)}, u32[]{:S(2)}, u32[]{:S(2)}) collective-permute-start(bf16[40,8,128]{2,1,0:T(8,128)(2,1)S(1)} %collective-permute-done.11.refs_3_), channel_id=1, source_target_pairs={{0,1},{1,0},{2,3},{3,2},{4,5},{5,4},{6,7},{7,6},{8,9},{9,8},{10,11... | collective-permute-start | bytes 245768 | tf_op jit(solution)/shard_map/ppermute | solution.py:491
  25.3 8.5 %collective-permute-start.17 = (f32[512]{0:T(512)}, f32[512]{0:T(512)S(1)}, u32[]{:S(2)}, u32[]{:S(2)}) collective-permute-start(f32[512]{0:T(512)} %param.13), channel_id=1, source_target_pairs={{0,1},{1,0},{2,3},{3,2},{4,5},{5,4},{6,7},{7,6},{8,9},{9,8},{10,11... | collective-permute-start | bytes 6152 | tf_op jit(solution)/shard_map/ppermute | solution.py:491
  28.4 19.6 %copy-start = (bf16[1680,512]{1,0:T(8,128)(2,1)S(1)}, bf16[1680,512]{1,0:T(8,128)(2,1)}, u32[]{:S(2)}) copy-start(bf16[1680,512]{1,0:T(8,128)(2,1)} %basis_own.3) | copy-start | bytes 5160964
  28.4 19.6 %copy-start.3 = (f32[4]{0:T(128)S(1)}, f32[4]{0:T(128)}, u32[]{:S(2)}) copy-start(f32[4]{0:T(128)} %prior_far.1) | copy-start | bytes 52
  48.0 12.6 %copy-start.1 = (f32[512]{0:T(512)S(1)}, f32[512]{0:T(512)}, u32[]{:S(2)}) copy-start(f32[512]{0:T(512)} %param.13) | copy-start | bytes 6148
  59.2 1.4 %collective-permute-start.18 = (bf16[8,8,1024]{2,1,0:T(8,128)(2,1)S(1)}, bf16[8,8,1024]{2,1,0:T(8,128)(2,1)S(1)}, u32[]{:S(2)}, u32[]{:S(2)}) collective-permute-start(bf16[8,8,1024]{2,1,0:T(8,128)(2,1)S(1)} %all_to_all.11.parts_own), channel_id=1, source_target_pairs={{0,1},{1,0},{2,3},{3,2},{4,5},{5,4},{6,7},{7,6},{8,9},{9,8},{10,11... | collective-permute-start | bytes 393224 | tf_op jit(solution)/shard_map/ppermute | solution.py:491
  59.2 1.4 %collective-permute-start.19 = (f32[8,1680]{1,0:T(8,128)S(1)}, f32[8,1680]{1,0:T(8,128)S(1)}, u32[]{:S(2)}, u32[]{:S(2)}) collective-permute-start(f32[8,1680]{1,0:T(8,128)S(1)} %get-tuple-element.34.flat_own), channel_id=1, source_target_pairs={{0,1},{1,0},{2,3},{3,2},{4,5},{5,4},{6,7},{7,6},{8,9},{9,8},{10,11... | collective-permute-start | bytes 161288 | tf_op jit(solution)/shard_map/ppermute | solution.py:491

commit v7 on v6

--- a/solution.py
+++ b/solution.py
@@ -181,7 +181,7 @@
         out_tile(tile, value.astype(jnp.bfloat16))
 
 
-def pack_kernel(index, prior_far, kernel, probes, *refs, order, half, packing):
+def pack_kernel(index, prior_far, kernel, probes, *refs, order, lean, half, packing, packing_probes):
     outs = refs[: len(order)]
     prior, kernel_here, probes_here, sems = refs[len(order) :]
     f32 = jnp.float32
@@ -209,7 +209,9 @@
     tiles = {}
     tails = {}
     for p in range(points):
-        store_packed(tiles.__setitem__, packing, 2 * points + p, padded(scaled[:, p, :] * prior[p]), tails)
+        value = padded(scaled[:, p, :] * prior[p])
+        store_packed(tiles.__setitem__, packing_probes, p, value, tails)
+    store_tails(tiles.__setitem__, tails)
     for copy in copies[2:]:
         copy.wait()
     for relative, out in zip(order, outs):
@@ -217,20 +219,21 @@
         def out_tile(tile, value, out=out):
             out[tile] = value
 
-        merged = dict(tails)
-        for tile, value in tiles.items():
-            out_tile(tile, value)
+        if relative not in lean:
+            for tile, value in tiles.items():
+                out_tile(packing.tiles + tile, value)
+        merged = {}
         for row in range(2 * points):
             value = padded(kernel_here[row // points, row % points, me ^ relative].astype(f32))
             store_packed(out_tile, packing, row, value, merged)
         store_tails(out_tile, merged)
 
 
-def unpack(source, row, packing):
+def unpack(source, row, packing, base=0):
     f32 = jnp.float32
-    tiles = [source[row * packing.full + t].astype(f32) for t in range(packing.full)]
+    tiles = [source[base + row * packing.full + t].astype(f32) for t in range(packing.full)]
     tile, lane = packing.place(row)
-    tiles.append(turned(source[tile].astype(f32), -lane))
+    tiles.append(turned(source[base + tile].astype(f32), -lane))
     return tiles
 
 
@@ -249,10 +252,10 @@
 
 
 def spectra(sources, table, spec, rows, *, packing, points, half, wide):
-    for b, (own, _) in enumerate(sources):
+    for b, (source, base) in enumerate(sources):
         for p in range(points):
             at = slice((b * points + p) * half, (b * points + p + 1) * half)
-            for t, tile in enumerate(unpack(own, 2 * points + p, packing)):
+            for t, tile in enumerate(unpack(source, p, packing, base)):
                 rows[at, t * LANES : (t + 1) * LANES] = tile
     got = jnp.dot(rows[...].astype(jnp.bfloat16), table[...], preferred_element_type=jnp.float32)
     real = got[:, :wide]
@@ -306,17 +309,18 @@
     return list(zip(refs[:count], refs[count : 2 * count]))
 
 
-def first_kernel(table, *refs, count, points, sens, half, wide, packing):
+def first_kernel(table, *refs, count, points, sens, half, wide, packing, packing_probes):
     sources = paired(refs, count)
     kern, data, spec, rows = refs[2 * count :]
-    spectra(sources, table, spec, rows, packing=packing, points=points, half=half, wide=wide)
+    probes = [(own, packing.tiles) for own, _ in sources]
+    spectra(probes, table, spec, rows, packing=packing_probes, points=points, half=half, wide=wide)
     widen(sources, kern, packing=packing, points=points, sens=sens)
     forward_sum(kern, spec, data, None, points=points, sens=sens, half=half, wide=wide)
 
 
 def bins_kernel(
-    index, noise_far, noise_other_far, table, weights, kern_first, data_first, *refs,
-    orders, points, sens, half, wide, packing, packing_back,
+    index, noise_far, noise_other_far, table, weights, kern_first, data_first, relayed, *refs,
+    orders, lean, points, sens, half, wide, packing, packing_probes,
 ):
     count = len(orders[1])
     sources = paired(refs, count)
@@ -330,7 +334,13 @@
     tiles = wide // LANES
     f32 = jnp.float32
     bf16 = jnp.bfloat16
-    spectra(sources, table, spec, rows, packing=packing, points=points, half=half, wide=wide)
+    probes = []
+    for relative, (own, _) in zip(orders[1], sources):
+        if relative in lean:
+            probes.append((relayed, lean.index(relative) * packing_probes.tiles))
+        else:
+            probes.append((own, packing.tiles))
+    spectra(probes, table, spec, rows, packing=packing_probes, points=points, half=half, wide=wide)
     widen(sources, kern, packing=packing, points=points, sens=sens)
     forward_sum(kern, spec, data, data_first, points=points, sens=sens, half=half, wide=wide)
     table_v = table[...]
@@ -355,10 +365,11 @@
     wdata[2] = real
 
     base = 0
-    group = 2 * points
     for source, order in ((kern_first, orders[0]), (kern, orders[1])):
 
-        def adjoint_tile(step, carry, source=source, base=base):
+        group = points if len(order) % 2 else 2 * points
+
+        def adjoint_tile(step, carry, source=source, base=base, group=group):
             first = step // tiles * group
             ft = step % tiles
             lanes = pl.ds(pl.multiple_of(ft * LANES, LANES), LANES)
@@ -393,7 +404,7 @@
         merged = {}
         for p in range(points):
             at = slice((b * points + p) * half, (b * points + p + 1) * half)
-            store_packed(out_tile, packing_back, p, back[at], merged)
+            store_packed(out_tile, packing_probes, p, back[at], merged)
         store_tails(out_tile, merged)
 
 
@@ -448,7 +459,18 @@
 def split_order(width):
     near = list(range(2, width // 2))
     far = list(range(width // 2, width))
-    return [0, far[0]] + near, far[1:] + [1]
+    return [0] + [r for r in far if r % 2 == 0] + near, [r for r in far if r % 2] + [1]
+
+
+def lean_partners(width):
+    return [r for r in range(width // 2, width) if r % 2]
+
+
+def relay_kernel(*refs, first_tile):
+    sources, out = refs[:-1], refs[-1]
+    count = out.shape[0] // len(sources)
+    for n, source in enumerate(sources):
+        out[n * count : (n + 1) * count] = source[first_tile:]
 
 
 def stage_kernel(far, near, sem):
@@ -494,17 +516,23 @@
         return lax.all_to_all(value, "pts", split_axis=0, concat_axis=0, tiled=False)
 
     table, weights = packed_tables(steps, wide)
-    packing = Packing(3 * points, bins_count)
-    packing_back = Packing(points, steps)
-    sizes = dict(points=points, sens=sens, half=half, wide=wide, packing=packing)
+    packing = Packing(2 * points, bins_count)
+    packing_probes = Packing(points, steps)
+    packings = dict(packing=packing, packing_probes=packing_probes)
+    sizes = dict(points=points, sens=sens, half=half, wide=wide, **packings)
     orders = split_order(width)
     order = orders[0] + orders[1]
     places = jnp.stack([me[0], core[0]])
-    chunk = jax.ShapeDtypeStruct((packing.tiles, sens, LANES), bf16)
+    lean = lean_partners(width)
+
+    def chunk(tiles):
+        return jax.ShapeDtypeStruct((tiles, sens, LANES), bf16)
+
+    both = packing.tiles + packing_probes.tiles
     in_hbm = pl.BlockSpec(memory_space=pltpu.HBM)
     sent = pl.pallas_call(
-        functools.partial(pack_kernel, order=order, half=half, packing=packing),
-        out_shape=(chunk,) * width,
+        functools.partial(pack_kernel, order=order, lean=lean, half=half, **packings),
+        out_shape=tuple(chunk(packing.tiles if r in lean else both) for r in order),
         in_specs=in_smem(1) + [in_hbm] * 3,
         out_specs=tuple(in_vmem(width)),
         scratch_shapes=[
@@ -523,6 +551,15 @@
             value = lax.ppermute(value, "pts", [(i, i ^ relative) for i in range(width)])
         blocks[relative] = value
         others[relative] = swap(value)
+    relayed = pl.pallas_call(
+        functools.partial(relay_kernel, first_tile=packing.tiles),
+        out_shape=chunk(len(lean) * packing_probes.tiles),
+        in_specs=in_vmem(len(lean)),
+        out_specs=in_vmem(1)[0],
+        compiler_params=limit(2),
+        name="relay",
+    )(*[blocks[r ^ 1] for r in lean])
+    relayed = lax.ppermute(relayed, "pts", [(i, i ^ 1) for i in range(width)])
     noise_other = swap(noise_weight)
     deflation_other = swap(deflation)
     basis_other = swap(basis)
@@ -560,9 +597,9 @@
     )(table, *ready(orders[0]))
     count = len(orders[1])
     back = pl.pallas_call(
-        functools.partial(bins_kernel, orders=orders, packing_back=packing_back, **sizes),
-        out_shape=jax.ShapeDtypeStruct((width, packing_back.tiles, half, LANES), bf16),
-        in_specs=in_smem(1) + [in_hbm] + in_vmem(5 + 2 * count),
+        functools.partial(bins_kernel, orders=orders, lean=lean, **sizes),
+        out_shape=jax.ShapeDtypeStruct((width, packing_probes.tiles, half, LANES), bf16),
+        in_specs=in_smem(1) + [in_hbm] + in_vmem(6 + 2 * count),
         out_specs=in_vmem(1)[0],
         scratch_shapes=[pltpu.VMEM((3, count * points, 2 * sens, wide), f32)]
         + scratch(count)
@@ -578,7 +615,7 @@
         name="bins",
     )(
         me, *kept(pltpu.HBM, noise_weight), noise_other, table, weights, kern_first, data_first,
-        *ready(orders[1]),
+        relayed, *ready(orders[1]),
     )
     back, basis_other, deflation_other = lax.optimization_barrier(
         (back, basis_other, deflation_other)
@@ -586,7 +623,7 @@
     basis, basis_other = kept(pltpu.VMEM, basis, basis_other)
     parts = exchange(back)
     flat, coeff = pl.pallas_call(
-        functools.partial(coeff_kernel, points=points, steps=steps, rank=rank, packing=packing_back),
+        functools.partial(coeff_kernel, points=points, steps=steps, rank=rank, packing=packing_probes),
         out_shape=(
             jax.ShapeDtypeStruct((half, points * steps), f32),
             jax.ShapeDtypeStruct((width, half, 2 * rank), bf16),

time: 62.6 us -> 66.2 us (1.058)
  waiting for transfers between devices: 7.84 us -> 13 us
  starting transfers between devices: 17.3 us -> 16 us
    ppermute x7, waiting for transfers between devices: 5.35 us -> 10.7 us  [local_split(): lax.ppermute(value, 'pts', [(i, i ^ relative) for i in range(width)])]
    ppermute x7, starting transfers between devices: 14 us -> 12 us  [local_split(): lax.ppermute(value, 'pts', [(i, i ^ relative) for i in range(width)])]
    ppermute x0 -> x1, starting transfers between devices: none -> 1.32 us  [local_split(): relayed = lax.ppermute(relayed, 'pts', [(i, i ^ 1) for i in range(width)])]
    pallas_call x2 -> x3, Pallas kernels: 7.13 us -> 7.05 us  [the longest x1 5.19 us: local_split(): pl.pallas_call(functools.partial(bins_kernel, orders=orders, lean=lean, *...]
  transfers between devices with their start and end apart: 20 -> 21, of which waited for: 5 -> 6; matrix products, arithmetic and copies ran while one was open for 0% -> 0% of each run, Pallas kernels for 16% -> 15%
where the time goes in v7:
time: 66.2 us; the launch traced here: 65.9 us
  blocking collectives  24.2 us (37%)
  starting transfers between devices  16 us (24%)
  waiting for transfers between devices  13 us (20%)
  Pallas kernels  12.6 us (19%)
    all_to_all x2, blocking collectives, exchange(): lax.all_to_all(value, 'pts', split_axis=0, concat_axis=0, tiled=False)  24.2 us
    ppermute x7, starting transfers between devices, local_split(): lax.ppermute(value, 'pts', [(i, i ^ relative) for i in range(width)])  12 us
    ppermute x7, waiting for transfers between devices, local_split(): lax.ppermute(value, 'pts', [(i, i ^ relative) for i in range(width)])  10.7 us
    pallas_call x1, Pallas kernels, local_split(): pl.pallas_call(functools.partial(bins_kernel, orders=orders, lean=lean, *...  5.19 us
    ppermute x13, starting transfers between devices, swap(): return lax.ppermute(value, 'sen', [(0, 1), (1, 0)])  2.61 us
    ppermute x13, waiting for transfers between devices, swap(): return lax.ppermute(value, 'sen', [(0, 1), (1, 0)])  2.24 us
    pallas_call x1, Pallas kernels, local_split(): pl.pallas_call(functools.partial(first_kernel, count=count, **sizes), out...  1.86 us
    pallas_call x1, Pallas kernels, local_split(): pl.pallas_call(functools.partial(pack_kernel, order=order, lean=lean, hal...  1.85 us
  transfers between devices with their start and end apart: 21, of which 6 were waited for; matrix products, arithmetic and copies ran while one was open for 0% of the time, Pallas kernels for 15%

profile of v7, /device:TPU:0, one launch (start us, length us, event | category | flops | bytes accessed | tf_op | source)
XLA Modules:
  0.0 65.9 jit_solution(6999421056441998670)
XLA Ops:
  0.0 0.5 collective-permute-start.17
  0.5 0.1 pad_add_fusion.index
  0.6 1.8 %pack.1 = (bf16[41,8,128]{2,1,0:T(8,128)(2,1)S(1)}, bf16[41,8,128]{2,1,0:T(8,128)(2,1)S(1)}, bf16[41,8,128]{2,1,0:T(8,128)(2,1)S(1)}, bf16[41,8,128]{2,1,0:T(8,1...) custom-call(s32[2]{0:T(128)S(1)} %pad_add_fusion.index, ...), custom_call_target="tpu_custom_call" | custom-call | tf_op jit(solution)/shard_map/pack/pallas_call | solution.py:533
  2.4 3.6 %collective-permute-start.1 = (bf16[41,8,128]{2,1,0:T(8,128)(2,1)S(1)}, bf16[41,8,128]{2,1,0:T(8,128)(2,1)S(1)}, u32[]{:S(2)}, u32[]{:S(2)}) collective-permute-start(bf16[41,8,128]{2,1,0:T(8,128)(2,1)S(1)} %get-tuple-element.21), channel_id=1, source_target_pairs={{0,8},{2,10},{4,12},{6,14},{8,0},{10,2},{12,4},{14,6},{1,9},{3,11}... | collective-permute-start | bytes 251912 | tf_op jit(solution)/shard_map/ppermute | solution.py:551
  6.1 1.3 %collective-permute-start.2 = (bf16[41,8,128]{2,1,0:T(8,128)(2,1)S(1)}, bf16[41,8,128]{2,1,0:T(8,128)(2,1)S(1)}, u32[]{:S(2)}, u32[]{:S(2)}) collective-permute-start(bf16[41,8,128]{2,1,0:T(8,128)(2,1)S(1)} %get-tuple-element.22), channel_id=1, source_target_pairs={{0,12},{2,14},{4,8},{6,10},{8,4},{10,6},{12,0},{14,2},{1,13},{3,15... | collective-permute-start | bytes 251912 | tf_op jit(solution)/shard_map/ppermute | solution.py:551
  7.4 2.6 %collective-permute-start.11 = (bf16[27,8,128]{2,1,0:T(8,128)(2,1)S(1)}, bf16[27,8,128]{2,1,0:T(8,128)(2,1)S(1)}, u32[]{:S(2)}, u32[]{:S(2)}) collective-permute-start(bf16[27,8,128]{2,1,0:T(8,128)(2,1)S(1)} %get-tuple-element.27), channel_id=1, source_target_pairs={{0,10},{2,8},{4,14},{6,12},{8,2},{10,0},{12,6},{14,4},{1,11},{3,9}... | collective-permute-start | bytes 165896 | tf_op jit(solution)/shard_map/ppermute | solution.py:551
  10.0 0.0 collective-permute-start
  10.0 1.3 %collective-permute-done.noise_other_far = f32[64]{0:T(128)S(1)} collective-permute-done((f32[64]{0:T(128)}, f32[64]{0:T(128)S(1)}, u32[]{:S(2)}, u32[]{:S(2)}) %collective-permute-start) | collective-permute-done | bytes 288 | tf_op jit(solution)/shard_map/ppermute | solution.py:513
  11.3 0.9 %collective-permute-start.12 = (bf16[27,8,128]{2,1,0:T(8,128)(2,1)S(1)}, bf16[27,8,128]{2,1,0:T(8,128)(2,1)S(1)}, u32[]{:S(2)}, u32[]{:S(2)}) collective-permute-start(bf16[27,8,128]{2,1,0:T(8,128)(2,1)S(1)} %get-tuple-element.28), channel_id=1, source_target_pairs={{0,14},{2,12},{4,10},{6,8},{8,6},{10,4},{12,2},{14,0},{1,15},{3,13... | collective-permute-start | bytes 165896 | tf_op jit(solution)/shard_map/ppermute | solution.py:551
  12.2 7.4 %collective-permute-done.11.refs_0_ = bf16[27,8,128]{2,1,0:T(8,128)(2,1)S(1)} collective-permute-done((bf16[27,8,128]{2,1,0:T(8,128)(2,1)S(1)}, bf16[27,8,128]{2,1,0:T(8,128)(2,1)S(1)}, u32[]{:S(2)}, u32[]{:S(2)}) %collective-permute-start.11) | collective-permute-done | bytes 55328 | tf_op jit(solution)/shard_map/ppermute | solution.py:551
  19.6 0.0 collective-permute-start.3
  19.6 0.0 collective-permute-done.12.refs_1_
  19.6 1.7 %collective-permute-start.4 = (bf16[41,8,128]{2,1,0:T(8,128)(2,1)S(1)}, bf16[41,8,128]{2,1,0:T(8,128)(2,1)S(1)}, u32[]{:S(2)}, u32[]{:S(2)}) collective-permute-start(bf16[41,8,128]{2,1,0:T(8,128)(2,1)S(1)} %get-tuple-element.24), channel_id=1, source_target_pairs={{0,6},{2,4},{4,2},{6,0},{8,14},{10,12},{12,10},{14,8},{1,7},{3,5},... | collective-permute-start | bytes 251912 | tf_op jit(solution)/shard_map/ppermute | solution.py:551
  21.3 0.0 collective-permute-done.1.refs_1_.refs_0_
  21.3 0.0 collective-permute-start.5
  21.3 0.0 collective-permute-done.2.refs_2_.refs_1_
  21.3 1.9 %collective-permute-start.13 = (bf16[41,8,128]{2,1,0:T(8,128)(2,1)S(1)}, bf16[41,8,128]{2,1,0:T(8,128)(2,1)S(1)}, u32[]{:S(2)}, u32[]{:S(2)}) collective-permute-start(bf16[41,8,128]{2,1,0:T(8,128)(2,1)S(1)} %get-tuple-element.29), channel_id=1, source_target_pairs={{0,2},{2,0},{4,6},{6,4},{8,10},{10,8},{12,14},{14,12},{1,3},{3,1},... | collective-permute-start | bytes 251912 | tf_op jit(solution)/shard_map/ppermute | solution.py:551
  23.2 0.9 %collective-permute-done.3.refs_3_ = bf16[41,8,128]{2,1,0:T(8,128)(2,1)S(1)} collective-permute-done((bf16[41,8,128]{2,1,0:T(8,128)(2,1)S(1)}, bf16[41,8,128]{2,1,0:T(8,128)(2,1)S(1)}, u32[]{:S(2)}, u32[]{:S(2)}) %collective-permute-start.3) | collective-permute-done | bytes 84000 | tf_op jit(solution)/shard_map/ppermute | solution.py:551
  24.1 0.0 collective-permute-start.6
  24.1 1.2 %collective-permute-done.4.refs_4_ = bf16[41,8,128]{2,1,0:T(8,128)(2,1)S(1)} collective-permute-done((bf16[41,8,128]{2,1,0:T(8,128)(2,1)S(1)}, bf16[41,8,128]{2,1,0:T(8,128)(2,1)S(1)}, u32[]{:S(2)}, u32[]{:S(2)}) %collective-permute-start.4) | collective-permute-done | bytes 84000 | tf_op jit(solution)/shard_map/ppermute | solution.py:551
  25.3 0.0 collective-permute-start.7
  25.3 0.0 collective-permute-done.5.refs_5_
  25.3 0.5 collective-permute-start.14
  25.8 1.2 %collective-permute-done.13.refs_2_ = bf16[41,8,128]{2,1,0:T(8,128)(2,1)S(1)} collective-permute-done((bf16[41,8,128]{2,1,0:T(8,128)(2,1)S(1)}, bf16[41,8,128]{2,1,0:T(8,128)(2,1)S(1)}, u32[]{:S(2)}, u32[]{:S(2)}) %collective-permute-start.13) | collective-permute-done | bytes 84000 | tf_op jit(solution)/shard_map/ppermute | solution.py:551
  27.0 0.1 collective-permute-start.8
  27.1 0.0 collective-permute-done.14.refs_3_
  27.1 0.4 collective-permute-start.9
  27.5 0.0 collective-permute-done.6.refs_6_
  27.5 0.1 collective-permute-start.16
  27.6 0.0 copy-start.2
  27.6 0.0 collective-permute-done.7.refs_7_
  27.6 1.3 %collective-permute-start.10 = (bf16[28,8,128]{2,1,0:T(8,128)(2,1)S(1)}, bf16[28,8,128]{2,1,0:T(8,128)(2,1)S(1)}, u32[]{:S(2)}, u32[]{:S(2)}) collective-permute-start(bf16[28,8,128]{2,1,0:T(8,128)(2,1)S(1)} %relay.1), channel_id=1, source_target_pairs={{0,2},{2,0},{4,6},{6,4},{8,10},{10,8},{12,14},{14,12},{1,3},{3,1},... | collective-permute-start | bytes 172040 | tf_op jit(solution)/shard_map/ppermute | solution.py:562
  28.9 0.0 collective-permute-done.8.refs_8_
  28.9 0.2 collective-permute-start.15
  29.1 0.0 collective-permute-done.9.refs_9_
  29.1 0.3 collective-permute-start.18
  29.4 1.2 %stage.1.table = bf16[512,1024]{1,0:T(8,128)(2,1)S(1)} custom-call(bf16[512,1024]{1,0:T(8,128)(2,1)} %constant.12.clone.far), custom_call_target="tpu_custom_call" | custom-call | tf_op jit(solution)/shard_map/stage/pallas_call | solution.py:576
  30.7 1.9 %first.1 = (f32[3,20,16,512]{3,2,1,0:T(8,128)S(1)}, f32[128,1024]{1,0:T(8,128)S(1)}) custom-call(bf16[512,1024]{1,0:T(8,128)(2,1)S(1)} %stage.1.table, bf16[41,8,128]{2,1,0:T(8,128)(2,1)S(1)} %get-tuple-element.20.refs_0_, bf16[41,8,128]{2,1,0:T(8,128)(2,1)S(1)} %collective-permute-done.1.refs_1_.refs_0_, ...), custom_call_target="tpu_custom_call" | custom-call | tf_op jit(solution)/shard_map/first/pallas_call | solution.py:586
  32.6 0.0 collective-permute-done.15.refs_4_
  32.6 0.0 collective-permute-done.10.relayed
  32.6 0.0 collective-permute-done.16.refs_5_
  32.6 0.0 copy-done.2
  32.6 0.0 copy-start
  32.6 0.0 copy-start.3
  32.6 5.2 %bins.1 = bf16[8,14,8,128]{3,2,1,0:T(8,128)(2,1)S(1)} custom-call(s32[1]{0:T(128)} %bitcast.2.index, f32[64]{0:T(128)} %noise_far.1, f32[64]{0:T(128)S(1)} %collective-permute-done.noise_other_far, bf16[512,1024]{1,0:T(8,128)(2,1)S(1)} %stage.1.table, f32[1,512]{1,0:T(1,128)S(1)} %copy-done.2, f32[3,20,16,512]{3,2,1,0:T(8,128)S(1)} %get-tuple-element.25.kern_first, ...), custom_call_target="tpu_custom_call" | custom-call | tf_op jit(solution)/shard_map/bins/pallas_call | solution.py:599
  37.8 0.0 collective-permute-done.18
  37.8 0.0 collective-permute-done.17.basis_other
  37.8 13.7 %all_to_all.10.parts = bf16[8,14,8,128]{3,2,1,0:T(8,128)(2,1)S(1)} all-to-all(bf16[8,14,8,128]{3,2,1,0:T(8,128)(2,1)S(1)} %bins.1), channel_id=1, replica_groups=mesh['grp'=2,'pts'=8,'sen'=2] {'pts'}, dimensions={0} | all-to-all | bytes 458752 | tf_op jit(solution)/shard_map/all_to_all | solution.py:516
  51.5 0.0 copy-done
  51.5 0.0 copy-done.3
  51.5 0.0 copy-start.1
  51.5 0.6 coeff.1
  52.2 10.5 %all_to_all.11.parts_own = bf16[8,8,1024]{2,1,0:T(8,128)(2,1)S(1)} all-to-all(bf16[8,8,1024]{2,1,0:T(8,128)(2,1)S(1)} %get-tuple-element.32), channel_id=1, replica_groups=mesh['grp'=2,'pts'=8,'sen'=2] {'pts'}, dimensions={0} | all-to-all | bytes 262144 | tf_op jit(solution)/shard_map/all_to_all | solution.py:516
  62.7 0.0 collective-permute-start.19
  62.7 0.5 collective-permute-start.20
  63.2 0.9 %collective-permute-done.20.flat_other = f32[8,1680]{1,0:T(8,128)S(1)} collective-permute-done((f32[8,1680]{1,0:T(8,128)S(1)}, f32[8,1680]{1,0:T(8,128)S(1)}, u32[]{:S(2)}, u32[]{:S(2)}) %collective-permute-start.20) | collective-permute-done | bytes 53792 | tf_op jit(solution)/shard_map/ppermute | solution.py:513
  64.1 0.0 collective-permute-done.19.parts_other
  64.1 0.0 copy-done.1
  64.1 1.8 %deflate.1 = f32[16,4,420]{2,1,0:T(4,128)} custom-call(s32[1]{0:T(128)} %bitcast.core, bf16[8,8,1024]{2,1,0:T(8,128)(2,1)S(1)} %all_to_all.11.parts_own, bf16[8,8,1024]{2,1,0:T(8,128)(2,1)S(1)} %collective-permute-done.19.parts_other, f32[1,512]{1,0:T(1,128)S(1)} %bitcast.6, f32[1,512]{1,0:T(1,128)S(1)} %bitcast.7, ...), custom_call_target="tpu_custom_call" | custom-call | tf_op jit(solution)/shard_map/deflate/pallas_call | solution.py:639
  (1 shorter events, 0.0 us)
Async XLA Ops:
  0.0 37.8 %collective-permute-start.17 = (bf16[1680,512]{1,0:T(8,128)(2,1)}, bf16[1680,512]{1,0:T(8,128)(2,1)S(1)}, u32[]{:S(2)}, u32[]{:S(2)}) collective-permute-start(bf16[1680,512]{1,0:T(8,128)(2,1)} %basis_own.3), channel_id=1, source_target_pairs={{0,1},{1,0},{2,3},{3,2},{4,5},{5,4},{6,7},{7,6},{8,9},{9,8},{10,11... | collective-permute-start | bytes 5160968 | tf_op jit(solution)/shard_map/ppermute | solution.py:513
  2.4 18.9 %collective-permute-start.1 = (bf16[41,8,128]{2,1,0:T(8,128)(2,1)S(1)}, bf16[41,8,128]{2,1,0:T(8,128)(2,1)S(1)}, u32[]{:S(2)}, u32[]{:S(2)}) collective-permute-start(bf16[41,8,128]{2,1,0:T(8,128)(2,1)S(1)} %get-tuple-element.21), channel_id=1, source_target_pairs={{0,8},{2,10},{4,12},{6,14},{8,0},{10,2},{12,4},{14,6},{1,9},{3,11}... | collective-permute-start | bytes 251912 | tf_op jit(solution)/shard_map/ppermute | solution.py:551
  6.1 15.2 %collective-permute-start.2 = (bf16[41,8,128]{2,1,0:T(8,128)(2,1)S(1)}, bf16[41,8,128]{2,1,0:T(8,128)(2,1)S(1)}, u32[]{:S(2)}, u32[]{:S(2)}) collective-permute-start(bf16[41,8,128]{2,1,0:T(8,128)(2,1)S(1)} %get-tuple-element.22), channel_id=1, source_target_pairs={{0,12},{2,14},{4,8},{6,10},{8,4},{10,6},{12,0},{14,2},{1,13},{3,15... | collective-permute-start | bytes 251912 | tf_op jit(solution)/shard_map/ppermute | solution.py:551
  7.4 12.2 %collective-permute-start.11 = (bf16[27,8,128]{2,1,0:T(8,128)(2,1)S(1)}, bf16[27,8,128]{2,1,0:T(8,128)(2,1)S(1)}, u32[]{:S(2)}, u32[]{:S(2)}) collective-permute-start(bf16[27,8,128]{2,1,0:T(8,128)(2,1)S(1)} %get-tuple-element.27), channel_id=1, source_target_pairs={{0,10},{2,8},{4,14},{6,12},{8,2},{10,0},{12,6},{14,4},{1,11},{3,9}... | collective-permute-start | bytes 165896 | tf_op jit(solution)/shard_map/ppermute | solution.py:551
  10.0 1.3 %collective-permute-start = (f32[64]{0:T(128)}, f32[64]{0:T(128)S(1)}, u32[]{:S(2)}, u32[]{:S(2)}) collective-permute-start(f32[64]{0:T(128)} %noise_far.1), channel_id=1, source_target_pairs={{0,1},{1,0},{2,3},{3,2},{4,5},{5,4},{6,7},{7,6},{8,9},{9,8},{10,11... | collective-permute-start | bytes 776 | tf_op jit(solution)/shard_map/ppermute | solution.py:513
  11.3 8.3 %collective-permute-start.12 = (bf16[27,8,128]{2,1,0:T(8,128)(2,1)S(1)}, bf16[27,8,128]{2,1,0:T(8,128)(2,1)S(1)}, u32[]{:S(2)}, u32[]{:S(2)}) collective-permute-start(bf16[27,8,128]{2,1,0:T(8,128)(2,1)S(1)} %get-tuple-element.28), channel_id=1, source_target_pairs={{0,14},{2,12},{4,10},{6,8},{8,6},{10,4},{12,2},{14,0},{1,15},{3,13... | collective-permute-start | bytes 165896 | tf_op jit(solution)/shard_map/ppermute | solution.py:551
  19.6 4.5 %collective-permute-start.3 = (bf16[41,8,128]{2,1,0:T(8,128)(2,1)S(1)}, bf16[41,8,128]{2,1,0:T(8,128)(2,1)S(1)}, u32[]{:S(2)}, u32[]{:S(2)}) collective-permute-start(bf16[41,8,128]{2,1,0:T(8,128)(2,1)S(1)} %get-tuple-element.23), channel_id=1, source_target_pairs={{0,4},{2,6},{4,0},{6,2},{8,12},{10,14},{12,8},{14,10},{1,5},{3,7},... | collective-permute-start | bytes 251912 | tf_op jit(solution)/shard_map/ppermute | solution.py:551
  19.6 5.7 %collective-permute-start.4 = (bf16[41,8,128]{2,1,0:T(8,128)(2,1)S(1)}, bf16[41,8,128]{2,1,0:T(8,128)(2,1)S(1)}, u32[]{:S(2)}, u32[]{:S(2)}) collective-permute-start(bf16[41,8,128]{2,1,0:T(8,128)(2,1)S(1)} %get-tuple-element.24), channel_id=1, source_target_pairs={{0,6},{2,4},{4,2},{6,0},{8,14},{10,12},{12,10},{14,8},{1,7},{3,5},... | collective-permute-start | bytes 251912 | tf_op jit(solution)/shard_map/ppermute | solution.py:551
  21.3 4.0 %collective-permute-start.5 = (bf16[41,8,128]{2,1,0:T(8,128)(2,1)S(1)}, bf16[41,8,128]{2,1,0:T(8,128)(2,1)S(1)}, u32[]{:S(2)}, u32[]{:S(2)}) collective-permute-start(bf16[41,8,128]{2,1,0:T(8,128)(2,1)S(1)} %get-tuple-element.20.refs_0_), channel_id=1, source_target_pairs={{0,1},{1,0},{2,3},{3,2},{4,5},{5,4},{6,7},{7,6},{8,9},{9,8},{10,11... | collective-permute-start | bytes 251912 | tf_op jit(solution)/shard_map/ppermute | solution.py:513
  21.3 5.7 %collective-permute-start.13 = (bf16[41,8,128]{2,1,0:T(8,128)(2,1)S(1)}, bf16[41,8,128]{2,1,0:T(8,128)(2,1)S(1)}, u32[]{:S(2)}, u32[]{:S(2)}) collective-permute-start(bf16[41,8,128]{2,1,0:T(8,128)(2,1)S(1)} %get-tuple-element.29), channel_id=1, source_target_pairs={{0,2},{2,0},{4,6},{6,4},{8,10},{10,8},{12,14},{14,12},{1,3},{3,1},... | collective-permute-start | bytes 251912 | tf_op jit(solution)/shard_map/ppermute | solution.py:551
  24.1 3.4 %collective-permute-start.6 = (bf16[41,8,128]{2,1,0:T(8,128)(2,1)S(1)}, bf16[41,8,128]{2,1,0:T(8,128)(2,1)S(1)}, u32[]{:S(2)}, u32[]{:S(2)}) collective-permute-start(bf16[41,8,128]{2,1,0:T(8,128)(2,1)S(1)} %collective-permute-done.1.refs_1_.refs_0_), channel_id=1, source_target_pairs={{0,1},{1,0},{2,3},{3,2},{4,5},{5,4},{6,7},{7,6},{8,9},{9,8},{10,11... | collective-permute-start | bytes 251912 | tf_op jit(solution)/shard_map/ppermute | solution.py:513
  25.3 2.3 %collective-permute-start.7 = (bf16[41,8,128]{2,1,0:T(8,128)(2,1)S(1)}, bf16[41,8,128]{2,1,0:T(8,128)(2,1)S(1)}, u32[]{:S(2)}, u32[]{:S(2)}) collective-permute-start(bf16[41,8,128]{2,1,0:T(8,128)(2,1)S(1)} %collective-permute-done.2.refs_2_.refs_1_), channel_id=1, source_target_pairs={{0,1},{1,0},{2,3},{3,2},{4,5},{5,4},{6,7},{7,6},{8,9},{9,8},{10,11... | collective-permute-start | bytes 251912 | tf_op jit(solution)/shard_map/ppermute | solution.py:513
  25.3 1.8 %collective-permute-start.14 = (bf16[27,8,128]{2,1,0:T(8,128)(2,1)S(1)}, bf16[27,8,128]{2,1,0:T(8,128)(2,1)S(1)}, u32[]{:S(2)}, u32[]{:S(2)}) collective-permute-start(bf16[27,8,128]{2,1,0:T(8,128)(2,1)S(1)} %collective-permute-done.11.refs_0_), channel_id=1, source_target_pairs={{0,1},{1,0},{2,3},{3,2},{4,5},{5,4},{6,7},{7,6},{8,9},{9,8},{10,11... | collective-permute-start | bytes 165896 | tf_op jit(solution)/shard_map/ppermute | solution.py:513
  27.0 1.9 %collective-permute-start.8 = (bf16[41,8,128]{2,1,0:T(8,128)(2,1)S(1)}, bf16[41,8,128]{2,1,0:T(8,128)(2,1)S(1)}, u32[]{:S(2)}, u32[]{:S(2)}) collective-permute-start(bf16[41,8,128]{2,1,0:T(8,128)(2,1)S(1)} %collective-permute-done.3.refs_3_), channel_id=1, source_target_pairs={{0,1},{1,0},{2,3},{3,2},{4,5},{5,4},{6,7},{7,6},{8,9},{9,8},{10,11... | collective-permute-start | bytes 251912 | tf_op jit(solution)/shard_map/ppermute | solution.py:513
  27.1 2.0 %collective-permute-start.9 = (bf16[41,8,128]{2,1,0:T(8,128)(2,1)S(1)}, bf16[41,8,128]{2,1,0:T(8,128)(2,1)S(1)}, u32[]{:S(2)}, u32[]{:S(2)}) collective-permute-start(bf16[41,8,128]{2,1,0:T(8,128)(2,1)S(1)} %collective-permute-done.4.refs_4_), channel_id=1, source_target_pairs={{0,1},{1,0},{2,3},{3,2},{4,5},{5,4},{6,7},{7,6},{8,9},{9,8},{10,11... | collective-permute-start | bytes 251912 | tf_op jit(solution)/shard_map/ppermute | solution.py:513
  27.5 5.1 %collective-permute-start.16 = (bf16[41,8,128]{2,1,0:T(8,128)(2,1)S(1)}, bf16[41,8,128]{2,1,0:T(8,128)(2,1)S(1)}, u32[]{:S(2)}, u32[]{:S(2)}) collective-permute-start(bf16[41,8,128]{2,1,0:T(8,128)(2,1)S(1)} %collective-permute-done.13.refs_2_), channel_id=1, source_target_pairs={{0,1},{1,0},{2,3},{3,2},{4,5},{5,4},{6,7},{7,6},{8,9},{9,8},{10,11... | collective-permute-start | bytes 251912 | tf_op jit(solution)/shard_map/ppermute | solution.py:513
  27.6 5.0 %copy-start.2 = (f32[1,512]{1,0:T(1,128)S(1)}, f32[1,512]{1,0:T(1,128)}, u32[]{:S(2)}) copy-start(f32[1,512]{1,0:T(1,128)} %constant.13.clone.weights) | copy-start | bytes 6148
  27.6 5.0 %collective-permute-start.10 = (bf16[28,8,128]{2,1,0:T(8,128)(2,1)S(1)}, bf16[28,8,128]{2,1,0:T(8,128)(2,1)S(1)}, u32[]{:S(2)}, u32[]{:S(2)}) collective-permute-start(bf16[28,8,128]{2,1,0:T(8,128)(2,1)S(1)} %relay.1), channel_id=1, source_target_pairs={{0,2},{2,0},{4,6},{6,4},{8,10},{10,8},{12,14},{14,12},{1,3},{3,1},... | collective-permute-start | bytes 172040 | tf_op jit(solution)/shard_map/ppermute | solution.py:562
  28.9 3.6 %collective-permute-start.15 = (bf16[27,8,128]{2,1,0:T(8,128)(2,1)S(1)}, bf16[27,8,128]{2,1,0:T(8,128)(2,1)S(1)}, u32[]{:S(2)}, u32[]{:S(2)}) collective-permute-start(bf16[27,8,128]{2,1,0:T(8,128)(2,1)S(1)} %collective-permute-done.12.refs_1_), channel_id=1, source_target_pairs={{0,1},{1,0},{2,3},{3,2},{4,5},{5,4},{6,7},{7,6},{8,9},{9,8},{10,11... | collective-permute-start | bytes 165896 | tf_op jit(solution)/shard_map/ppermute | solution.py:513
  29.1 8.7 %collective-permute-start.18 = (f32[512]{0:T(512)}, f32[512]{0:T(512)S(1)}, u32[]{:S(2)}, u32[]{:S(2)}) collective-permute-start(f32[512]{0:T(512)} %param.13), channel_id=1, source_target_pairs={{0,1},{1,0},{2,3},{3,2},{4,5},{5,4},{6,7},{7,6},{8,9},{9,8},{10,11... | collective-permute-start | bytes 6152 | tf_op jit(solution)/shard_map/ppermute | solution.py:513
  32.6 18.9 %copy-start = (bf16[1680,512]{1,0:T(8,128)(2,1)S(1)}, bf16[1680,512]{1,0:T(8,128)(2,1)}, u32[]{:S(2)}) copy-start(bf16[1680,512]{1,0:T(8,128)(2,1)} %basis_own.3) | copy-start | bytes 5160964
  32.6 18.9 %copy-start.3 = (f32[4]{0:T(128)S(1)}, f32[4]{0:T(128)}, u32[]{:S(2)}) copy-start(f32[4]{0:T(128)} %prior_far.1) | copy-start | bytes 52
  51.5 12.6 %copy-start.1 = (f32[512]{0:T(512)S(1)}, f32[512]{0:T(512)}, u32[]{:S(2)}) copy-start(f32[512]{0:T(512)} %param.13) | copy-start | bytes 6148
  62.7 1.4 %collective-permute-start.19 = (bf16[8,8,1024]{2,1,0:T(8,128)(2,1)S(1)}, bf16[8,8,1024]{2,1,0:T(8,128)(2,1)S(1)}, u32[]{:S(2)}, u32[]{:S(2)}) collective-permute-start(bf16[8,8,1024]{2,1,0:T(8,128)(2,1)S(1)} %all_to_all.11.parts_own), channel_id=1, source_target_pairs={{0,1},{1,0},{2,3},{3,2},{4,5},{5,4},{6,7},{7,6},{8,9},{9,8},{10,11... | collective-permute-start | bytes 393224 | tf_op jit(solution)/shard_map/ppermute | solution.py:513
  62.7 1.4 %collective-permute-start.20 = (f32[8,1680]{1,0:T(8,128)S(1)}, f32[8,1680]{1,0:T(8,128)S(1)}, u32[]{:S(2)}, u32[]{:S(2)}) collective-permute-start(f32[8,1680]{1,0:T(8,128)S(1)} %get-tuple-element.34.flat_own), channel_id=1, source_target_pairs={{0,1},{1,0},{2,3},{3,2},{4,5},{5,4},{6,7},{7,6},{8,9},{9,8},{10,11... | collective-permute-start | bytes 161288 | tf_op jit(solution)/shard_map/ppermute | solution.py:513

commit v8 on v7

--- a/solution.py
+++ b/solution.py
@@ -181,10 +181,14 @@
         out_tile(tile, value.astype(jnp.bfloat16))
 
 
-def pack_kernel(index, prior_far, kernel, probes, *refs, order, lean, half, packing, packing_probes):
+def pack_kernel(
+    index, prior_far, noise_far, kernel, probes, table_far, *refs,
+    order, lean, half, packing, packing_probes,
+):
     outs = refs[: len(order)]
-    prior, kernel_here, probes_here, sems = refs[len(order) :]
+    table, prior, noise, kernel_here, probes_here, sems = refs[len(order) :]
     f32 = jnp.float32
+    bf16 = jnp.bfloat16
     _, points, _ = probes_here.shape
     edge = packing.full * LANES
     me = index[0]
@@ -196,6 +200,8 @@
     for row in range(2 * points):
         at = (row // points, row % points)
         copies.append(pltpu.make_async_copy(kernel.at[at], kernel_here.at[at], sems.at[2 + row]))
+    copies.append(pltpu.make_async_copy(noise_far, noise, sems.at[2 + 2 * points]))
+    copies.append(pltpu.make_async_copy(table_far, table, sems.at[3 + 2 * points]))
     for copy in copies:
         copy.start()
 
@@ -212,7 +218,7 @@
         value = padded(scaled[:, p, :] * prior[p])
         store_packed(tiles.__setitem__, packing_probes, p, value, tails)
     store_tails(tiles.__setitem__, tails)
-    for copy in copies[2:]:
+    for copy in copies[2:-1]:
         copy.wait()
     for relative, out in zip(order, outs):
 
@@ -227,6 +233,19 @@
             value = padded(kernel_here[row // points, row % points, me ^ relative].astype(f32))
             store_packed(out_tile, packing, row, value, merged)
         store_tails(out_tile, merged)
+    sens = outs[0].shape[1]
+    shape = (sens, LANES)
+    where = lax.broadcasted_iota(jnp.int32, shape, 0)
+    lane = lax.broadcasted_iota(jnp.int32, shape, 1)
+    column = jnp.zeros(shape, f32)
+    for s in range(sens):
+        column = jnp.where(where == s, noise[me * sens + s], column)
+    high = column.astype(bf16).astype(f32)
+    middle = (column - high).astype(bf16).astype(f32)
+    low = column - high - middle
+    pieces = jnp.where(lane == 0, high, jnp.where(lane == 1, middle, jnp.where(lane == 2, low, 0.0)))
+    outs[0][outs[0].shape[0] - 1] = pieces.astype(bf16)
+    copies[-1].wait()
 
 
 def unpack(source, row, packing, base=0):
@@ -319,25 +338,22 @@
 
 
 def bins_kernel(
-    index, noise_far, noise_other_far, table, weights, kern_first, data_first, relayed, *refs,
+    index, noise_far, neighbour, table, weights, kern_first, data_first, *refs,
     orders, lean, points, sens, half, wide, packing, packing_probes,
 ):
     count = len(orders[1])
     sources = paired(refs, count)
-    out, kern, spec, rows, data, wdata, adjoint, noise_own, noise_other, sems = refs[2 * count :]
-    copies = [
-        pltpu.make_async_copy(noise_far, noise_own, sems.at[0]),
-        pltpu.make_async_copy(noise_other_far, noise_other, sems.at[1]),
-    ]
-    for copy in copies:
-        copy.start()
+    out, kern, spec, rows, data, wdata, adjoint, noise_own, sem = refs[2 * count :]
+    copy = pltpu.make_async_copy(noise_far, noise_own, sem)
+    copy.start()
     tiles = wide // LANES
     f32 = jnp.float32
     bf16 = jnp.bfloat16
     probes = []
     for relative, (own, _) in zip(orders[1], sources):
         if relative in lean:
-            probes.append((relayed, lean.index(relative) * packing_probes.tiles))
+            behind = packing.tiles + (1 + lean.index(relative)) * packing_probes.tiles
+            probes.append((sources[orders[1].index(1)][0], behind))
         else:
             probes.append((own, packing.tiles))
     spectra(probes, table, spec, rows, packing=packing_probes, points=points, half=half, wide=wide)
@@ -349,11 +365,11 @@
         [data[:, :wide] * weight_rows, data[:, wide:] * weight_rows], axis=1
     ).astype(bf16)
     observed = lax.dot_general(scaled, table_v, NT, preferred_element_type=f32)
-    for copy in copies:
-        copy.wait()
-    mine = index[0] * sens
-    scales = [noise_own[mine + s] for s in range(sens)]
-    scales += [noise_other[mine + s] for s in range(sens)]
+    copy.wait()
+    pieces = neighbour[neighbour.shape[0] - 1].astype(f32)
+    column = pieces[:, 0:1] + pieces[:, 1:2] + pieces[:, 2:3]
+    scales = [noise_own[index[0] * sens + s] for s in range(sens)]
+    scales += [column[s : s + 1] for s in range(sens)]
     residual = jnp.concatenate(
         [observed[s * half : (s + 1) * half] * scale for s, scale in enumerate(scales)], axis=0
     ).astype(bf16)
@@ -416,7 +432,7 @@
 
 
 def coeff_kernel(
-    prior, parts, basis_own, basis_other, flat, coeff, *, points, steps, rank, packing
+    prior, deflation, parts, basis_own, basis_other, flat, coeff, *, points, steps, rank, packing
 ):
     f32 = jnp.float32
     total = summed(parts)
@@ -426,7 +442,9 @@
         tiles.append(turned(total[tile], -lane))
         piece = jnp.concatenate(tiles, axis=1) * prior[:, p : p + 1]
         flat[:, p * steps : (p + 1) * steps] = piece[:, :steps]
-    low = flat[...].astype(jnp.bfloat16)
+    low = flat[:, : points * steps].astype(jnp.bfloat16)
+    behind = flat.shape[1] - rank
+    flat[:, behind:] = jnp.broadcast_to(deflation[...], (flat.shape[0], rank))
     own = jnp.dot(low, basis_own[...], preferred_element_type=f32).astype(jnp.bfloat16)
     other = jnp.dot(low, basis_other[...], preferred_element_type=f32).astype(jnp.bfloat16)
     for j in range(coeff.shape[0]):
@@ -435,8 +453,7 @@
 
 
 def deflate_kernel(
-    core, parts_own, parts_other, deflation_own, deflation_other, flat_own, flat_other,
-    basis_own, basis_other, out,
+    core, parts_own, parts_other, flat_own, flat_other, basis_own, basis_other, out,
     *, points, steps, rank,
 ):
     f32 = jnp.float32
@@ -444,11 +461,15 @@
     own = summed(parts_own)
     other = summed(parts_other)
     half = own.shape[0]
-    here = jnp.concatenate([own[:, :rank], other[:, rank:]], axis=0) * deflation_own[...]
-    there = jnp.concatenate([own[:, rank:], other[:, :rank]], axis=0) * deflation_other[...]
+    behind = flat_own.shape[1] - rank
+    deflation_own = flat_own[0:1, behind:]
+    deflation_other = flat_other[0:1, behind:]
+    size = points * steps
+    here = jnp.concatenate([own[:, :rank], other[:, rank:]], axis=0) * deflation_own
+    there = jnp.concatenate([own[:, rank:], other[:, :rank]], axis=0) * deflation_other
     correction = lax.dot_general(here.astype(bf16), basis_own[...], NT, preferred_element_type=f32)
     correction += lax.dot_general(there.astype(bf16), basis_other[...], NT, preferred_element_type=f32)
-    result = jnp.concatenate([flat_own[...], flat_other[...]], axis=0) - correction
+    result = jnp.concatenate([flat_own[:, :size], flat_other[:, :size]], axis=0) - correction
     mine = core[0] * half
     for p in range(points):
         piece = result[:, p * steps : (p + 1) * steps]
@@ -459,24 +480,22 @@
 def split_order(width):
     near = list(range(2, width // 2))
     far = list(range(width // 2, width))
-    return [0] + [r for r in far if r % 2 == 0] + near, [r for r in far if r % 2] + [1]
+    order = [0] + [r for r in far if r % 2 == 0] + near + [r for r in far if r % 2] + [1]
+    return order[: width // 2], order[width // 2 :]
 
 
 def lean_partners(width):
     return [r for r in range(width // 2, width) if r % 2]
 
 
-def relay_kernel(*refs, first_tile):
+def relay_kernel(ours, *refs, first_tile):
     sources, out = refs[:-1], refs[-1]
-    count = out.shape[0] // len(sources)
-    for n, source in enumerate(sources):
-        out[n * count : (n + 1) * count] = source[first_tile:]
-
-
-def stage_kernel(far, near, sem):
-    copy = pltpu.make_async_copy(far, near, sem)
-    copy.start()
-    copy.wait()
+    base = ours.shape[0]
+    out[:base] = ours[...]
+    for source in sources:
+        count = source.shape[0] - first_tile
+        out[base : base + count] = source[first_tile:]
+        base += count
 
 
 def kept(space, *values):
@@ -529,39 +548,50 @@
         return jax.ShapeDtypeStruct((tiles, sens, LANES), bf16)
 
     both = packing.tiles + packing_probes.tiles
+    tiles = [packing.tiles if r in lean else both for r in order]
+    tiles[0] += 1
     in_hbm = pl.BlockSpec(memory_space=pltpu.HBM)
-    sent = pl.pallas_call(
+    *sent, table = pl.pallas_call(
         functools.partial(pack_kernel, order=order, lean=lean, half=half, **packings),
-        out_shape=tuple(chunk(packing.tiles if r in lean else both) for r in order),
-        in_specs=in_smem(1) + [in_hbm] * 3,
-        out_specs=tuple(in_vmem(width)),
+        out_shape=tuple(chunk(count) for count in tiles) + (pltpu.VMEM(table.shape, bf16),),
+        in_specs=in_smem(1) + [in_hbm] * 5,
+        out_specs=tuple(in_vmem(width + 1)),
         scratch_shapes=[
             pltpu.SMEM(prior_scale.shape, f32),
+            pltpu.SMEM(noise_weight.shape, f32),
             pltpu.VMEM((2, points, width, sens, bins_count), bf16),
             pltpu.VMEM((half, points, steps), bf16),
-            pltpu.SemaphoreType.DMA((2 + 2 * points,)),
+            pltpu.SemaphoreType.DMA((4 + 2 * points,)),
         ],
         compiler_params=limit(8),
         name="pack",
-    )(places, *kept(pltpu.HBM, prior_scale, kernel.reshape(2, points, width, sens, bins_count), probes))
+    )(
+        places,
+        *kept(
+            pltpu.HBM,
+            prior_scale,
+            noise_weight,
+            kernel.reshape(2, points, width, sens, bins_count),
+            probes,
+            table,
+        ),
+    )
     blocks = {}
     others = {}
     for relative, value in zip(order, sent):
+        if relative == 1:
+            value = pl.pallas_call(
+                functools.partial(relay_kernel, first_tile=packing.tiles),
+                out_shape=chunk(both + len(lean) * packing_probes.tiles),
+                in_specs=in_vmem(1 + len(lean)),
+                out_specs=in_vmem(1)[0],
+                compiler_params=limit(2),
+                name="relay",
+            )(value, *[blocks[r ^ 1] for r in lean])
         if relative:
             value = lax.ppermute(value, "pts", [(i, i ^ relative) for i in range(width)])
         blocks[relative] = value
         others[relative] = swap(value)
-    relayed = pl.pallas_call(
-        functools.partial(relay_kernel, first_tile=packing.tiles),
-        out_shape=chunk(len(lean) * packing_probes.tiles),
-        in_specs=in_vmem(len(lean)),
-        out_specs=in_vmem(1)[0],
-        compiler_params=limit(2),
-        name="relay",
-    )(*[blocks[r ^ 1] for r in lean])
-    relayed = lax.ppermute(relayed, "pts", [(i, i ^ 1) for i in range(width)])
-    noise_other = swap(noise_weight)
-    deflation_other = swap(deflation)
     basis_other = swap(basis)
 
     def scratch(count):
@@ -573,15 +603,6 @@
     def ready(part):
         return [blocks[r] for r in part] + [others[r] for r in part]
 
-    table = pl.pallas_call(
-        stage_kernel,
-        out_shape=pltpu.VMEM(table.shape, bf16),
-        in_specs=[in_hbm],
-        out_specs=in_vmem(1)[0],
-        scratch_shapes=[pltpu.SemaphoreType.DMA],
-        compiler_params=limit(2),
-        name="stage",
-    )(*kept(pltpu.HBM, table))
     count = len(orders[0])
     kern_first, data_first = pl.pallas_call(
         functools.partial(first_kernel, count=count, **sizes),
@@ -599,7 +620,7 @@
     back = pl.pallas_call(
         functools.partial(bins_kernel, orders=orders, lean=lean, **sizes),
         out_shape=jax.ShapeDtypeStruct((width, packing_probes.tiles, half, LANES), bf16),
-        in_specs=in_smem(1) + [in_hbm] + in_vmem(6 + 2 * count),
+        in_specs=in_smem(1) + [in_hbm] + in_vmem(5 + 2 * count),
         out_specs=in_vmem(1)[0],
         scratch_shapes=[pltpu.VMEM((3, count * points, 2 * sens, wide), f32)]
         + scratch(count)
@@ -608,44 +629,40 @@
             pltpu.VMEM((3, 2 * sens * half, wide), f32),
             pltpu.VMEM((width * points * half, 2 * wide), f32),
             pltpu.SMEM(noise_weight.shape, f32),
-            pltpu.SMEM(noise_weight.shape, f32),
-            pltpu.SemaphoreType.DMA((2,)),
+            pltpu.SemaphoreType.DMA,
         ],
         compiler_params=limit(20),
         name="bins",
     )(
-        me, *kept(pltpu.HBM, noise_weight), noise_other, table, weights, kern_first, data_first,
-        relayed, *ready(orders[1]),
-    )
-    back, basis_other, deflation_other = lax.optimization_barrier(
-        (back, basis_other, deflation_other)
-    )
+        me, *kept(pltpu.HBM, noise_weight), others[0], table, weights, kern_first, data_first,
+        *ready(orders[1]),
+    )
+    back, basis_other = lax.optimization_barrier((back, basis_other))
     basis, basis_other = kept(pltpu.VMEM, basis, basis_other)
     parts = exchange(back)
     flat, coeff = pl.pallas_call(
         functools.partial(coeff_kernel, points=points, steps=steps, rank=rank, packing=packing_probes),
         out_shape=(
-            jax.ShapeDtypeStruct((half, points * steps), f32),
+            jax.ShapeDtypeStruct((half, round_up(points * steps, LANES) + rank), f32),
             jax.ShapeDtypeStruct((width, half, 2 * rank), bf16),
         ),
-        in_specs=in_vmem(4),
+        in_specs=in_vmem(5),
         out_specs=tuple(in_vmem(2)),
         compiler_params=limit(12),
         name="coeff",
-    )(prior_scale[None, :], parts, basis, basis_other)
+    )(prior_scale[None, :], deflation[None, :], parts, basis, basis_other)
     flat_other = swap(flat)
     coeff_parts = exchange(coeff)
     coeff_other = swap(coeff_parts)
     return pl.pallas_call(
         functools.partial(deflate_kernel, points=points, steps=steps, rank=rank),
         out_shape=jax.ShapeDtypeStruct((probe_count, points, steps), f32),
-        in_specs=in_smem(1) + in_vmem(8),
+        in_specs=in_smem(1) + in_vmem(6),
         out_specs=in_vmem(1)[0],
         compiler_params=limit(12),
         name="deflate",
     )(
-        core, coeff_parts, coeff_other, deflation[None, :], deflation_other[None, :],
-        flat, flat_other, basis, basis_other,
+        core, coeff_parts, coeff_other, flat, flat_other, basis, basis_other,
     )
 
 

time: 66.2 us -> 66.5 us (level)
  waiting for transfers between devices: 13 us -> 17.6 us
  blocking collectives: 24.2 us -> 22.3 us
  starting transfers between devices: 16 us -> 14.8 us
  Pallas kernels: 12.6 us -> 11.5 us
    ppermute x7, waiting for transfers between devices: 10.7 us -> 15.9 us  [local_split(): lax.ppermute(value, 'pts', [(i, i ^ relative) for i in range(width)])]
    all_to_all x2, blocking collectives: 24.2 us -> 22.3 us  [exchange(): lax.all_to_all(value, 'pts', split_axis=0, concat_axis=0, tiled=False)]
    ppermute x1 -> x0, starting transfers between devices: 1.32 us -> none  [local_split(): relayed = lax.ppermute(relayed, 'pts', [(i, i ^ 1) for i in range(width)])]
    pallas_call x1 -> x0, Pallas kernels: 1.23 us -> none  [local_split(): pl.pallas_call(stage_kernel, out_shape=pltpu.VMEM(table.shape, bf16), in_...]
    ppermute x13 -> x11, waiting for transfers between devices: 2.24 us -> 1.66 us  [swap(): return lax.ppermute(value, 'sen', [(0, 1), (1, 0)])]
    ppermute x13 -> x11, starting transfers between devices: 2.61 us -> 2.59 us  [swap(): return lax.ppermute(value, 'sen', [(0, 1), (1, 0)])]
  transfers between devices with their start and end apart: 21 -> 18, of which waited for: 6 -> 6; matrix products, arithmetic and copies ran while one was open for 0% -> 0% of each run, Pallas kernels for 15% -> 14%
where the time goes in v8:
time: 66.5 us; the launch traced here: 66.3 us
  blocking collectives  22.3 us (34%)
  waiting for transfers between devices  17.6 us (26%)
  starting transfers between devices  14.8 us (22%)
  Pallas kernels  11.5 us (17%)
    all_to_all x2, blocking collectives, exchange(): lax.all_to_all(value, 'pts', split_axis=0, concat_axis=0, tiled=False)  22.3 us
    ppermute x7, waiting for transfers between devices, local_split(): lax.ppermute(value, 'pts', [(i, i ^ relative) for i in range(width)])  15.9 us
    ppermute x7, starting transfers between devices, local_split(): lax.ppermute(value, 'pts', [(i, i ^ relative) for i in range(width)])  12.2 us
    pallas_call x1, Pallas kernels, local_split(): pl.pallas_call(functools.partial(bins_kernel, orders=orders, lean=lean, *...  5.35 us
    ppermute x11, starting transfers between devices, swap(): return lax.ppermute(value, 'sen', [(0, 1), (1, 0)])  2.59 us
    pallas_call x1, Pallas kernels, local_split(): pl.pallas_call(functools.partial(pack_kernel, order=order, lean=lean, hal...  2.16 us
    pallas_call x1, Pallas kernels, local_split(): pl.pallas_call(functools.partial(deflate_kernel, points=points, steps=ste...  1.77 us
    ppermute x11, waiting for transfers between devices, swap(): return lax.ppermute(value, 'sen', [(0, 1), (1, 0)])  1.66 us
  transfers between devices with their start and end apart: 18, of which 6 were waited for; matrix products, arithmetic and copies ran while one was open for 0% of the time, Pallas kernels for 14%

profile of v8, /device:TPU:0, one launch (start us, length us, event | category | flops | bytes accessed | tf_op | source)
XLA Modules:
  0.0 66.3 jit_solution(9211833264404647776)
XLA Ops:
  0.0 0.5 collective-permute-start.15
  0.5 0.1 pad_add_fusion.index
  0.6 0.0 copy-start.2
  0.6 2.2 %pack.1 = (bf16[42,8,128]{2,1,0:T(8,128)(2,1)S(1)}, bf16[41,8,128]{2,1,0:T(8,128)(2,1)S(1)}, bf16[41,8,128]{2,1,0:T(8,128)(2,1)S(1)}, bf16[41,8,128]{2,1,0:T(8,1...) custom-call(s32[2]{0:T(128)S(1)} %pad_add_fusion.index, ...), custom_call_target="tpu_custom_call" | custom-call | tf_op jit(solution)/shard_map/pack/pallas_call | solution.py:554
  2.7 3.6 %collective-permute-start.1 = (bf16[41,8,128]{2,1,0:T(8,128)(2,1)S(1)}, bf16[41,8,128]{2,1,0:T(8,128)(2,1)S(1)}, u32[]{:S(2)}, u32[]{:S(2)}) collective-permute-start(bf16[41,8,128]{2,1,0:T(8,128)(2,1)S(1)} %get-tuple-element.22), channel_id=1, source_target_pairs={{0,8},{2,10},{4,12},{6,14},{8,0},{10,2},{12,4},{14,6},{1,9},{3,11}... | collective-permute-start | bytes 251912 | tf_op jit(solution)/shard_map/ppermute | solution.py:592
  6.4 1.3 %collective-permute-start.2 = (bf16[41,8,128]{2,1,0:T(8,128)(2,1)S(1)}, bf16[41,8,128]{2,1,0:T(8,128)(2,1)S(1)}, u32[]{:S(2)}, u32[]{:S(2)}) collective-permute-start(bf16[41,8,128]{2,1,0:T(8,128)(2,1)S(1)} %get-tuple-element.23), channel_id=1, source_target_pairs={{0,12},{2,14},{4,8},{6,10},{8,4},{10,6},{12,0},{14,2},{1,13},{3,15... | collective-permute-start | bytes 251912 | tf_op jit(solution)/shard_map/ppermute | solution.py:592
  7.7 5.6 %collective-permute-done.1.refs_1_.refs_0_ = bf16[41,8,128]{2,1,0:T(8,128)(2,1)S(1)} collective-permute-done((bf16[41,8,128]{2,1,0:T(8,128)(2,1)S(1)}, bf16[41,8,128]{2,1,0:T(8,128)(2,1)S(1)}, u32[]{:S(2)}, u32[]{:S(2)}) %collective-permute-start.1) | collective-permute-done | bytes 84000 | tf_op jit(solution)/shard_map/ppermute | solution.py:592
  13.3 0.0 collective-permute-done.2.refs_2_.refs_1_
  13.3 1.9 %collective-permute-start.10 = (bf16[69,8,128]{2,1,0:T(8,128)(2,1)S(1)}, bf16[69,8,128]{2,1,0:T(8,128)(2,1)S(1)}, u32[]{:S(2)}, u32[]{:S(2)}) collective-permute-start(bf16[69,8,128]{2,1,0:T(8,128)(2,1)S(1)} %relay.1), channel_id=1, source_target_pairs={{0,2},{2,0},{4,6},{6,4},{8,10},{10,8},{12,14},{14,12},{1,3},{3,1},... | collective-permute-start | bytes 423944 | tf_op jit(solution)/shard_map/ppermute | solution.py:592
  15.2 3.9 %collective-permute-start.8 = (bf16[27,8,128]{2,1,0:T(8,128)(2,1)S(1)}, bf16[27,8,128]{2,1,0:T(8,128)(2,1)S(1)}, u32[]{:S(2)}, u32[]{:S(2)}) collective-permute-start(bf16[27,8,128]{2,1,0:T(8,128)(2,1)S(1)} %get-tuple-element.28), channel_id=1, source_target_pairs={{0,10},{2,8},{4,14},{6,12},{8,2},{10,0},{12,6},{14,4},{1,11},{3,9}... | collective-permute-start | bytes 165896 | tf_op jit(solution)/shard_map/ppermute | solution.py:592
  19.1 1.4 %collective-permute-start.9 = (bf16[27,8,128]{2,1,0:T(8,128)(2,1)S(1)}, bf16[27,8,128]{2,1,0:T(8,128)(2,1)S(1)}, u32[]{:S(2)}, u32[]{:S(2)}) collective-permute-start(bf16[27,8,128]{2,1,0:T(8,128)(2,1)S(1)} %get-tuple-element.29), channel_id=1, source_target_pairs={{0,14},{2,12},{4,10},{6,8},{8,6},{10,4},{12,2},{14,0},{1,15},{3,13... | collective-permute-start | bytes 165896 | tf_op jit(solution)/shard_map/ppermute | solution.py:592
  20.5 0.0 collective-permute-start.3
  20.5 1.6 %collective-permute-done.8.refs_1_ = bf16[27,8,128]{2,1,0:T(8,128)(2,1)S(1)} collective-permute-done((bf16[27,8,128]{2,1,0:T(8,128)(2,1)S(1)}, bf16[27,8,128]{2,1,0:T(8,128)(2,1)S(1)}, u32[]{:S(2)}, u32[]{:S(2)}) %collective-permute-start.8) | collective-permute-done | bytes 55328 | tf_op jit(solution)/shard_map/ppermute | solution.py:592
  22.2 0.0 collective-permute-start
  22.2 3.8 %collective-permute-done.9.refs_2_ = bf16[27,8,128]{2,1,0:T(8,128)(2,1)S(1)} collective-permute-done((bf16[27,8,128]{2,1,0:T(8,128)(2,1)S(1)}, bf16[27,8,128]{2,1,0:T(8,128)(2,1)S(1)}, u32[]{:S(2)}, u32[]{:S(2)}) %collective-permute-start.9) | collective-permute-done | bytes 55328 | tf_op jit(solution)/shard_map/ppermute | solution.py:592
  26.0 0.0 collective-permute-start.7
  26.0 0.0 collective-permute-done.3.refs_3_
  26.0 0.0 collective-permute-start.4
  26.0 0.0 collective-permute-done.10.refs_3_
  26.0 0.5 collective-permute-start.14
  26.5 4.8 %collective-permute-done.7.refs_0_ = bf16[41,8,128]{2,1,0:T(8,128)(2,1)S(1)} collective-permute-done((bf16[41,8,128]{2,1,0:T(8,128)(2,1)S(1)}, bf16[41,8,128]{2,1,0:T(8,128)(2,1)S(1)}, u32[]{:S(2)}, u32[]{:S(2)}) %collective-permute-start.7) | collective-permute-done | bytes 84000 | tf_op jit(solution)/shard_map/ppermute | solution.py:592
  31.4 0.0 collective-permute-start.5
  31.4 0.0 collective-permute-done.refs_4_.neighbour
  31.4 0.5 collective-permute-start.6
  31.9 0.0 collective-permute-done.4.refs_5_
  31.9 0.1 collective-permute-start.11
  32.0 0.7 %collective-permute-done.5.refs_6_ = bf16[41,8,128]{2,1,0:T(8,128)(2,1)S(1)} collective-permute-done((bf16[41,8,128]{2,1,0:T(8,128)(2,1)S(1)}, bf16[41,8,128]{2,1,0:T(8,128)(2,1)S(1)}, u32[]{:S(2)}, u32[]{:S(2)}) %collective-permute-start.5) | collective-permute-done | bytes 84000 | tf_op jit(solution)/shard_map/ppermute | solution.py:532
  32.7 0.2 collective-permute-start.12
  32.8 0.0 collective-permute-done.6.refs_7_
  32.8 0.4 collective-permute-start.13
  33.2 1.5 %first.1 = (f32[3,16,16,512]{3,2,1,0:T(8,128)S(1)}, f32[128,1024]{1,0:T(8,128)S(1)}) custom-call(bf16[512,1024]{1,0:T(8,128)(2,1)S(1)} %get-tuple-element.21.table, bf16[42,8,128]{2,1,0:T(8,128)(2,1)S(1)} %get-tuple-element.20.refs_0_, bf16[41,8,128]{2,1,0:T(8,128)(2,1)S(1)} %collective-permute-done.1.refs_1_.refs_0_, ...), custom_call_target="tpu_custom_call" | custom-call | tf_op jit(solution)/shard_map/first/pallas_call | solution.py:607
  34.7 0.0 collective-permute-done.12.refs_5_
  34.7 0.0 collective-permute-done.13.refs_6_
  34.7 0.0 collective-permute-done.11.refs_4_
  34.8 0.0 collective-permute-done.14.refs_7_
  34.8 0.0 copy-done.2
  34.8 0.0 copy-start
  34.8 0.0 copy-start.1
  34.8 0.0 copy-start.3
  34.8 5.3 %bins.1 = bf16[8,14,8,128]{3,2,1,0:T(8,128)(2,1)S(1)} custom-call(s32[1]{0:T(128)} %bitcast.3.index, f32[64]{0:T(128)} %noise_far.3, bf16[42,8,128]{2,1,0:T(8,128)(2,1)S(1)} %collective-permute-done.refs_4_.neighbour, bf16[512,1024]{1,0:T(8,128)(2,1)S(1)} %get-tuple-element.21.table, f32[1,512]{1,0:T(1,128)S(1)} %copy-done.2, ...), custom_call_target="tpu_custom_call" | custom-call | tf_op jit(solution)/shard_map/bins/pallas_call | solution.py:620
  40.2 0.0 collective-permute-done.15.basis_other
  40.2 11.8 %all_to_all.10.parts = bf16[8,14,8,128]{3,2,1,0:T(8,128)(2,1)S(1)} all-to-all(bf16[8,14,8,128]{3,2,1,0:T(8,128)(2,1)S(1)} %bins.1), channel_id=1, replica_groups=mesh['grp'=2,'pts'=8,'sen'=2] {'pts'}, dimensions={0} | all-to-all | bytes 458752 | tf_op jit(solution)/shard_map/all_to_all | solution.py:535
  52.0 0.0 copy-done
  52.0 0.0 copy-done.1
  52.0 0.0 copy-done.3
  52.0 0.6 coeff.1
  52.6 10.5 %all_to_all.11.parts_own = bf16[8,8,1024]{2,1,0:T(8,128)(2,1)S(1)} all-to-all(bf16[8,8,1024]{2,1,0:T(8,128)(2,1)S(1)} %get-tuple-element.33), channel_id=1, replica_groups=mesh['grp'=2,'pts'=8,'sen'=2] {'pts'}, dimensions={0} | all-to-all | bytes 262144 | tf_op jit(solution)/shard_map/all_to_all | solution.py:535
  63.1 0.0 collective-permute-start.16
  63.1 0.5 collective-permute-start.17
  63.6 0.9 %collective-permute-done.17.flat_other = f32[8,2304]{1,0:T(8,128)S(1)} collective-permute-done((f32[8,2304]{1,0:T(8,128)S(1)}, f32[8,2304]{1,0:T(8,128)S(1)}, u32[]{:S(2)}, u32[]{:S(2)}) %collective-permute-start.17) | collective-permute-done | bytes 73760 | tf_op jit(solution)/shard_map/ppermute | solution.py:532
  64.6 0.0 collective-permute-done.16.parts_other
  64.6 1.8 %deflate.1 = f32[16,4,420]{2,1,0:T(4,128)} custom-call(s32[1]{0:T(128)} %bitcast.core, bf16[8,8,1024]{2,1,0:T(8,128)(2,1)S(1)} %all_to_all.11.parts_own, bf16[8,8,1024]{2,1,0:T(8,128)(2,1)S(1)} %collective-permute-done.16.parts_other, f32[8,2304]{1,0:T(8,128)S(1)} %get-tuple-element.34.flat_own, f32[8,2304]{1,0:T(8,128)S(1)} %collective-permute-done.17.flat_other, ...), custom_call_target="tpu_custom_call" | custom-call | tf_op jit(solution)/shard_map/deflate/pallas_call | solution.py:657
  (1 shorter events, 0.0 us)
Async XLA Ops:
  0.0 40.2 %collective-permute-start.15 = (bf16[1680,512]{1,0:T(8,128)(2,1)}, bf16[1680,512]{1,0:T(8,128)(2,1)S(1)}, u32[]{:S(2)}, u32[]{:S(2)}) collective-permute-start(bf16[1680,512]{1,0:T(8,128)(2,1)} %basis_own.3), channel_id=1, source_target_pairs={{0,1},{1,0},{2,3},{3,2},{4,5},{5,4},{6,7},{7,6},{8,9},{9,8},{10,11... | collective-permute-start | bytes 5160968 | tf_op jit(solution)/shard_map/ppermute | solution.py:532
  0.6 34.2 %copy-start.2 = (f32[1,512]{1,0:T(1,128)S(1)}, f32[1,512]{1,0:T(1,128)}, u32[]{:S(2)}) copy-start(f32[1,512]{1,0:T(1,128)} %constant.13.clone.weights) | copy-start | bytes 6148
  2.7 10.6 %collective-permute-start.1 = (bf16[41,8,128]{2,1,0:T(8,128)(2,1)S(1)}, bf16[41,8,128]{2,1,0:T(8,128)(2,1)S(1)}, u32[]{:S(2)}, u32[]{:S(2)}) collective-permute-start(bf16[41,8,128]{2,1,0:T(8,128)(2,1)S(1)} %get-tuple-element.22), channel_id=1, source_target_pairs={{0,8},{2,10},{4,12},{6,14},{8,0},{10,2},{12,4},{14,6},{1,9},{3,11}... | collective-permute-start | bytes 251912 | tf_op jit(solution)/shard_map/ppermute | solution.py:592
  6.4 6.9 %collective-permute-start.2 = (bf16[41,8,128]{2,1,0:T(8,128)(2,1)S(1)}, bf16[41,8,128]{2,1,0:T(8,128)(2,1)S(1)}, u32[]{:S(2)}, u32[]{:S(2)}) collective-permute-start(bf16[41,8,128]{2,1,0:T(8,128)(2,1)S(1)} %get-tuple-element.23), channel_id=1, source_target_pairs={{0,12},{2,14},{4,8},{6,10},{8,4},{10,6},{12,0},{14,2},{1,13},{3,15... | collective-permute-start | bytes 251912 | tf_op jit(solution)/shard_map/ppermute | solution.py:592
  13.3 12.7 %collective-permute-start.10 = (bf16[69,8,128]{2,1,0:T(8,128)(2,1)S(1)}, bf16[69,8,128]{2,1,0:T(8,128)(2,1)S(1)}, u32[]{:S(2)}, u32[]{:S(2)}) collective-permute-start(bf16[69,8,128]{2,1,0:T(8,128)(2,1)S(1)} %relay.1), channel_id=1, source_target_pairs={{0,2},{2,0},{4,6},{6,4},{8,10},{10,8},{12,14},{14,12},{1,3},{3,1},... | collective-permute-start | bytes 423944 | tf_op jit(solution)/shard_map/ppermute | solution.py:592
  15.2 6.9 %collective-permute-start.8 = (bf16[27,8,128]{2,1,0:T(8,128)(2,1)S(1)}, bf16[27,8,128]{2,1,0:T(8,128)(2,1)S(1)}, u32[]{:S(2)}, u32[]{:S(2)}) collective-permute-start(bf16[27,8,128]{2,1,0:T(8,128)(2,1)S(1)} %get-tuple-element.28), channel_id=1, source_target_pairs={{0,10},{2,8},{4,14},{6,12},{8,2},{10,0},{12,6},{14,4},{1,11},{3,9}... | collective-permute-start | bytes 165896 | tf_op jit(solution)/shard_map/ppermute | solution.py:592
  19.1 6.9 %collective-permute-start.9 = (bf16[27,8,128]{2,1,0:T(8,128)(2,1)S(1)}, bf16[27,8,128]{2,1,0:T(8,128)(2,1)S(1)}, u32[]{:S(2)}, u32[]{:S(2)}) collective-permute-start(bf16[27,8,128]{2,1,0:T(8,128)(2,1)S(1)} %get-tuple-element.29), channel_id=1, source_target_pairs={{0,14},{2,12},{4,10},{6,8},{8,6},{10,4},{12,2},{14,0},{1,15},{3,13... | collective-permute-start | bytes 165896 | tf_op jit(solution)/shard_map/ppermute | solution.py:592
  20.5 5.5 %collective-permute-start.3 = (bf16[41,8,128]{2,1,0:T(8,128)(2,1)S(1)}, bf16[41,8,128]{2,1,0:T(8,128)(2,1)S(1)}, u32[]{:S(2)}, u32[]{:S(2)}) collective-permute-start(bf16[41,8,128]{2,1,0:T(8,128)(2,1)S(1)} %get-tuple-element.24), channel_id=1, source_target_pairs={{0,4},{2,6},{4,0},{6,2},{8,12},{10,14},{12,8},{14,10},{1,5},{3,7},... | collective-permute-start | bytes 251912 | tf_op jit(solution)/shard_map/ppermute | solution.py:592
  22.2 9.2 %collective-permute-start = (bf16[42,8,128]{2,1,0:T(8,128)(2,1)S(1)}, bf16[42,8,128]{2,1,0:T(8,128)(2,1)S(1)}, u32[]{:S(2)}, u32[]{:S(2)}) collective-permute-start(bf16[42,8,128]{2,1,0:T(8,128)(2,1)S(1)} %get-tuple-element.20.refs_0_), channel_id=1, source_target_pairs={{0,1},{1,0},{2,3},{3,2},{4,5},{5,4},{6,7},{7,6},{8,9},{9,8},{10,11... | collective-permute-start | bytes 258056 | tf_op jit(solution)/shard_map/ppermute | solution.py:532
  26.0 5.4 %collective-permute-start.7 = (bf16[41,8,128]{2,1,0:T(8,128)(2,1)S(1)}, bf16[41,8,128]{2,1,0:T(8,128)(2,1)S(1)}, u32[]{:S(2)}, u32[]{:S(2)}) collective-permute-start(bf16[41,8,128]{2,1,0:T(8,128)(2,1)S(1)} %get-tuple-element.27), channel_id=1, source_target_pairs={{0,6},{2,4},{4,2},{6,0},{8,14},{10,12},{12,10},{14,8},{1,7},{3,5},... | collective-permute-start | bytes 251912 | tf_op jit(solution)/shard_map/ppermute | solution.py:592
  26.0 5.9 %collective-permute-start.4 = (bf16[41,8,128]{2,1,0:T(8,128)(2,1)S(1)}, bf16[41,8,128]{2,1,0:T(8,128)(2,1)S(1)}, u32[]{:S(2)}, u32[]{:S(2)}) collective-permute-start(bf16[41,8,128]{2,1,0:T(8,128)(2,1)S(1)} %collective-permute-done.1.refs_1_.refs_0_), channel_id=1, source_target_pairs={{0,1},{1,0},{2,3},{3,2},{4,5},{5,4},{6,7},{7,6},{8,9},{9,8},{10,11... | collective-permute-start | bytes 251912 | tf_op jit(solution)/shard_map/ppermute | solution.py:532
  26.0 8.7 %collective-permute-start.14 = (bf16[69,8,128]{2,1,0:T(8,128)(2,1)S(1)}, bf16[69,8,128]{2,1,0:T(8,128)(2,1)S(1)}, u32[]{:S(2)}, u32[]{:S(2)}) collective-permute-start(bf16[69,8,128]{2,1,0:T(8,128)(2,1)S(1)} %collective-permute-done.10.refs_3_), channel_id=1, source_target_pairs={{0,1},{1,0},{2,3},{3,2},{4,5},{5,4},{6,7},{7,6},{8,9},{9,8},{10,11... | collective-permute-start | bytes 423944 | tf_op jit(solution)/shard_map/ppermute | solution.py:532
  31.4 1.3 %collective-permute-start.5 = (bf16[41,8,128]{2,1,0:T(8,128)(2,1)S(1)}, bf16[41,8,128]{2,1,0:T(8,128)(2,1)S(1)}, u32[]{:S(2)}, u32[]{:S(2)}) collective-permute-start(bf16[41,8,128]{2,1,0:T(8,128)(2,1)S(1)} %collective-permute-done.2.refs_2_.refs_1_), channel_id=1, source_target_pairs={{0,1},{1,0},{2,3},{3,2},{4,5},{5,4},{6,7},{7,6},{8,9},{9,8},{10,11... | collective-permute-start | bytes 251912 | tf_op jit(solution)/shard_map/ppermute | solution.py:532
  31.4 1.4 %collective-permute-start.6 = (bf16[41,8,128]{2,1,0:T(8,128)(2,1)S(1)}, bf16[41,8,128]{2,1,0:T(8,128)(2,1)S(1)}, u32[]{:S(2)}, u32[]{:S(2)}) collective-permute-start(bf16[41,8,128]{2,1,0:T(8,128)(2,1)S(1)} %collective-permute-done.3.refs_3_), channel_id=1, source_target_pairs={{0,1},{1,0},{2,3},{3,2},{4,5},{5,4},{6,7},{7,6},{8,9},{9,8},{10,11... | collective-permute-start | bytes 251912 | tf_op jit(solution)/shard_map/ppermute | solution.py:532
  31.9 2.9 %collective-permute-start.11 = (bf16[41,8,128]{2,1,0:T(8,128)(2,1)S(1)}, bf16[41,8,128]{2,1,0:T(8,128)(2,1)S(1)}, u32[]{:S(2)}, u32[]{:S(2)}) collective-permute-start(bf16[41,8,128]{2,1,0:T(8,128)(2,1)S(1)} %collective-permute-done.7.refs_0_), channel_id=1, source_target_pairs={{0,1},{1,0},{2,3},{3,2},{4,5},{5,4},{6,7},{7,6},{8,9},{9,8},{10,11... | collective-permute-start | bytes 251912 | tf_op jit(solution)/shard_map/ppermute | solution.py:532
  32.7 2.1 %collective-permute-start.12 = (bf16[27,8,128]{2,1,0:T(8,128)(2,1)S(1)}, bf16[27,8,128]{2,1,0:T(8,128)(2,1)S(1)}, u32[]{:S(2)}, u32[]{:S(2)}) collective-permute-start(bf16[27,8,128]{2,1,0:T(8,128)(2,1)S(1)} %collective-permute-done.8.refs_1_), channel_id=1, source_target_pairs={{0,1},{1,0},{2,3},{3,2},{4,5},{5,4},{6,7},{7,6},{8,9},{9,8},{10,11... | collective-permute-start | bytes 165896 | tf_op jit(solution)/shard_map/ppermute | solution.py:532
  32.8 1.9 %collective-permute-start.13 = (bf16[27,8,128]{2,1,0:T(8,128)(2,1)S(1)}, bf16[27,8,128]{2,1,0:T(8,128)(2,1)S(1)}, u32[]{:S(2)}, u32[]{:S(2)}) collective-permute-start(bf16[27,8,128]{2,1,0:T(8,128)(2,1)S(1)} %collective-permute-done.9.refs_2_), channel_id=1, source_target_pairs={{0,1},{1,0},{2,3},{3,2},{4,5},{5,4},{6,7},{7,6},{8,9},{9,8},{10,11... | collective-permute-start | bytes 165896 | tf_op jit(solution)/shard_map/ppermute | solution.py:532
  34.8 17.2 %copy-start = (bf16[1680,512]{1,0:T(8,128)(2,1)S(1)}, bf16[1680,512]{1,0:T(8,128)(2,1)}, u32[]{:S(2)}) copy-start(bf16[1680,512]{1,0:T(8,128)(2,1)} %basis_own.3) | copy-start | bytes 5160964
  34.8 17.2 %copy-start.1 = (f32[512]{0:T(512)S(1)}, f32[512]{0:T(512)}, u32[]{:S(2)}) copy-start(f32[512]{0:T(512)} %param.13) | copy-start | bytes 6148
  34.8 17.2 %copy-start.3 = (f32[4]{0:T(128)S(1)}, f32[4]{0:T(128)}, u32[]{:S(2)}) copy-start(f32[4]{0:T(128)} %prior_far.1) | copy-start | bytes 52
  63.1 1.5 %collective-permute-start.16 = (bf16[8,8,1024]{2,1,0:T(8,128)(2,1)S(1)}, bf16[8,8,1024]{2,1,0:T(8,128)(2,1)S(1)}, u32[]{:S(2)}, u32[]{:S(2)}) collective-permute-start(bf16[8,8,1024]{2,1,0:T(8,128)(2,1)S(1)} %all_to_all.11.parts_own), channel_id=1, source_target_pairs={{0,1},{1,0},{2,3},{3,2},{4,5},{5,4},{6,7},{7,6},{8,9},{9,8},{10,11... | collective-permute-start | bytes 393224 | tf_op jit(solution)/shard_map/ppermute | solution.py:532
  63.1 1.5 %collective-permute-start.17 = (f32[8,2304]{1,0:T(8,128)S(1)}, f32[8,2304]{1,0:T(8,128)S(1)}, u32[]{:S(2)}, u32[]{:S(2)}) collective-permute-start(f32[8,2304]{1,0:T(8,128)S(1)} %get-tuple-element.34.flat_own), channel_id=1, source_target_pairs={{0,1},{1,0},{2,3},{3,2},{4,5},{5,4},{6,7},{7,6},{8,9},{9,8},{10,11... | collective-permute-start | bytes 221192 | tf_op jit(solution)/shard_map/ppermute | solution.py:532

commit v9 on v8

--- a/solution.py
+++ b/solution.py
@@ -338,7 +338,7 @@
 
 
 def bins_kernel(
-    index, noise_far, neighbour, table, weights, kern_first, data_first, *refs,
+    index, noise_far, neighbour, table, weights, kern_first, data_first, relayed, *refs,
     orders, lean, points, sens, half, wide, packing, packing_probes,
 ):
     count = len(orders[1])
@@ -352,8 +352,7 @@
     probes = []
     for relative, (own, _) in zip(orders[1], sources):
         if relative in lean:
-            behind = packing.tiles + (1 + lean.index(relative)) * packing_probes.tiles
-            probes.append((sources[orders[1].index(1)][0], behind))
+            probes.append((relayed, lean.index(relative) * packing_probes.tiles))
         else:
             probes.append((own, packing.tiles))
     spectra(probes, table, spec, rows, packing=packing_probes, points=points, half=half, wide=wide)
@@ -478,24 +477,20 @@
 
 
 def split_order(width):
-    near = list(range(2, width // 2))
-    far = list(range(width // 2, width))
-    order = [0] + [r for r in far if r % 2 == 0] + near + [r for r in far if r % 2] + [1]
-    return order[: width // 2], order[width // 2 :]
+    middle, half = width // 4, width // 2
+    soon = [0, half, 1, middle]
+    return soon, [r for r in (half + middle, half + 1, half + middle + 1, middle + 1)]
 
 
 def lean_partners(width):
     return [r for r in range(width // 2, width) if r % 2]
 
 
-def relay_kernel(ours, *refs, first_tile):
+def relay_kernel(*refs, first_tile):
     sources, out = refs[:-1], refs[-1]
-    base = ours.shape[0]
-    out[:base] = ours[...]
-    for source in sources:
-        count = source.shape[0] - first_tile
-        out[base : base + count] = source[first_tile:]
-        base += count
+    count = out.shape[0] // len(sources)
+    for n, source in enumerate(sources):
+        out[n * count : (n + 1) * count] = source[first_tile:]
 
 
 def kept(space, *values):
@@ -579,19 +574,19 @@
     blocks = {}
     others = {}
     for relative, value in zip(order, sent):
-        if relative == 1:
-            value = pl.pallas_call(
-                functools.partial(relay_kernel, first_tile=packing.tiles),
-                out_shape=chunk(both + len(lean) * packing_probes.tiles),
-                in_specs=in_vmem(1 + len(lean)),
-                out_specs=in_vmem(1)[0],
-                compiler_params=limit(2),
-                name="relay",
-            )(value, *[blocks[r ^ 1] for r in lean])
         if relative:
             value = lax.ppermute(value, "pts", [(i, i ^ relative) for i in range(width)])
         blocks[relative] = value
         others[relative] = swap(value)
+    relayed = pl.pallas_call(
+        functools.partial(relay_kernel, first_tile=packing.tiles),
+        out_shape=chunk(len(lean) * packing_probes.tiles),
+        in_specs=in_vmem(len(lean)),
+        out_specs=in_vmem(1)[0],
+        compiler_params=limit(2),
+        name="relay",
+    )(*[blocks[r ^ 1] for r in lean])
+    relayed = lax.ppermute(relayed, "pts", [(i, i ^ 1) for i in range(width)])
     basis_other = swap(basis)
 
     def scratch(count):
@@ -620,7 +615,7 @@
     back = pl.pallas_call(
         functools.partial(bins_kernel, orders=orders, lean=lean, **sizes),
         out_shape=jax.ShapeDtypeStruct((width, packing_probes.tiles, half, LANES), bf16),
-        in_specs=in_smem(1) + [in_hbm] + in_vmem(5 + 2 * count),
+        in_specs=in_smem(1) + [in_hbm] + in_vmem(6 + 2 * count),
         out_specs=in_vmem(1)[0],
         scratch_shapes=[pltpu.VMEM((3, count * points, 2 * sens, wide), f32)]
         + scratch(count)
@@ -635,7 +630,7 @@
         name="bins",
     )(
         me, *kept(pltpu.HBM, noise_weight), others[0], table, weights, kern_first, data_first,
-        *ready(orders[1]),
+        relayed, *ready(orders[1]),
     )
     back, basis_other = lax.optimization_barrier((back, basis_other))
     basis, basis_other = kept(pltpu.VMEM, basis, basis_other)

time: 66.5 us -> 63.4 us (0.953)
  waiting for transfers between devices: 17.6 us -> 11.6 us
  starting transfers between devices: 14.8 us -> 17.6 us
    ppermute x7, waiting for transfers between devices: 15.9 us -> 8.85 us  [local_split(): lax.ppermute(value, 'pts', [(i, i ^ relative) for i in range(width)])]
    ppermute x0 -> x1, starting transfers between devices: none -> 1.73 us  [local_split(): relayed = lax.ppermute(relayed, 'pts', [(i, i ^ 1) for i in range(width)])]
    ppermute x7, starting transfers between devices: 12.2 us -> 13.7 us  [local_split(): lax.ppermute(value, 'pts', [(i, i ^ relative) for i in range(width)])]
    ppermute x0 -> x1, waiting for transfers between devices: none -> 0.88 us  [local_split(): relayed = lax.ppermute(relayed, 'pts', [(i, i ^ 1) for i in range(width)])]
  transfers between devices with their start and end apart: 18 -> 19, of which waited for: 6 -> 7; matrix products, arithmetic and copies ran while one was open for 0% -> 0% of each run, Pallas kernels for 14% -> 14%
where the time goes in v9:
time: 63.4 us; the launch traced here: 63.2 us
  blocking collectives  22.4 us (35%)
  starting transfers between devices  17.6 us (28%)
  waiting for transfers between devices  11.6 us (18%)
  Pallas kernels  11.5 us (18%)
    all_to_all x2, blocking collectives, exchange(): lax.all_to_all(value, 'pts', split_axis=0, concat_axis=0, tiled=False)  22.4 us
    ppermute x7, starting transfers between devices, local_split(): lax.ppermute(value, 'pts', [(i, i ^ relative) for i in range(width)])  13.7 us
    ppermute x7, waiting for transfers between devices, local_split(): lax.ppermute(value, 'pts', [(i, i ^ relative) for i in range(width)])  8.85 us
    pallas_call x1, Pallas kernels, local_split(): pl.pallas_call(functools.partial(bins_kernel, orders=orders, lean=lean, *...  5.35 us
    pallas_call x1, Pallas kernels, local_split(): pl.pallas_call(functools.partial(pack_kernel, order=order, lean=lean, hal...  2.16 us
    ppermute x11, starting transfers between devices, swap(): return lax.ppermute(value, 'sen', [(0, 1), (1, 0)])  2.1 us
    ppermute x11, waiting for transfers between devices, swap(): return lax.ppermute(value, 'sen', [(0, 1), (1, 0)])  1.86 us
    pallas_call x1, Pallas kernels, local_split(): pl.pallas_call(functools.partial(deflate_kernel, points=points, steps=ste...  1.77 us
  transfers between devices with their start and end apart: 19, of which 7 were waited for; matrix products, arithmetic and copies ran while one was open for 0% of the time, Pallas kernels for 14%

profile of v9, /device:TPU:0, one launch (start us, length us, event | category | flops | bytes accessed | tf_op | source)
XLA Modules:
  0.0 63.2 jit_solution(11534933859814243732)
XLA Ops:
  0.0 0.5 collective-permute-start.16
  0.5 0.1 pad_add_fusion.index
  0.6 0.0 copy-start.2
  0.6 2.2 %pack.1 = (bf16[42,8,128]{2,1,0:T(8,128)(2,1)S(1)}, bf16[41,8,128]{2,1,0:T(8,128)(2,1)S(1)}, bf16[41,8,128]{2,1,0:T(8,128)(2,1)S(1)}, bf16[41,8,128]{2,1,0:T(8,1...) custom-call(s32[2]{0:T(128)S(1)} %pad_add_fusion.index, ...), custom_call_target="tpu_custom_call" | custom-call | tf_op jit(solution)/shard_map/pack/pallas_call | solution.py:549
  2.7 3.6 %collective-permute-start.1 = (bf16[41,8,128]{2,1,0:T(8,128)(2,1)S(1)}, bf16[41,8,128]{2,1,0:T(8,128)(2,1)S(1)}, u32[]{:S(2)}, u32[]{:S(2)}) collective-permute-start(bf16[41,8,128]{2,1,0:T(8,128)(2,1)S(1)} %get-tuple-element.22), channel_id=1, source_target_pairs={{0,8},{2,10},{4,12},{6,14},{8,0},{10,2},{12,4},{14,6},{1,9},{3,11}... | collective-permute-start | bytes 251912 | tf_op jit(solution)/shard_map/ppermute | solution.py:578
  6.4 1.5 %collective-permute-start.2 = (bf16[41,8,128]{2,1,0:T(8,128)(2,1)S(1)}, bf16[41,8,128]{2,1,0:T(8,128)(2,1)S(1)}, u32[]{:S(2)}, u32[]{:S(2)}) collective-permute-start(bf16[41,8,128]{2,1,0:T(8,128)(2,1)S(1)} %get-tuple-element.23), channel_id=1, source_target_pairs={{0,2},{2,0},{4,6},{6,4},{8,10},{10,8},{12,14},{14,12},{1,3},{3,1},... | collective-permute-start | bytes 251912 | tf_op jit(solution)/shard_map/ppermute | solution.py:578
  7.9 0.0 collective-permute-start.9
  7.9 4.8 %collective-permute-start.10 = (bf16[27,8,128]{2,1,0:T(8,128)(2,1)S(1)}, bf16[27,8,128]{2,1,0:T(8,128)(2,1)S(1)}, u32[]{:S(2)}, u32[]{:S(2)}) collective-permute-start(bf16[27,8,128]{2,1,0:T(8,128)(2,1)S(1)} %get-tuple-element.29), channel_id=1, source_target_pairs={{0,14},{2,12},{4,10},{6,8},{8,6},{10,4},{12,2},{14,0},{1,15},{3,13... | collective-permute-start | bytes 165896 | tf_op jit(solution)/shard_map/ppermute | solution.py:578
  12.7 3.8 %collective-permute-done.9.refs_1_ = bf16[27,8,128]{2,1,0:T(8,128)(2,1)S(1)} collective-permute-done((bf16[27,8,128]{2,1,0:T(8,128)(2,1)S(1)}, bf16[27,8,128]{2,1,0:T(8,128)(2,1)S(1)}, u32[]{:S(2)}, u32[]{:S(2)}) %collective-permute-start.9) | collective-permute-done | bytes 55328 | tf_op jit(solution)/shard_map/ppermute | solution.py:578
  16.5 0.0 collective-permute-start.3
  16.5 0.0 collective-permute-done.10.refs_2_
  16.5 0.0 collective-permute-start
  16.5 0.0 collective-permute-done.1.refs_1_.refs_0_
  16.5 3.0 %collective-permute-start.7 = (bf16[41,8,128]{2,1,0:T(8,128)(2,1)S(1)}, bf16[41,8,128]{2,1,0:T(8,128)(2,1)S(1)}, u32[]{:S(2)}, u32[]{:S(2)}) collective-permute-start(bf16[41,8,128]{2,1,0:T(8,128)(2,1)S(1)} %get-tuple-element.27), channel_id=1, source_target_pairs={{0,12},{2,14},{4,8},{6,10},{8,4},{10,6},{12,0},{14,2},{1,13},{3,15... | collective-permute-start | bytes 251912 | tf_op jit(solution)/shard_map/ppermute | solution.py:578
  19.5 0.0 collective-permute-done.2.refs_2_
  19.5 0.8 %collective-permute-start.11 = (bf16[41,8,128]{2,1,0:T(8,128)(2,1)S(1)}, bf16[41,8,128]{2,1,0:T(8,128)(2,1)S(1)}, u32[]{:S(2)}, u32[]{:S(2)}) collective-permute-start(bf16[41,8,128]{2,1,0:T(8,128)(2,1)S(1)} %get-tuple-element.30), channel_id=1, source_target_pairs={{0,6},{2,4},{4,2},{6,0},{8,14},{10,12},{12,10},{14,8},{1,7},{3,5},... | collective-permute-start | bytes 251912 | tf_op jit(solution)/shard_map/ppermute | solution.py:578
  20.3 0.7 %collective-permute-done.3.refs_3_ = bf16[41,8,128]{2,1,0:T(8,128)(2,1)S(1)} collective-permute-done((bf16[41,8,128]{2,1,0:T(8,128)(2,1)S(1)}, bf16[41,8,128]{2,1,0:T(8,128)(2,1)S(1)}, u32[]{:S(2)}, u32[]{:S(2)}) %collective-permute-start.3) | collective-permute-done | bytes 84000 | tf_op jit(solution)/shard_map/ppermute | solution.py:578
  20.9 0.0 collective-permute-start.4
  20.9 3.6 %collective-permute-done.7.refs_1_.refs_0_ = bf16[41,8,128]{2,1,0:T(8,128)(2,1)S(1)} collective-permute-done((bf16[41,8,128]{2,1,0:T(8,128)(2,1)S(1)}, bf16[41,8,128]{2,1,0:T(8,128)(2,1)S(1)}, u32[]{:S(2)}, u32[]{:S(2)}) %collective-permute-start.7) | collective-permute-done | bytes 84000 | tf_op jit(solution)/shard_map/ppermute | solution.py:578
  24.5 0.0 collective-permute-start.5
  24.5 0.8 %collective-permute-done.11.refs_3_ = bf16[41,8,128]{2,1,0:T(8,128)(2,1)S(1)} collective-permute-done((bf16[41,8,128]{2,1,0:T(8,128)(2,1)S(1)}, bf16[41,8,128]{2,1,0:T(8,128)(2,1)S(1)}, u32[]{:S(2)}, u32[]{:S(2)}) %collective-permute-start.11) | collective-permute-done | bytes 84000 | tf_op jit(solution)/shard_map/ppermute | solution.py:578
  25.4 0.0 collective-permute-start.6
  25.4 0.0 collective-permute-done.refs_4_.neighbour
  25.4 0.5 collective-permute-start.13
  25.9 0.9 %collective-permute-done.13.refs_5_ = bf16[27,8,128]{2,1,0:T(8,128)(2,1)S(1)} collective-permute-done((bf16[27,8,128]{2,1,0:T(8,128)(2,1)S(1)}, bf16[27,8,128]{2,1,0:T(8,128)(2,1)S(1)}, u32[]{:S(2)}, u32[]{:S(2)}) %collective-permute-start.13) | collective-permute-done | bytes 55328 | tf_op jit(solution)/shard_map/ppermute | solution.py:527
  26.8 0.4 collective-permute-start.12
  27.1 0.0 collective-permute-done.4.refs_5_
  27.1 0.2 collective-permute-start.15
  27.3 0.0 collective-permute-done.5.refs_6_
  27.3 1.7 %collective-permute-start.8 = (bf16[28,8,128]{2,1,0:T(8,128)(2,1)S(1)}, bf16[28,8,128]{2,1,0:T(8,128)(2,1)S(1)}, u32[]{:S(2)}, u32[]{:S(2)}) collective-permute-start(bf16[28,8,128]{2,1,0:T(8,128)(2,1)S(1)} %relay.1), channel_id=1, source_target_pairs={{0,2},{2,0},{4,6},{6,4},{8,10},{10,8},{12,14},{14,12},{1,3},{3,1},... | collective-permute-start | bytes 172040 | tf_op jit(solution)/shard_map/ppermute | solution.py:589
  29.0 0.0 collective-permute-done.6.refs_7_
  29.0 0.1 collective-permute-start.14
  29.1 1.5 %first.1 = (f32[3,16,16,512]{3,2,1,0:T(8,128)S(1)}, f32[128,1024]{1,0:T(8,128)S(1)}) custom-call(bf16[512,1024]{1,0:T(8,128)(2,1)S(1)} %get-tuple-element.21.table, bf16[42,8,128]{2,1,0:T(8,128)(2,1)S(1)} %get-tuple-element.20.refs_0_, bf16[41,8,128]{2,1,0:T(8,128)(2,1)S(1)} %collective-permute-done.1.refs_1_.refs_0_, ...), custom_call_target="tpu_custom_call" | custom-call | tf_op jit(solution)/shard_map/first/pallas_call | solution.py:602
  30.6 0.0 collective-permute-done.14.refs_6_
  30.7 0.9 %collective-permute-done.8.relayed = bf16[28,8,128]{2,1,0:T(8,128)(2,1)S(1)} collective-permute-done((bf16[28,8,128]{2,1,0:T(8,128)(2,1)S(1)}, bf16[28,8,128]{2,1,0:T(8,128)(2,1)S(1)}, u32[]{:S(2)}, u32[]{:S(2)}) %collective-permute-start.8) | collective-permute-done | bytes 57376 | tf_op jit(solution)/shard_map/ppermute | solution.py:589
  31.5 0.0 collective-permute-done.12.refs_4_
  31.5 0.0 collective-permute-done.15.refs_7_
  31.5 0.0 copy-done.2
  31.5 0.0 copy-start
  31.6 0.0 copy-start.1
  31.6 0.0 copy-start.3
  31.6 5.3 %bins.1 = bf16[8,14,8,128]{3,2,1,0:T(8,128)(2,1)S(1)} custom-call(s32[1]{0:T(128)} %bitcast.3.index, f32[64]{0:T(128)} %noise_far.3, bf16[42,8,128]{2,1,0:T(8,128)(2,1)S(1)} %collective-permute-done.refs_4_.neighbour, bf16[512,1024]{1,0:T(8,128)(2,1)S(1)} %get-tuple-element.21.table, f32[1,512]{1,0:T(1,128)S(1)} %copy-done.2, ...), custom_call_target="tpu_custom_call" | custom-call | tf_op jit(solution)/shard_map/bins/pallas_call | solution.py:615
  36.9 0.0 collective-permute-done.16.basis_other
  37.0 12.1 %all_to_all.10.parts = bf16[8,14,8,128]{3,2,1,0:T(8,128)(2,1)S(1)} all-to-all(bf16[8,14,8,128]{3,2,1,0:T(8,128)(2,1)S(1)} %bins.1), channel_id=1, replica_groups=mesh['grp'=2,'pts'=8,'sen'=2] {'pts'}, dimensions={0} | all-to-all | bytes 458752 | tf_op jit(solution)/shard_map/all_to_all | solution.py:530
  49.0 0.0 copy-done
  49.0 0.0 copy-done.1
  49.0 0.0 copy-done.3
  49.0 0.6 %coeff.1 = (f32[8,2304]{1,0:T(8,128)S(1)}, bf16[8,8,1024]{2,1,0:T(8,128)(2,1)S(1)}) custom-call(f32[1,4]{1,0:T(1,128)S(1)} %bitcast.6, f32[1,512]{1,0:T(1,128)S(1)} %bitcast.5, bf16[8,14,8,128]{3,2,1,0:T(8,128)(2,1)S(1)} %all_to_all.10.parts, bf16[1680,512]{1,0:T(8,128)(2,1)S(1)} %copy-done, bf16[1680,512]{1,0:T(8,128)(2,1)S(1)} %collective-permute-done.16.basis_other), custom_call_target="tpu_custom_call" | custom-call | tf_op jit(solution)/shard_map/coeff/pallas_call | solution.py:638
  49.7 10.3 %all_to_all.11.parts_own = bf16[8,8,1024]{2,1,0:T(8,128)(2,1)S(1)} all-to-all(bf16[8,8,1024]{2,1,0:T(8,128)(2,1)S(1)} %get-tuple-element.33), channel_id=1, replica_groups=mesh['grp'=2,'pts'=8,'sen'=2] {'pts'}, dimensions={0} | all-to-all | bytes 262144 | tf_op jit(solution)/shard_map/all_to_all | solution.py:530
  60.0 0.0 collective-permute-start.17
  60.0 0.5 collective-permute-start.18
  60.5 0.9 %collective-permute-done.18.flat_other = f32[8,2304]{1,0:T(8,128)S(1)} collective-permute-done((f32[8,2304]{1,0:T(8,128)S(1)}, f32[8,2304]{1,0:T(8,128)S(1)}, u32[]{:S(2)}, u32[]{:S(2)}) %collective-permute-start.18) | collective-permute-done | bytes 73760 | tf_op jit(solution)/shard_map/ppermute | solution.py:527
  61.4 0.0 collective-permute-done.17.parts_other
  61.4 1.8 %deflate.1 = f32[16,4,420]{2,1,0:T(4,128)} custom-call(s32[1]{0:T(128)} %bitcast.core, bf16[8,8,1024]{2,1,0:T(8,128)(2,1)S(1)} %all_to_all.11.parts_own, bf16[8,8,1024]{2,1,0:T(8,128)(2,1)S(1)} %collective-permute-done.17.parts_other, f32[8,2304]{1,0:T(8,128)S(1)} %get-tuple-element.34.flat_own, f32[8,2304]{1,0:T(8,128)S(1)} %collective-permute-done.18.flat_other, ...), custom_call_target="tpu_custom_call" | custom-call | tf_op jit(solution)/shard_map/deflate/pallas_call | solution.py:652
  (1 shorter events, 0.0 us)
Async XLA Ops:
  0.0 36.9 %collective-permute-start.16 = (bf16[1680,512]{1,0:T(8,128)(2,1)}, bf16[1680,512]{1,0:T(8,128)(2,1)S(1)}, u32[]{:S(2)}, u32[]{:S(2)}) collective-permute-start(bf16[1680,512]{1,0:T(8,128)(2,1)} %basis_own.3), channel_id=1, source_target_pairs={{0,1},{1,0},{2,3},{3,2},{4,5},{5,4},{6,7},{7,6},{8,9},{9,8},{10,11... | collective-permute-start | bytes 5160968 | tf_op jit(solution)/shard_map/ppermute | solution.py:527
  0.6 31.0 %copy-start.2 = (f32[1,512]{1,0:T(1,128)S(1)}, f32[1,512]{1,0:T(1,128)}, u32[]{:S(2)}) copy-start(f32[1,512]{1,0:T(1,128)} %constant.13.clone.weights) | copy-start | bytes 6148
  2.7 13.7 %collective-permute-start.1 = (bf16[41,8,128]{2,1,0:T(8,128)(2,1)S(1)}, bf16[41,8,128]{2,1,0:T(8,128)(2,1)S(1)}, u32[]{:S(2)}, u32[]{:S(2)}) collective-permute-start(bf16[41,8,128]{2,1,0:T(8,128)(2,1)S(1)} %get-tuple-element.22), channel_id=1, source_target_pairs={{0,8},{2,10},{4,12},{6,14},{8,0},{10,2},{12,4},{14,6},{1,9},{3,11}... | collective-permute-start | bytes 251912 | tf_op jit(solution)/shard_map/ppermute | solution.py:578
  6.4 13.1 %collective-permute-start.2 = (bf16[41,8,128]{2,1,0:T(8,128)(2,1)S(1)}, bf16[41,8,128]{2,1,0:T(8,128)(2,1)S(1)}, u32[]{:S(2)}, u32[]{:S(2)}) collective-permute-start(bf16[41,8,128]{2,1,0:T(8,128)(2,1)S(1)} %get-tuple-element.23), channel_id=1, source_target_pairs={{0,2},{2,0},{4,6},{6,4},{8,10},{10,8},{12,14},{14,12},{1,3},{3,1},... | collective-permute-start | bytes 251912 | tf_op jit(solution)/shard_map/ppermute | solution.py:578
  7.9 8.6 %collective-permute-start.9 = (bf16[27,8,128]{2,1,0:T(8,128)(2,1)S(1)}, bf16[27,8,128]{2,1,0:T(8,128)(2,1)S(1)}, u32[]{:S(2)}, u32[]{:S(2)}) collective-permute-start(bf16[27,8,128]{2,1,0:T(8,128)(2,1)S(1)} %get-tuple-element.28), channel_id=1, source_target_pairs={{0,10},{2,8},{4,14},{6,12},{8,2},{10,0},{12,6},{14,4},{1,11},{3,9}... | collective-permute-start | bytes 165896 | tf_op jit(solution)/shard_map/ppermute | solution.py:578
  7.9 8.5 %collective-permute-start.10 = (bf16[27,8,128]{2,1,0:T(8,128)(2,1)S(1)}, bf16[27,8,128]{2,1,0:T(8,128)(2,1)S(1)}, u32[]{:S(2)}, u32[]{:S(2)}) collective-permute-start(bf16[27,8,128]{2,1,0:T(8,128)(2,1)S(1)} %get-tuple-element.29), channel_id=1, source_target_pairs={{0,14},{2,12},{4,10},{6,8},{8,6},{10,4},{12,2},{14,0},{1,15},{3,13... | collective-permute-start | bytes 165896 | tf_op jit(solution)/shard_map/ppermute | solution.py:578
  16.5 4.5 %collective-permute-start.3 = (bf16[41,8,128]{2,1,0:T(8,128)(2,1)S(1)}, bf16[41,8,128]{2,1,0:T(8,128)(2,1)S(1)}, u32[]{:S(2)}, u32[]{:S(2)}) collective-permute-start(bf16[41,8,128]{2,1,0:T(8,128)(2,1)S(1)} %get-tuple-element.24), channel_id=1, source_target_pairs={{0,4},{2,6},{4,0},{6,2},{8,12},{10,14},{12,8},{14,10},{1,5},{3,7},... | collective-permute-start | bytes 251912 | tf_op jit(solution)/shard_map/ppermute | solution.py:578
  16.5 8.9 %collective-permute-start = (bf16[42,8,128]{2,1,0:T(8,128)(2,1)S(1)}, bf16[42,8,128]{2,1,0:T(8,128)(2,1)S(1)}, u32[]{:S(2)}, u32[]{:S(2)}) collective-permute-start(bf16[42,8,128]{2,1,0:T(8,128)(2,1)S(1)} %get-tuple-element.20.refs_0_), channel_id=1, source_target_pairs={{0,1},{1,0},{2,3},{3,2},{4,5},{5,4},{6,7},{7,6},{8,9},{9,8},{10,11... | collective-permute-start | bytes 258056 | tf_op jit(solution)/shard_map/ppermute | solution.py:527
  16.5 8.0 %collective-permute-start.7 = (bf16[41,8,128]{2,1,0:T(8,128)(2,1)S(1)}, bf16[41,8,128]{2,1,0:T(8,128)(2,1)S(1)}, u32[]{:S(2)}, u32[]{:S(2)}) collective-permute-start(bf16[41,8,128]{2,1,0:T(8,128)(2,1)S(1)} %get-tuple-element.27), channel_id=1, source_target_pairs={{0,12},{2,14},{4,8},{6,10},{8,4},{10,6},{12,0},{14,2},{1,13},{3,15... | collective-permute-start | bytes 251912 | tf_op jit(solution)/shard_map/ppermute | solution.py:578
  19.5 5.9 %collective-permute-start.11 = (bf16[41,8,128]{2,1,0:T(8,128)(2,1)S(1)}, bf16[41,8,128]{2,1,0:T(8,128)(2,1)S(1)}, u32[]{:S(2)}, u32[]{:S(2)}) collective-permute-start(bf16[41,8,128]{2,1,0:T(8,128)(2,1)S(1)} %get-tuple-element.30), channel_id=1, source_target_pairs={{0,6},{2,4},{4,2},{6,0},{8,14},{10,12},{12,10},{14,8},{1,7},{3,5},... | collective-permute-start | bytes 251912 | tf_op jit(solution)/shard_map/ppermute | solution.py:578
  20.9 6.2 %collective-permute-start.4 = (bf16[41,8,128]{2,1,0:T(8,128)(2,1)S(1)}, bf16[41,8,128]{2,1,0:T(8,128)(2,1)S(1)}, u32[]{:S(2)}, u32[]{:S(2)}) collective-permute-start(bf16[41,8,128]{2,1,0:T(8,128)(2,1)S(1)} %collective-permute-done.1.refs_1_.refs_0_), channel_id=1, source_target_pairs={{0,1},{1,0},{2,3},{3,2},{4,5},{5,4},{6,7},{7,6},{8,9},{9,8},{10,11... | collective-permute-start | bytes 251912 | tf_op jit(solution)/shard_map/ppermute | solution.py:527
  24.5 2.7 %collective-permute-start.5 = (bf16[41,8,128]{2,1,0:T(8,128)(2,1)S(1)}, bf16[41,8,128]{2,1,0:T(8,128)(2,1)S(1)}, u32[]{:S(2)}, u32[]{:S(2)}) collective-permute-start(bf16[41,8,128]{2,1,0:T(8,128)(2,1)S(1)} %collective-permute-done.2.refs_2_), channel_id=1, source_target_pairs={{0,1},{1,0},{2,3},{3,2},{4,5},{5,4},{6,7},{7,6},{8,9},{9,8},{10,11... | collective-permute-start | bytes 251912 | tf_op jit(solution)/shard_map/ppermute | solution.py:527
  25.4 3.7 %collective-permute-start.6 = (bf16[41,8,128]{2,1,0:T(8,128)(2,1)S(1)}, bf16[41,8,128]{2,1,0:T(8,128)(2,1)S(1)}, u32[]{:S(2)}, u32[]{:S(2)}) collective-permute-start(bf16[41,8,128]{2,1,0:T(8,128)(2,1)S(1)} %collective-permute-done.3.refs_3_), channel_id=1, source_target_pairs={{0,1},{1,0},{2,3},{3,2},{4,5},{5,4},{6,7},{7,6},{8,9},{9,8},{10,11... | collective-permute-start | bytes 251912 | tf_op jit(solution)/shard_map/ppermute | solution.py:527
  25.4 1.4 %collective-permute-start.13 = (bf16[27,8,128]{2,1,0:T(8,128)(2,1)S(1)}, bf16[27,8,128]{2,1,0:T(8,128)(2,1)S(1)}, u32[]{:S(2)}, u32[]{:S(2)}) collective-permute-start(bf16[27,8,128]{2,1,0:T(8,128)(2,1)S(1)} %collective-permute-done.9.refs_1_), channel_id=1, source_target_pairs={{0,1},{1,0},{2,3},{3,2},{4,5},{5,4},{6,7},{7,6},{8,9},{9,8},{10,11... | collective-permute-start | bytes 165896 | tf_op jit(solution)/shard_map/ppermute | solution.py:527
  26.8 4.8 %collective-permute-start.12 = (bf16[41,8,128]{2,1,0:T(8,128)(2,1)S(1)}, bf16[41,8,128]{2,1,0:T(8,128)(2,1)S(1)}, u32[]{:S(2)}, u32[]{:S(2)}) collective-permute-start(bf16[41,8,128]{2,1,0:T(8,128)(2,1)S(1)} %collective-permute-done.7.refs_1_.refs_0_), channel_id=1, source_target_pairs={{0,1},{1,0},{2,3},{3,2},{4,5},{5,4},{6,7},{7,6},{8,9},{9,8},{10,11... | collective-permute-start | bytes 251912 | tf_op jit(solution)/shard_map/ppermute | solution.py:527
  27.1 4.4 %collective-permute-start.15 = (bf16[41,8,128]{2,1,0:T(8,128)(2,1)S(1)}, bf16[41,8,128]{2,1,0:T(8,128)(2,1)S(1)}, u32[]{:S(2)}, u32[]{:S(2)}) collective-permute-start(bf16[41,8,128]{2,1,0:T(8,128)(2,1)S(1)} %collective-permute-done.11.refs_3_), channel_id=1, source_target_pairs={{0,1},{1,0},{2,3},{3,2},{4,5},{5,4},{6,7},{7,6},{8,9},{9,8},{10,11... | collective-permute-start | bytes 251912 | tf_op jit(solution)/shard_map/ppermute | solution.py:527
  27.3 4.2 %collective-permute-start.8 = (bf16[28,8,128]{2,1,0:T(8,128)(2,1)S(1)}, bf16[28,8,128]{2,1,0:T(8,128)(2,1)S(1)}, u32[]{:S(2)}, u32[]{:S(2)}) collective-permute-start(bf16[28,8,128]{2,1,0:T(8,128)(2,1)S(1)} %relay.1), channel_id=1, source_target_pairs={{0,2},{2,0},{4,6},{6,4},{8,10},{10,8},{12,14},{14,12},{1,3},{3,1},... | collective-permute-start | bytes 172040 | tf_op jit(solution)/shard_map/ppermute | solution.py:589
  29.0 1.6 %collective-permute-start.14 = (bf16[27,8,128]{2,1,0:T(8,128)(2,1)S(1)}, bf16[27,8,128]{2,1,0:T(8,128)(2,1)S(1)}, u32[]{:S(2)}, u32[]{:S(2)}) collective-permute-start(bf16[27,8,128]{2,1,0:T(8,128)(2,1)S(1)} %collective-permute-done.10.refs_2_), channel_id=1, source_target_pairs={{0,1},{1,0},{2,3},{3,2},{4,5},{5,4},{6,7},{7,6},{8,9},{9,8},{10,11... | collective-permute-start | bytes 165896 | tf_op jit(solution)/shard_map/ppermute | solution.py:527
  31.5 17.5 %copy-start = (bf16[1680,512]{1,0:T(8,128)(2,1)S(1)}, bf16[1680,512]{1,0:T(8,128)(2,1)}, u32[]{:S(2)}) copy-start(bf16[1680,512]{1,0:T(8,128)(2,1)} %basis_own.3) | copy-start | bytes 5160964
  31.6 17.5 %copy-start.1 = (f32[512]{0:T(512)S(1)}, f32[512]{0:T(512)}, u32[]{:S(2)}) copy-start(f32[512]{0:T(512)} %param.13) | copy-start | bytes 6148
  31.6 17.5 %copy-start.3 = (f32[4]{0:T(128)S(1)}, f32[4]{0:T(128)}, u32[]{:S(2)}) copy-start(f32[4]{0:T(128)} %prior_far.1) | copy-start | bytes 52
  60.0 1.5 %collective-permute-start.17 = (bf16[8,8,1024]{2,1,0:T(8,128)(2,1)S(1)}, bf16[8,8,1024]{2,1,0:T(8,128)(2,1)S(1)}, u32[]{:S(2)}, u32[]{:S(2)}) collective-permute-start(bf16[8,8,1024]{2,1,0:T(8,128)(2,1)S(1)} %all_to_all.11.parts_own), channel_id=1, source_target_pairs={{0,1},{1,0},{2,3},{3,2},{4,5},{5,4},{6,7},{7,6},{8,9},{9,8},{10,11... | collective-permute-start | bytes 393224 | tf_op jit(solution)/shard_map/ppermute | solution.py:527
  60.0 1.5 %collective-permute-start.18 = (f32[8,2304]{1,0:T(8,128)S(1)}, f32[8,2304]{1,0:T(8,128)S(1)}, u32[]{:S(2)}, u32[]{:S(2)}) collective-permute-start(f32[8,2304]{1,0:T(8,128)S(1)} %get-tuple-element.34.flat_own), channel_id=1, source_target_pairs={{0,1},{1,0},{2,3},{3,2},{4,5},{5,4},{6,7},{7,6},{8,9},{9,8},{10,11... | collective-permute-start | bytes 221192 | tf_op jit(solution)/shard_map/ppermute | solution.py:527
